TPU v7x, 256 devices: a whole 4x4x8 slice. The times are simulated.
256 devices in a mesh: seq: 64 (over z, x, core), head: 4 (over y).
Axes of the slice: x: 4, y: 4, z: 8, core: 2. Of those that a mesh axis runs over, the one named last changes fastest.
Arguments:
- queries: bfloat16 [65536, 2048], P('seq', 'head'), may hold values from -200 to 200
- keys: bfloat16 [65536, 2048], P('seq', 'head'), may hold values from -6 to 6
- values: bfloat16 [65536, 2048], P('seq', 'head'), may hold values from -12 to 12
- gate_bias: float32 [16], P('head'), may hold values from -2 to 2
- out_weight: bfloat16 [2048, 4096], P(None, 'head'), may hold values from -0.125 to 0.125
Outputs:
- layer_out: bfloat16 [65536, 4096], P('seq', 'head')
All inputs are finite; a program needn't handle non-finite values.
Results may differ from a plain program's by a relative error of at most 0.007.
Values may be sent and summed in bfloat16 or wider, within the bound.
No kernel may reach another device: no remote copies, remote signals or barrier semaphores. Data moves between devices by JAX's collectives and lax.ppermute only.
A program may use at most 128 MiB of HBM per device.

v0:
```python
import jax
import jax.numpy as jnp
from jax import lax
from jax.sharding import Mesh
from jax.sharding import PartitionSpec as P

DH = 128
SEG = 256
SEQ = ("seq_0", "seq_1", "seq_2")


def nothing_yet(value, identity):
    return jax.tree.map(
        lambda a, e: jnp.broadcast_to(jnp.asarray(e, a.dtype), a.shape), value, identity
    )


def prefix_by_axis(value, axes, combine, identity):
    before = start = nothing_yet(value, identity)
    so_far = value
    for axis in reversed(axes):
        length, position = (lax.axis_size(axis), lax.axis_index(axis))
        pieces = jax.tree.map(
            lambda part, kind: lax.all_gather(part.astype(kind), axis),
            so_far,
            (jnp.bfloat16, jnp.bfloat16),
        )
        inside, so_far = (start, start)
        for k in range(length):
            passed = k < position
            so_far = combine(
                so_far, jax.tree.map(lambda part, own: part[k].astype(own.dtype), pieces, value)
            )
            inside = jax.tree.map(lambda new, old: jnp.where(passed, new, old), so_far, inside)
        before = combine(inside, before)
    return before


def add_states(earlier, later):
    return (earlier[0] + later[0], earlier[1] + later[1])


def body(queries, keys, values, gate_bias, out_weight):
    local_heads = gate_bias.shape[0]
    row_count = queries.shape[0]
    seg_count = row_count // SEG
    blk_shape = (seg_count, SEG, local_heads, DH)
    query_blk = queries.reshape(blk_shape)
    key_blk = keys.reshape(blk_shape)
    value_blk = values.reshape(blk_shape)
    high = lax.Precision.HIGHEST
    query_map = jax.nn.elu(query_blk.astype(jnp.float32)) + 1.0
    key_map = (jax.nn.elu(key_blk.astype(jnp.float32)) + 1.0).astype(jnp.bfloat16)
    deltas = jnp.einsum("sthd,sthe->shde", key_map, value_blk, preferred_element_type=jnp.float32)
    norm_sums = jnp.sum(key_map.astype(jnp.float32), axis=1)
    mem_total = jnp.sum(deltas, axis=0)
    norm_total = jnp.sum(norm_sums, axis=0)
    mem_before, norm_before = prefix_by_axis(
        (mem_total, norm_total),
        SEQ,
        add_states,
        (jnp.zeros_like(mem_total), jnp.zeros_like(norm_total)),
    )
    mem_inner = jnp.concatenate(
        [jnp.zeros_like(deltas[:1]), jnp.cumsum(deltas, axis=0)[:-1]], axis=0
    )
    norm_inner = jnp.concatenate(
        [jnp.zeros_like(norm_sums[:1]), jnp.cumsum(norm_sums, axis=0)[:-1]], axis=0
    )
    mem_prev = mem_before[None] + mem_inner
    norm_prev = norm_before[None] + norm_inner
    recall = jnp.einsum("sthd,shde->sthe", query_map, mem_prev, precision=high)
    denominator = jnp.einsum("sthd,shd->sth", query_map, norm_prev, precision=high) + 1.0
    recall = recall / denominator[..., None]
    positions = jnp.arange(SEG)
    causal = positions[:, None] >= positions[None, :]
    scores = jnp.einsum("sqhd,skhd->shqk", query_blk, key_blk, preferred_element_type=jnp.float32)
    scores = scores * (1.0 / DH**0.5)
    scores = jnp.where(causal[None, None], scores, jnp.float32(-1e30))
    weights = jax.nn.softmax(scores, axis=-1).astype(jnp.bfloat16)
    local_out = jnp.einsum(
        "shqk,skhd->sqhd", weights, value_blk, preferred_element_type=jnp.float32
    )
    gate_open = jax.nn.sigmoid(gate_bias)
    mixed = (
        gate_open[None, None, :, None] * recall + (1.0 - gate_open)[None, None, :, None] * local_out
    )
    context = mixed.astype(jnp.bfloat16).reshape(row_count, local_heads * DH)
    projected = jnp.dot(
        lax.all_gather(context, "head", axis=1, tiled=True),
        out_weight,
        preferred_element_type=jnp.float32,
    )
    return projected.astype(jnp.bfloat16)


def solution(mesh):
    finer = Mesh(
        mesh.devices.reshape(8, 4, 2, mesh.shape["head"]), ("seq_0", "seq_1", "seq_2", "head")
    )
    placed = (P(SEQ, "head"), P(SEQ, "head"), P(SEQ, "head"), P("head"), P(None, "head"))
    return jax.shard_map(
        body, mesh=finer, in_specs=placed, out_specs=P(SEQ, "head"), check_vma=False
    )
```

profile of v0, /device:TPU:1, one launch (start us, length us, event | category | flops | bytes accessed | tf_op | source)
XLA Modules:
  0.0 145.6 jit_solution(89534307836540232)
XLA Ops:
  6.5 0.0 copy-start.2
  6.5 0.0 all-gather.4.cloned.1.call-start
  6.5 1.4 reshape.39
  8.0 0.1 copy-done.2
  8.1 0.3 reshape.40
  8.4 0.0 copy-start.3
  8.4 1.0 copy-done.3
  9.3 2.3 %fusion.83 = (bf16[4,128,128]{2,1,0:T(8,128)(2,1)S(1)}, f32[4,4,128,128]{3,2,1,0:T(8,128)}) fusion(bf16[4,256,4,128]{3,2,1,0:T(4,128)(2,1)S(1)} %reshape.40, bf16[4,256,4,128]{3,2,1,0:T(4,128)(2,1)S(1)} %reshape.39), kind=kOutput, calls=%fused_computation.113 | convolution fusion | flops 137560064 | bytes 3276800 | tf_op jit(solution)/shard_map/sthd,sthe->shde/dot_general | solution.py:54
  11.6 0.0 copy-start
  11.6 5.0 %all-gather = bf16[8,128,128]{2,1,0:T(8,128)(2,1)S(1)} all-gather(bf16[4,128,128]{2,1,0:T(8,128)(2,1)S(1)} %get-tuple-element.9), channel_id=2, replica_groups=mesh['seq_0'=8,'seq_1'=4,'seq_2'=2,'head'=4] {'seq_2'}, dimensions={0}, use_global_device_ids=true | all-gather | bytes 393216 | tf_op jit(solution)/shard_map/all_gather | solution.py:24
  16.7 9.9 %all_gather.30 = bf16[4,4,128,128]{3,2,1,0:T(8,128)(2,1)S(1)} all-gather(bf16[1,4,128,128]{3,2,1,0:T(8,128)(2,1)S(1)} %fusion.56), channel_id=1, replica_groups=mesh['seq_0'=8,'seq_1'=4,'seq_2'=2,'head'=4] {'seq_1'}, dimensions={0}, use_global_device_ids=true | all-gather | bytes 655360 | tf_op jit(solution)/shard_map/all_gather | solution.py:24
  26.6 0.7 fusion.54
  27.3 0.0 all-gather.4.cloned.1.call-update
  27.3 0.0 all-gather.6.cloned.1.call-start
  27.4 1.0 convert_reduce_fusion
  28.3 0.0 copy-done
  28.3 1.0 fusion.28
  29.3 1.3 reshape.41
  30.7 5.2 %all_gather.33 = bf16[2,4,128]{2,1,0:T(4,128)(2,1)S(1)} all-gather(bf16[1,4,128]{2,1,0:T(4,128)(2,1)S(1)} %bitcast.43), channel_id=1, replica_groups=mesh['seq_0'=8,'seq_1'=4,'seq_2'=2,'head'=4] {'seq_2'}, dimensions={0}, use_global_device_ids=true | all-gather | bytes 3072 | tf_op jit(solution)/shard_map/all_gather | solution.py:24
  35.9 5.5 %all_gather.34 = bf16[4,4,128]{2,1,0:T(4,128)(2,1)S(1)} all-gather(bf16[1,4,128]{2,1,0:T(4,128)(2,1)S(1)} %fusion.73), channel_id=1, replica_groups=mesh['seq_0'=8,'seq_1'=4,'seq_2'=2,'head'=4] {'seq_1'}, dimensions={0}, use_global_device_ids=true | all-gather | bytes 5120 | tf_op jit(solution)/shard_map/all_gather | solution.py:24
  41.4 17.7 %all_gather.35 = bf16[8,4,128]{2,1,0:T(4,128)(2,1)S(1)} all-gather(bf16[1,4,128]{2,1,0:T(4,128)(2,1)S(1)} %fusion.72), channel_id=1, replica_groups=mesh['seq_0'=8,'seq_1'=4,'seq_2'=2,'head'=4] {'seq_0'}, dimensions={0}, use_global_device_ids=true | all-gather | bytes 9216 | tf_op jit(solution)/shard_map/all_gather | solution.py:24
  59.2 1.3 fusion.84
  60.5 0.0 copy-start.1
  60.5 0.0 copy-start.5
  60.6 2.5 %fusion.16 = f32[4,4,1,256]{3,2,1,0:T(1,128)S(1)} fusion(f32[4,4,128,1]{2,3,1,0:T(1,128)S(1)} %bitcast.42, bf16[4,256,4,128]{3,2,1,0:T(4,128)(2,1)S(1)} %reshape.41), kind=kOutput, calls=%fused_computation.29 | convolution fusion | flops 8912896 | bytes 1073152 | tf_op jit(solution)/shard_map/sthd,shd->sth/dot_general | solution.py:73
  63.1 0.0 copy-done.5
  63.1 0.0 copy-done.1
  63.2 0.7 fusion.32
  63.9 0.0 copy-start.4
  63.9 1.2 fusion.82
  65.1 0.0 copy-done.4
  65.1 1.9 %fusion.14 = f32[4,4,256,128]{2,3,1,0:T(8,128)} fusion(f32[4,4,256,256]{2,3,1,0:T(8,128)S(1)} %get-tuple-element.8, f32[4,4,256]{2,1,0:T(4,128)S(1)} %get-tuple-element.7, bf16[4,256,4,128]{3,2,1,0:T(4,128)(2,1)S(1)} %copy-done.4), kind=kOutput, calls=%fused_computation.26 | convolution fusion | flops 270532608 | bytes 7356416 | tf_op jit(solution)/shard_map/shqk,skhd->sqhd/dot_general | solution.py:81
  67.0 0.0 slice-start
  67.0 0.0 all-gather.4.cloned.1.call-done
  67.0 1.7 %fusion.43 = f32[4,128,128]{2,1,0:T(8,128)S(1)} fusion(bf16[8,4,128,128]{3,2,1,0:T(8,128)(2,1)} %all-gather.4.cloned.1.call-done, pred[]{:T(512)S(6)} %gt.68, pred[]{:T(512)S(6)} %gt.69, pred[]{:T(512)S(6)} %gt.67, pred[]{:T(512)S(6)} %gt.66, pred[]{:T(512)S(6)} %gt.65, pred[]{:T(512)S(6)} %gt.64, pred[]{:T(512)S(6)} %gt.63, pred[]{:T(512)S(6)} %gt.62, ...), kind=kLoop, calls=%fused_computation.59 | loop fusion | flops 2686976 | bytes 2097166 | tf_op jit(solution)/shard_map/add | solution.py:70
  68.8 0.0 slice-done
  68.8 5.7 %fusion.10 = bf16[4,256,4,128]{1,3,2,0:T(8,128)(2,1)} fusion(f32[4,4,256,128]{2,3,1,0:T(8,128)} %fusion.14, f32[4]{0:T(128)S(1)} %get-tuple-element.5, f32[4,256,4]{1,2,0:T(4,128)S(1)} %fusion.57, f32[3,4,128,128]{3,2,1,0:T(8,128)S(1)} %slice-done, f32[4]{0:T(128)S(1)} %get-tuple-element.6, bf16[4,256,4,128]{3,2,1,0:T(4,128)(2,1)S(1)} %reshape.41, ...), kind=kOutput, calls=%fused_computation.20 | convolution fusion | flops 810811392 | bytes 5259296 | tf_op jit(solution)/shard_map/sthd,shde->sthe/dot_general | solution.py:72
  74.5 1.6 %copy.37 = bf16[4,256,4,128]{3,2,1,0:T(4,128)(2,1)S(1)} copy(bf16[4,256,4,128]{1,3,2,0:T(8,128)(2,1)} %fusion.10) | data formatting | bytes 2097152 | tf_op jit(solution)/shard_map/convert_element_type | solution.py:88
  76.1 1.2 copy.71
  77.2 0.0 all-gather.6.cloned.1.call-update
  77.3 52.2 %all-gather.6.cloned.1.call-done = bf16[1024,2048]{1,0:T(8,128)(2,1)} async-done(((bf16[1024,512]{1,0:T(8,128)(2,1)}), bf16[1024,2048]{1,0:T(8,128)(2,1)}) %all-gather.6.cloned.1.call-update) | async-done | bytes 4194320 | tf_op jit(solution)/shard_map/all_gather | solution.py:90
  129.4 9.3 %convolution_convert_fusion = bf16[1024,1024]{1,0:T(8,128)(2,1)} fusion(bf16[1024,2048]{1,0:T(8,128)(2,1)} %all-gather.6.cloned.1.call-done, bf16[2048,1024]{1,0:T(8,128)(2,1)} %param.9), kind=kOutput, calls=%fused_computation.28 | convolution fusion | flops 4296015872 | bytes 10485760 | tf_op jit(solution)/shard_map/dot_general | solution.py:89
  (10 shorter events, 0.1 us)
Async XLA Ops:
  6.5 1.5 %copy-start.2 = (bf16[1024,512]{1,0:T(8,128)(2,1)S(1)}, bf16[1024,512]{1,0:T(8,128)(2,1)}, u32[]{:S(2)}) copy-start(bf16[1024,512]{1,0:T(8,128)(2,1)} %param.7) | copy-start | bytes 3145732
  6.5 60.5 %all-gather.4.cloned.1.call-start = ((), (), s32[]{:S(2)}) async-start(), calls=%async_computation | async-start | bytes 1179648 | tf_op jit(solution)/shard_map/all_gather | solution.py:24
  8.4 1.0 copy-start.3
  11.6 16.7 %copy-start = (bf16[1024,512]{1,0:T(8,128)(2,1)S(1)}, bf16[1024,512]{1,0:T(8,128)(2,1)}, u32[]{:S(2)}) copy-start(bf16[1024,512]{1,0:T(8,128)(2,1)} %param.6) | copy-start | bytes 3145732
  27.3 102.1 %all-gather.6.cloned.1.call-start = ((), (), s32[]{:S(2)}) async-start(), calls=%async_computation.1 | async-start | bytes 5242880 | tf_op jit(solution)/shard_map/all_gather | solution.py:90
  60.5 2.6 %copy-start.1 = (f32[4,4,128,128]{3,2,1,0:T(8,128)}, f32[4,4,128,128]{3,2,1,0:T(8,128)S(1)}, u32[]{:S(2)}) copy-start(f32[4,4,128,128]{3,2,1,0:T(8,128)S(1)} %fusion.84) | copy-start | bytes 3145732
  60.5 2.5 %copy-start.5 = (f32[4]{0:T(128)S(1)}, f32[4]{0:T(128)}, u32[]{:S(2)}) copy-start(f32[4]{0:T(128)} %param.8) | copy-start | bytes 52
  63.9 1.3 copy-start.4
  67.0 1.7 %slice-start = ((f32[4,4,128,128]{3,2,1,0:T(8,128)}), f32[3,4,128,128]{3,2,1,0:T(8,128)S(1)}, s32[]{:S(2)}) async-start(f32[4,4,128,128]{3,2,1,0:T(8,128)} %copy-done.1), calls=%async_computation.2 | async-start | bytes 1572864 | tf_op jit(solution)/shard_map/slice | solution.py:65
Sparse Core Ops, SparseCore 0:
  27.4 37.6 all-gather.3
  77.4 52.0 all-gather.5
where the time goes:
time: 146 us
  waiting for transfers between devices  52.2 us (36%)
  blocking collectives  43.3 us (30%)
  matrix products  22.4 us (15%)
  between operations  13.6 us (9%)
  other arithmetic  7.07 us (5%)
  local copies, waits for them, and re-layouts  6.92 us (5%)
    all_gather x1, waiting for transfers between devices, body(): lax.all_gather(context, 'head', axis=1, tiled=True)  52.2 us
    all_gather x5, blocking collectives, prefix_by_axis(): lax.all_gather(part.astype(kind), axis)  43.3 us
    dot_general x1, matrix products, body(): jnp.dot(lax.all_gather(context, 'head', axis=1, tiled=True), out_weight,...  9.27 us
    dot_general x1, matrix products, body(): recall = jnp.einsum('sthd,shde->sthe', query_map, mem_prev, precision=high)  5.69 us
  transfers between devices with their start and end apart: 2, of which 1 were waited for; matrix products, arithmetic and copies ran while one was open for 8% of the time, Pallas kernels for 0%

commit v1 on v0

v1 whole, which is shorter than its diff:
```python
import jax
import jax.numpy as jnp
from jax import lax
from jax.experimental import pallas as pl
from jax.experimental.pallas import tpu as pltpu
from jax.sharding import Mesh
from jax.sharding import PartitionSpec as P

DH = 128
SEG = 256
SEQ = ("seq_0", "seq_1", "seq_2")
BF = jnp.bfloat16
F32 = jnp.float32
ROWS = DH + 8


def feature(x):
    x = x.astype(F32)
    return jnp.where(x > 0.0, x + 1.0, jnp.exp(jnp.minimum(x, 0.0)))


def state_kernel(k_ref, v_ref, total_ref, inner_ref, norm_ref):
    segs = k_ref.shape[0] // SEG
    heads = k_ref.shape[1] // DH
    first = pl.program_id(0) * heads
    for h in range(heads):
        cols = slice(h * DH, (h + 1) * DH)
        mem = jnp.zeros((DH, DH), F32)
        norm = jnp.zeros((ROWS - DH, DH), F32)
        for s in range(segs):
            rows = slice(s * SEG, (s + 1) * SEG)
            if s > 0:
                inner_ref[s - 1, first + h] = mem
            norm_ref[first + h, s : s + 1, :] = norm[:1]
            key_map = feature(k_ref[rows, cols]).astype(BF)
            mem = mem + lax.dot_general(
                key_map, v_ref[rows, cols], (((0,), (0,)), ((), ())), preferred_element_type=F32
            )
            norm = norm + jnp.dot(jnp.ones((ROWS - DH, SEG), BF), key_map, preferred_element_type=F32)
        total_ref[first + h, :DH, :] = mem
        total_ref[first + h, DH:, :] = norm


def local_kernel(gate_ref, q_ref, k_ref, v_ref, out_ref):
    heads = q_ref.shape[1] // DH
    scale = 1.0 / DH**0.5 * 1.4426950408889634
    for s in range(q_ref.shape[0] // SEG):
        rows = slice(s * SEG, (s + 1) * SEG)
        for h in range(heads):
            cols = slice(h * DH, (h + 1) * DH)
            rest = 1.0 - gate_ref[h]
            scores = lax.dot_general(
                q_ref[rows, cols], k_ref[rows, cols], (((1,), (1,)), ((), ())), preferred_element_type=F32
            )
            row_at = lax.broadcasted_iota(jnp.int32, (SEG, SEG), 0)
            col_at = lax.broadcasted_iota(jnp.int32, (SEG, SEG), 1)
            scores = jnp.where(row_at >= col_at, scores * scale, -1e30)
            weights = jnp.exp2(scores - jnp.max(scores, axis=1, keepdims=True)).astype(BF)
            wide = jnp.concatenate([v_ref[rows, cols], jnp.ones((SEG, DH), BF)], axis=1)
            out = jnp.dot(weights, wide, preferred_element_type=F32)
            out_ref[rows, cols] = (out[:, :DH] * (rest / out[:, DH:])).astype(out_ref.dtype)


def context_kernel(first, gate_ref, q_ref, local_ref, before_ref, inner_ref, norm_ref, out_ref):
    heads = q_ref.shape[1] // DH
    for i in range(out_ref.shape[0] // SEG):
        s = first + i
        rows = slice(s * SEG, (s + 1) * SEG)
        outs = slice(i * SEG, (i + 1) * SEG)
        for h in range(heads):
            cols = slice(h * DH, (h + 1) * DH)
            query_map = feature(q_ref[rows, cols]).astype(BF)
            mem = before_ref[h, :DH, :]
            norm = before_ref[h, DH : DH + 1, :] + norm_ref[h, s : s + 1, :]
            if s > 0:
                mem = mem + inner_ref[s - 1, h]
            norm = jnp.broadcast_to(norm.astype(BF), (DH, DH))
            top = jnp.dot(query_map, mem.astype(BF), preferred_element_type=F32)
            bottom = lax.dot_general(query_map, norm, (((1,), (1,)), ((), ())), preferred_element_type=F32)
            recall = gate_ref[h] * top / (bottom + 1.0)
            out_ref[outs, cols] = (recall + local_ref[rows, cols].astype(F32)).astype(BF)


def project_kernel(near, far, at_ref, *refs):
    own_ref, prev_ref, next_ref, far_a_ref, far_b_ref, w_ref, sum_ref = refs[:7]
    out_ref = refs[-1]
    rows, tile = out_ref.shape
    col = pl.multiple_of(pl.program_id(0) * tile, tile)
    width = own_ref.shape[1]
    groups = w_ref.shape[0] // width
    half = rows // 2

    def part(offset):
        start = pl.multiple_of(lax.rem(at_ref[0] + offset, groups) * width, width)
        return w_ref[pl.ds(start, width), pl.ds(col, tile)]

    if near:
        acc = jnp.dot(own_ref[...], part(0), preferred_element_type=F32)
        acc = acc + jnp.dot(prev_ref[...], part(groups - 1), preferred_element_type=F32)
        acc = acc + jnp.dot(next_ref[...], part(1), preferred_element_type=F32)
    else:
        acc = sum_ref[:, pl.ds(col, tile)]
    if far:
        weight = part(2)
        top = acc[:half] + jnp.dot(far_a_ref[...], weight, preferred_element_type=F32)
        bottom = acc[half:] + jnp.dot(far_b_ref[...], weight, preferred_element_type=F32)
        out_ref[:half, :] = top.astype(out_ref.dtype)
        out_ref[half:, :] = bottom.astype(out_ref.dtype)
    else:
        out_ref[...] = acc


VMEM_SPEC = pl.BlockSpec(memory_space=pltpu.VMEM)
SMEM_SPEC = pl.BlockSpec(memory_space=pltpu.SMEM)


def near_core(x):
    return pltpu.with_memory_space_constraint(x, pltpu.VMEM)


def params(mib):
    return pltpu.CompilerParams(vmem_limit_bytes=mib * 2**20)


def state_call(keys, values):
    heads = keys.shape[1] // DH
    segs = keys.shape[0] // SEG
    block = pl.BlockSpec((keys.shape[0], 2 * DH), lambda i: (0, i))
    return pl.pallas_call(
        state_kernel,
        grid=(heads // 2,),
        in_specs=[block, block],
        out_specs=(VMEM_SPEC,) * 3,
        out_shape=(
            pltpu.VMEM((heads, ROWS, DH), F32),
            pltpu.VMEM((segs - 1, heads, DH, DH), F32),
            pltpu.VMEM((heads, 8, DH), F32),
        ),
        compiler_params=params(12),
        name="state",
    )(keys, values)


def local_call(gate, q, k, v):
    n, width = q.shape
    return pl.pallas_call(
        local_kernel,
        in_specs=[SMEM_SPEC] + [VMEM_SPEC] * 3,
        out_specs=VMEM_SPEC,
        out_shape=pltpu.VMEM((n, width), BF),
        compiler_params=params(12),
        cost_estimate=pl.CostEstimate(
            flops=4 * n * SEG * width, transcendentals=n * SEG * 4, bytes_accessed=8 * n * width
        ),
        name="local",
    )(gate, q, k, v)


def context_call(first, count, gate, q, local, before, inner, norm):
    return pl.pallas_call(
        lambda *refs: context_kernel(first, *refs),
        in_specs=[SMEM_SPEC] + [VMEM_SPEC] * 5,
        out_specs=VMEM_SPEC,
        out_shape=pltpu.VMEM((count * SEG, q.shape[1]), BF),
        compiler_params=params(12),
    )(gate, q, local, near_core(before), inner, norm)


def project_call(at, pieces, weight, total_rows, chunk, near, far, partial, so_far):
    n = weight.shape[1]
    tile = n // 4
    rows = pieces[0].shape[0]
    if partial is None:
        partial = at
    kept = [pieces[0]] * 5
    for i, piece in enumerate(pieces):
        if piece is not None:
            kept[i] = piece
    operands = [at, *map(near_core, kept), weight, partial]
    specs = [SMEM_SPEC] + [VMEM_SPEC] * 6 + [SMEM_SPEC if partial is at else VMEM_SPEC]
    aliases = {}
    if so_far is not None:
        aliases = {len(operands): 0}
        operands.append(so_far)
        specs.append(pl.BlockSpec(memory_space=pl.ANY))
    if far:
        out_shape = jax.ShapeDtypeStruct((total_rows, n), BF)
        out_spec = pl.BlockSpec((rows, tile), lambda j: (chunk, j))
    else:
        out_shape = jax.ShapeDtypeStruct((rows, n), F32)
        out_spec = pl.BlockSpec((rows, tile), lambda j: (0, j))
    width = (3 * near + far) * weight.shape[0] // 4
    return pl.pallas_call(
        lambda *refs: project_kernel(near, far, *refs),
        grid=(n // tile,),
        in_specs=specs,
        out_specs=out_spec,
        out_shape=out_shape,
        input_output_aliases=aliases,
        compiler_params=params(12),
        cost_estimate=pl.CostEstimate(flops=2 * rows * width * n, transcendentals=0, bytes_accessed=2 * width * n),
    )(*operands)


def turn(value, axis, step):
    size = lax.axis_size(axis)
    return lax.ppermute(value, axis, [(i, (i + step) % size) for i in range(size)])


def states_before(total):
    heads = total.shape[0]
    halves = total.reshape(2, heads // 2 * ROWS, DH)
    core = lax.axis_index("seq_2")
    mine = lax.dynamic_index_in_dim(halves, core, 0, keepdims=False)
    theirs = lax.dynamic_index_in_dim(halves, 1 - core, 0, keepdims=False)
    got = turn(theirs.astype(BF), "seq_2", 1).astype(F32)
    chip = mine + got
    sent = chip.astype(BF)
    x = lax.axis_index("seq_1")
    size = lax.axis_size("seq_1")
    plane, before = chip, jnp.zeros_like(chip)
    for k in range(1, size):
        piece = turn(sent, "seq_1", k).astype(F32)
        plane = plane + piece
        before = before + jnp.where(x >= k, piece, 0.0)
    z = lax.axis_index("seq_0")
    size = lax.axis_size("seq_0")
    beside = lax.ppermute(plane.astype(BF), "seq_0", [(i, i ^ 1) for i in range(size)]).astype(F32)
    before = before + jnp.where(z % 2 == 1, beside, 0.0)
    pair = (plane + beside).astype(BF)
    for k in range(2, size, 2):
        piece = turn(pair, "seq_0", k)
        before = before + jnp.where(z >= k, piece.astype(F32), 0.0)
    first = core == 0
    swapped = turn(jnp.where(first, before + mine, before).astype(BF), "seq_2", 1).astype(F32)
    own = jnp.where(first, before, before + got)
    low = jnp.where(first, own, swapped)
    high = jnp.where(first, swapped, own)
    return jnp.concatenate([low, high], axis=0).reshape(heads, ROWS, DH)


def layer(queries, keys, values, gate_bias, out_weight):
    rows = queries.shape[0]
    segs = rows // SEG
    chunks = 2
    gate = jax.nn.sigmoid(gate_bias)
    at = jnp.full((1,), lax.axis_index("head"), jnp.int32)
    total, inner, norm = state_call(keys, values)
    before = states_before(total)
    near_q = near_core(queries)
    local = local_call(gate, near_q, near_core(keys), near_core(values))
    weight = near_core(out_weight)
    pieces = []
    for c in range(chunks):
        own = context_call(c * segs // chunks, segs // chunks, gate, near_q, local, before, inner, norm)
        half = own.shape[0] // 2
        prev = turn(own, "head", 1)
        nxt = turn(own, "head", -1)
        far_a = turn(prev[:half], "head", 1)
        far_b = turn(nxt[half:], "head", -1)
        pieces.append((own, prev, nxt, far_a, far_b))
    partial = project_call(at, (*pieces[1][:3], None, None), weight, rows, 1, True, False, None, None)
    out = project_call(at, pieces[0], weight, rows, 0, True, True, None, None)
    own, _, _, far_a, far_b = pieces[1]
    out = project_call(at, (own, None, None, far_a, far_b), weight, rows, 1, False, True, near_core(partial), out)
    return out


def solution(mesh):
    finer = Mesh(
        mesh.devices.reshape(8, 4, 2, mesh.shape["head"]), ("seq_0", "seq_1", "seq_2", "head")
    )
    placed = (P(SEQ, "head"), P(SEQ, "head"), P(SEQ, "head"), P("head"), P(None, "head"))
    return jax.shard_map(layer, mesh=finer, in_specs=placed, out_specs=P(SEQ, "head"), check_vma=False)
```

time: 146 us -> 84.9 us (0.58)
  blocking collectives: 43.3 us -> 0 us
  starting transfers between devices: 0.04 us -> 32.6 us
  waiting for transfers between devices: 52.2 us -> 28.4 us
  matrix products: 22.4 us -> 0 us
  Pallas kernels: 0 us -> 14.8 us
  between operations: 13.6 us -> 0.16 us
  other arithmetic: 7.07 us -> 1.85 us
    all_gather x2 -> x0, waiting for transfers between devices: 52.2 us -> none  [the longest x1 52.2 us: body(): lax.all_gather(context, 'head', axis=1, tiled=True)]
    all_gather x5 -> x0, blocking collectives: 43.3 us -> none  [prefix_by_axis(): lax.all_gather(part.astype(kind), axis)]
    ppermute x0 -> x17, starting transfers between devices: none -> 32.6 us  [the longest x16 31 us: turn(): lax.ppermute(value, axis, [(i, (i + step) % size) for i in range(size)])]
    ppermute x0 -> x17, waiting for transfers between devices: none -> 28.4 us  [the longest x16 26.7 us: turn(): lax.ppermute(value, axis, [(i, (i + step) % size) for i in range(size)])]
    dot_general x6 -> x0, matrix products: 22.4 us -> none  [the longest x1 9.27 us: body(): jnp.dot(lax.all_gather(context, 'head', axis=1, tiled=True), out_weight,...]
    pallas_call x0 -> x7, Pallas kernels: none -> 14.8 us  [the longest x3 9.48 us: project_call(): pl.pallas_call(lambda *refs: project_kernel(near, far, *refs), grid=(n //...]
    unnamed x13 -> x24, local copies, waits for them, and re-layouts: 2.24 us -> 6.65 us
    reshape x3 -> x0, local copies, waits for them, and re-layouts: 3.04 us -> none  [the longest x1 1.43 us: body(): key_blk = keys.reshape(blk_shape)]
  transfers between devices with their start and end apart: 2 -> 17, of which waited for: 1 -> 11; matrix products, arithmetic and copies ran while one was open for 8% -> 0% of each run, Pallas kernels for 0% -> 12%
where the time goes in v1:
time: 84.9 us; the launch traced here: 84.6 us
  starting transfers between devices  32.6 us (38%)
  waiting for transfers between devices  28.4 us (33%)
  Pallas kernels  14.8 us (17%)
  local copies, waits for them, and re-layouts  6.74 us (8%)
  other arithmetic  1.85 us (2%)
    ppermute x16, starting transfers between devices, turn(): lax.ppermute(value, axis, [(i, (i + step) % size) for i in range(size)])  31 us
    ppermute x16, waiting for transfers between devices, turn(): lax.ppermute(value, axis, [(i, (i + step) % size) for i in range(size)])  26.7 us
    pallas_call x3, Pallas kernels, project_call(): pl.pallas_call(lambda *refs: project_kernel(near, far, *refs), grid=(n //...  9.48 us
    unnamed x24, local copies, waits for them, and re-layouts  6.65 us
    pallas_call x2, Pallas kernels, context_call(): pl.pallas_call(lambda *refs: context_kernel(first, *refs), in_specs=[SMEM...  2.23 us
    pallas_call x1, Pallas kernels, local_call(): pl.pallas_call(local_kernel, in_specs=[SMEM_SPEC] + [VMEM_SPEC] * 3, out_...  2.02 us
    ppermute x1, waiting for transfers between devices, states_before(): lax.ppermute(plane.astype(BF), 'seq_0', [(i, i ^ 1) for i in range(size)])  1.7 us
  transfers between devices with their start and end apart: 17, of which 11 were waited for; matrix products, arithmetic and copies ran while one was open for 0% of the time, Pallas kernels for 12%

profile of v1, /device:TPU:1, one launch (start us, length us, event | category | flops | bytes accessed | tf_op | source)
XLA Modules:
  0.0 84.6 jit_solution(11572208097359876039)
XLA Ops:
  0.0 0.0 copy-start.3
  0.0 1.2 %copy-done.3 = bf16[1024,512]{1,0:T(8,128)(2,1)S(1)} copy-done((bf16[1024,512]{1,0:T(8,128)(2,1)S(1)}, bf16[1024,512]{1,0:T(8,128)(2,1)}, u32[]{:S(2)}) %copy-start.3) | copy-done | bytes 1048600
  1.2 0.0 copy-start.5
  1.2 1.2 %copy-done.5 = bf16[1024,512]{1,0:T(8,128)(2,1)S(1)} copy-done((bf16[1024,512]{1,0:T(8,128)(2,1)S(1)}, bf16[1024,512]{1,0:T(8,128)(2,1)}, u32[]{:S(2)}) %copy-start.5) | copy-done | bytes 1048600
  2.5 0.0 copy-start.11
  2.5 0.0 copy-start.2
  2.5 0.0 copy-start.4
  2.5 1.1 %state.1 = (f32[4,136,128]{2,1,0:T(8,128)S(1)}, f32[3,4,128,128]{3,2,1,0:T(8,128)S(1)}, f32[4,8,128]{2,1,0:T(8,128)S(1)}) custom-call(bf16[1024,512]{1,0:T(8,128)(2,1)S(1)} %copy-done.3, bf16[1024,512]{1,0:T(8,128)(2,1)S(1)} %copy-done.5), custom_call_target="tpu_custom_call" | custom-call | tf_op jit(solution)/shard_map/state/pallas_call | solution.py:129
  3.6 3.3 %collective-permute-start = (bf16[272,128]{1,0:T(8,128)(2,1)S(1)}, bf16[272,128]{1,0:T(8,128)(2,1)S(1)}, u32[]{:S(2)}, u32[]{:S(2)}) collective-permute-start(bf16[272,128]{1,0:T(8,128)(2,1)S(1)} %fusion.9), channel_id=1, source_target_pairs={{0,4},{4,0},{1,5},{5,1},{2,6},{6,2},{3,7},{7,3},{8,12},{12,8},{9,1... | collective-permute-start | bytes 208904 | tf_op jit(solution)/shard_map/ppermute | solution.py:207
  6.9 0.9 %collective-permute-done = bf16[272,128]{1,0:T(8,128)(2,1)S(1)} collective-permute-done((bf16[272,128]{1,0:T(8,128)(2,1)S(1)}, bf16[272,128]{1,0:T(8,128)(2,1)S(1)}, u32[]{:S(2)}, u32[]{:S(2)}) %collective-permute-start) | collective-permute-done | bytes 69664 | tf_op jit(solution)/shard_map/ppermute | solution.py:207
  7.8 0.8 %collective-permute-start.3 = (bf16[272,128]{1,0:T(8,128)(2,1)S(1)}, bf16[272,128]{1,0:T(8,128)(2,1)S(1)}, u32[]{:S(2)}, u32[]{:S(2)}) collective-permute-start(bf16[272,128]{1,0:T(8,128)(2,1)S(1)} %fusion.8), channel_id=1, source_target_pairs={{0,24},{8,0},{16,8},{24,16},{1,25},{9,1},{17,9},{25,17},{2,26},{10... | collective-permute-start | bytes 208904 | tf_op jit(solution)/shard_map/ppermute | solution.py:207
  8.6 0.5 collective-permute-start.2
  9.2 0.6 collective-permute-start.1
  9.8 1.3 %collective-permute-done.3 = bf16[272,128]{1,0:T(8,128)(2,1)S(1)} collective-permute-done((bf16[272,128]{1,0:T(8,128)(2,1)S(1)}, bf16[272,128]{1,0:T(8,128)(2,1)S(1)}, u32[]{:S(2)}, u32[]{:S(2)}) %collective-permute-start.3) | collective-permute-done | bytes 69664 | tf_op jit(solution)/shard_map/ppermute | solution.py:207
  11.0 2.3 %collective-permute-done.2 = bf16[272,128]{1,0:T(8,128)(2,1)S(1)} collective-permute-done((bf16[272,128]{1,0:T(8,128)(2,1)S(1)}, bf16[272,128]{1,0:T(8,128)(2,1)S(1)}, u32[]{:S(2)}, u32[]{:S(2)}) %collective-permute-start.2) | collective-permute-done | bytes 69664 | tf_op jit(solution)/shard_map/ppermute | solution.py:207
  13.4 2.0 %collective-permute-done.1 = bf16[272,128]{1,0:T(8,128)(2,1)S(1)} collective-permute-done((bf16[272,128]{1,0:T(8,128)(2,1)S(1)}, bf16[272,128]{1,0:T(8,128)(2,1)S(1)}, u32[]{:S(2)}, u32[]{:S(2)}) %collective-permute-start.1) | collective-permute-done | bytes 69664 | tf_op jit(solution)/shard_map/ppermute | solution.py:207
  15.3 0.1 fusion.11
  15.4 1.6 %collective-permute-start.4 = (bf16[272,128]{1,0:T(8,128)(2,1)S(1)}, bf16[272,128]{1,0:T(8,128)(2,1)S(1)}, u32[]{:S(2)}, u32[]{:S(2)}) collective-permute-start(bf16[272,128]{1,0:T(8,128)(2,1)S(1)} %get-tuple-element.13), channel_id=1, source_target_pairs={{0,32},{32,0},{64,96},{96,64},{128,160},{160,128},{192,224},{224,1... | collective-permute-start | bytes 208904 | tf_op jit(solution)/shard_map/ppermute | solution.py:228
  17.0 1.7 %collective-permute-done.4 = bf16[272,128]{1,0:T(8,128)(2,1)S(1)} collective-permute-done((bf16[272,128]{1,0:T(8,128)(2,1)S(1)}, bf16[272,128]{1,0:T(8,128)(2,1)S(1)}, u32[]{:S(2)}, u32[]{:S(2)}) %collective-permute-start.4) | collective-permute-done | bytes 69664 | tf_op jit(solution)/shard_map/ppermute | solution.py:228
  18.7 0.6 fusion.6
  19.4 5.8 %collective-permute-start.7 = (bf16[272,128]{1,0:T(8,128)(2,1)}, bf16[272,128]{1,0:T(8,128)(2,1)}, u32[]{:S(2)}, u32[]{:S(2)}) collective-permute-start(bf16[272,128]{1,0:T(8,128)(2,1)} %fusion.6), channel_id=1, source_target_pairs={{0,192},{32,224},{64,0},{96,32},{128,64},{160,96},{192,128},{224,1... | collective-permute-start | bytes 208904 | tf_op jit(solution)/shard_map/ppermute | solution.py:207
  25.2 0.9 %collective-permute-start.6 = (bf16[272,128]{1,0:T(8,128)(2,1)}, bf16[272,128]{1,0:T(8,128)(2,1)}, u32[]{:S(2)}, u32[]{:S(2)}) collective-permute-start(bf16[272,128]{1,0:T(8,128)(2,1)} %fusion.6), channel_id=1, source_target_pairs={{0,128},{32,160},{64,192},{96,224},{128,0},{160,32},{192,64},{224,... | collective-permute-start | bytes 208904 | tf_op jit(solution)/shard_map/ppermute | solution.py:207
  26.1 2.4 %collective-permute-start.5 = (bf16[272,128]{1,0:T(8,128)(2,1)}, bf16[272,128]{1,0:T(8,128)(2,1)}, u32[]{:S(2)}, u32[]{:S(2)}) collective-permute-start(bf16[272,128]{1,0:T(8,128)(2,1)} %fusion.6), channel_id=1, source_target_pairs={{0,64},{32,96},{64,128},{96,160},{128,192},{160,224},{192,0},{224,... | collective-permute-start | bytes 208904 | tf_op jit(solution)/shard_map/ppermute | solution.py:207
  28.5 0.0 collective-permute-done.7
  28.5 4.3 %collective-permute-done.6 = bf16[272,128]{1,0:T(8,128)(2,1)} collective-permute-done((bf16[272,128]{1,0:T(8,128)(2,1)}, bf16[272,128]{1,0:T(8,128)(2,1)}, u32[]{:S(2)}, u32[]{:S(2)}) %collective-permute-start.6) | collective-permute-done | bytes 69664 | tf_op jit(solution)/shard_map/ppermute | solution.py:207
  32.8 0.2 collective-permute-done.5
  33.0 1.1 %fusion.7 = (bf16[272,128]{1,0:T(8,128)(2,1)S(1)}, f32[272,128]{1,0:T(8,128)S(1)}) fusion(f32[2,272,128]{2,1,0:T(8,128)S(1)} %bitcast.18, s32[]{:T(128)S(6)} %select_n.80, pred[]{:T(512)S(6)} %eq.8, bf16[272,128]{1,0:T(8,128)(2,1)} %collective-permute-done.7, pred[]{:T(512)S(6)} %ge.23, bf16[272,128]{1,0:T(8,128)(2,1)} %collective-permute-done.6, ...), kind=kLoop, calls=%fused_computation.21 | loop fusion | flops 800768 | bytes 835596 | tf_op jit(solution)/shard_map/convert_element_type | solution.py:235
  34.1 4.0 %collective-permute-start.8 = (bf16[272,128]{1,0:T(8,128)(2,1)S(1)}, bf16[272,128]{1,0:T(8,128)(2,1)S(1)}, u32[]{:S(2)}, u32[]{:S(2)}) collective-permute-start(bf16[272,128]{1,0:T(8,128)(2,1)S(1)} %get-tuple-element.11), channel_id=1, source_target_pairs={{0,4},{4,0},{1,5},{5,1},{2,6},{6,2},{3,7},{7,3},{8,12},{12,8},{9,1... | collective-permute-start | bytes 208904 | tf_op jit(solution)/shard_map/ppermute | solution.py:207
  38.1 0.0 copy-done.11
  38.2 0.0 copy-done.2
  38.2 0.0 copy-done.4
  38.2 0.0 copy-start.6
  38.2 1.2 %copy-done.6 = bf16[1024,512]{1,0:T(8,128)(2,1)S(1)} copy-done((bf16[1024,512]{1,0:T(8,128)(2,1)S(1)}, bf16[1024,512]{1,0:T(8,128)(2,1)}, u32[]{:S(2)}) %copy-start.6) | copy-done | bytes 1048600
  39.4 2.0 %local.1.refs_2_ = bf16[1024,512]{1,0:T(8,128)(2,1)S(1)} custom-call(f32[4]{0:T(128)S(1)} %add_divide_fusion.gate_ref.refs_0_, bf16[1024,512]{1,0:T(8,128)(2,1)S(1)} %copy-done.2, bf16[1024,512]{1,0:T(8,128)(2,1)S(1)} %copy-done.4, bf16[1024,512]{1,0:T(8,128)(2,1)S(1)} %copy-done.6), custom_call_target="tpu_custom_call" | custom-call | flops 536870912 | bytes 4194304 | tf_op jit(solution)/shard_map/local/pallas_call | solution.py:146
  41.4 0.0 collective-permute-done.8
  41.5 1.1 %shard_map.57.refs_1_ = bf16[512,512]{1,0:T(8,128)(2,1)S(1)} custom-call(f32[4]{0:T(128)S(1)} %add_divide_fusion.gate_ref.refs_0_, bf16[1024,512]{1,0:T(8,128)(2,1)S(1)} %copy-done.2, bf16[1024,512]{1,0:T(8,128)(2,1)S(1)} %local.1.refs_2_, f32[4,136,128]{2,1,0:T(8,128)S(1)} %bitcast.13, f32[3,4,128,128]{3,2,1,0:T(8,128)S(1)} %get-tuple-element.9.refs_4_, ...), custom_call_target="tpu_custom_call" | custom-call | tf_op jit(solution)/shard_map/pallas_call | solution.py:160
  42.6 2.8 %collective-permute-start.14 = (bf16[512,512]{1,0:T(8,128)(2,1)S(1)}, bf16[512,512]{1,0:T(8,128)(2,1)S(1)}, u32[]{:S(2)}, u32[]{:S(2)}) collective-permute-start(bf16[512,512]{1,0:T(8,128)(2,1)S(1)} %shard_map.57.refs_1_), channel_id=1, source_target_pairs={{0,3},{1,0},{2,1},{3,2},{4,7},{5,4},{6,5},{7,6},{8,11},{9,8},{10,9... | collective-permute-start | bytes 1572872 | tf_op jit(solution)/shard_map/ppermute | solution.py:207
  45.4 0.0 collective-permute-start.13
  45.4 1.1 %shard_map.55.refs_1_.refs_4_.refs_5_.refs_2_.refs_3_ = bf16[512,512]{1,0:T(8,128)(2,1)S(1)} custom-call(f32[4]{0:T(128)S(1)} %add_divide_fusion.gate_ref.refs_0_, bf16[1024,512]{1,0:T(8,128)(2,1)S(1)} %copy-done.2, bf16[1024,512]{1,0:T(8,128)(2,1)S(1)} %local.1.refs_2_, f32[4,136,128]{2,1,0:T(8,128)S(1)} %bitcast.14, ...), custom_call_target="tpu_custom_call" | custom-call | tf_op jit(solution)/shard_map/pallas_call | solution.py:160
  46.6 2.8 %collective-permute-start.11 = (bf16[512,512]{1,0:T(8,128)(2,1)S(1)}, bf16[512,512]{1,0:T(8,128)(2,1)S(1)}, u32[]{:S(2)}, u32[]{:S(2)}) collective-permute-start(bf16[512,512]{1,0:T(8,128)(2,1)S(1)} %shard_map.55.refs_1_.refs_4_.refs_5_.refs_2_.refs_3_), channel_id=1, source_target_pairs={{0,3},{1,0},{2,1},{3,2},{4,7},{5,4},{6,5},{7,6},{8,11},{9,8},{10,9... | collective-permute-start | bytes 1572872 | tf_op jit(solution)/shard_map/ppermute | solution.py:207
  49.3 0.0 collective-permute-start.9
  49.3 7.4 %collective-permute-done.14.refs_3_ = bf16[512,512]{1,0:T(8,128)(2,1)S(1)} collective-permute-done((bf16[512,512]{1,0:T(8,128)(2,1)S(1)}, bf16[512,512]{1,0:T(8,128)(2,1)S(1)}, u32[]{:S(2)}, u32[]{:S(2)}) %collective-permute-start.14) | collective-permute-done | bytes 524320 | tf_op jit(solution)/shard_map/ppermute | solution.py:207
  56.7 0.0 copy-start.7
  56.7 3.5 %collective-permute-start.16 = (bf16[256,512]{1,0:T(8,128)(2,1)S(1)}, bf16[256,512]{1,0:T(8,128)(2,1)S(1)}, u32[]{:S(2)}, u32[]{:S(2)}) collective-permute-start(bf16[256,512]{1,0:T(8,128)(2,1)S(1)} %slice.19), channel_id=1, source_target_pairs={{0,3},{1,0},{2,1},{3,2},{4,7},{5,4},{6,5},{7,6},{8,11},{9,8},{10,9... | collective-permute-start | bytes 786440 | tf_op jit(solution)/shard_map/ppermute | solution.py:207
  60.2 0.0 collective-permute-done.13.refs_2_
  60.2 0.0 copy-done.7
  60.2 0.8 copy-done.9
  61.0 0.0 collective-permute-start.15
  61.0 6.9 %collective-permute-done.11.refs_3_ = bf16[512,512]{1,0:T(8,128)(2,1)S(1)} collective-permute-done((bf16[512,512]{1,0:T(8,128)(2,1)S(1)}, bf16[512,512]{1,0:T(8,128)(2,1)S(1)}, u32[]{:S(2)}, u32[]{:S(2)}) %collective-permute-start.11) | collective-permute-done | bytes 524320 | tf_op jit(solution)/shard_map/ppermute | solution.py:207
  67.9 3.5 %collective-permute-start.12 = (bf16[256,512]{1,0:T(8,128)(2,1)S(1)}, bf16[256,512]{1,0:T(8,128)(2,1)S(1)}, u32[]{:S(2)}, u32[]{:S(2)}) collective-permute-start(bf16[256,512]{1,0:T(8,128)(2,1)S(1)} %slice.17), channel_id=1, source_target_pairs={{0,3},{1,0},{2,1},{3,2},{4,7},{5,4},{6,5},{7,6},{8,11},{9,8},{10,9... | collective-permute-start | bytes 786440 | tf_op jit(solution)/shard_map/ppermute | solution.py:207
  71.4 0.0 collective-permute-done.9.refs_2_
  71.4 0.1 collective-permute-start.10
  71.5 0.0 copy-start
  71.5 2.2 %copy-done = bf16[2048,1024]{1,0:T(8,128)(2,1)S(1)} copy-done((bf16[2048,1024]{1,0:T(8,128)(2,1)S(1)}, bf16[2048,1024]{1,0:T(8,128)(2,1)}, u32[]{:S(2)}) %copy-start) | copy-done | bytes 4194328
  73.7 2.5 %shard_map.56.refs_7_ = f32[512,1024]{1,0:T(8,128)S(1)} custom-call(s32[1]{0:T(128)} %bitcast.refs_0_.refs_7_, bf16[512,512]{1,0:T(8,128)(2,1)S(1)} %shard_map.55.refs_1_.refs_4_.refs_5_.refs_2_.refs_3_, bf16[512,512]{1,0:T(8,128)(2,1)S(1)} %collective-permute-done.9.refs_2_, bf16[512,512]{1,0:T(8,128)(2,1)S(1)} %collective-permute-done.11.refs_3_, ...), custom_call_target="tpu_custom_call" | custom-call | flops 1610612736 | bytes 3145728 | tf_op jit(solution)/shard_map/pallas_call | solution.py:193
  76.2 0.0 collective-permute-done.16.refs_5_
  76.2 0.5 collective-permute-done.15.refs_4_
  76.8 0.0 copy-done.1
  76.8 0.0 copy-done.8
  76.8 0.0 copy-done.10
  76.8 4.6 %shard_map.58.refs_8_ = bf16[1024,1024]{1,0:T(8,128)(2,1)} custom-call(s32[1]{0:T(128)} %bitcast.refs_0_.refs_7_, bf16[512,512]{1,0:T(8,128)(2,1)S(1)} %shard_map.57.refs_1_, bf16[512,512]{1,0:T(8,128)(2,1)S(1)} %copy-done.10, bf16[512,512]{1,0:T(8,128)(2,1)S(1)} %copy-done.8, bf16[256,512]{1,0:T(8,128)(2,1)} %collective-permute-done.15.refs_4_, ...), custom_call_target="tpu_custom_call" | custom-call | flops 2147483648 | bytes 4194304 | tf_op jit(solution)/shard_map/pallas_call | solution.py:193
  81.4 0.0 collective-permute-done.12.refs_5_
  81.4 0.8 %collective-permute-done.10.refs_4_ = bf16[256,512]{1,0:T(8,128)(2,1)S(1)} collective-permute-done((bf16[256,512]{1,0:T(8,128)(2,1)S(1)}, bf16[256,512]{1,0:T(8,128)(2,1)S(1)}, u32[]{:S(2)}, u32[]{:S(2)}) %collective-permute-start.10) | collective-permute-done | bytes 262176 | tf_op jit(solution)/shard_map/ppermute | solution.py:207
  82.3 2.3 %shard_map.59 = bf16[1024,1024]{1,0:T(8,128)(2,1)} custom-call(s32[1]{0:T(128)} %bitcast.refs_0_.refs_7_, bf16[512,512]{1,0:T(8,128)(2,1)S(1)} %shard_map.55.refs_1_.refs_4_.refs_5_.refs_2_.refs_3_, bf16[512,512]{1,0:T(8,128)(2,1)S(1)} %shard_map.55.refs_1_.refs_4_.refs_5_.refs_2_.refs_3_, ...), custom_call_target="tpu_custom_call", output_to_operand_aliasing={{}: (8, {})} | custom-call | flops 536870912 | bytes 1048576 | tf_op jit(solution)/shard_map/pallas_call | solution.py:193
  (13 shorter events, 0.2 us)
Async XLA Ops:
  0.0 1.2 %copy-start.3 = (bf16[1024,512]{1,0:T(8,128)(2,1)S(1)}, bf16[1024,512]{1,0:T(8,128)(2,1)}, u32[]{:S(2)}) copy-start(bf16[1024,512]{1,0:T(8,128)(2,1)} %k_ref.3) | copy-start | bytes 3145732
  1.2 1.2 %copy-start.5 = (bf16[1024,512]{1,0:T(8,128)(2,1)S(1)}, bf16[1024,512]{1,0:T(8,128)(2,1)}, u32[]{:S(2)}) copy-start(bf16[1024,512]{1,0:T(8,128)(2,1)} %v_ref.3) | copy-start | bytes 3145732
  2.5 35.7 %copy-start.11 = (f32[4]{0:T(128)S(1)}, f32[4]{0:T(128)}, u32[]{:S(2)}) copy-start(f32[4]{0:T(128)} %param.8) | copy-start | bytes 52
  2.5 35.7 %copy-start.2 = (bf16[1024,512]{1,0:T(8,128)(2,1)S(1)}, bf16[1024,512]{1,0:T(8,128)(2,1)}, u32[]{:S(2)}) copy-start(bf16[1024,512]{1,0:T(8,128)(2,1)} %refs_1_.3) | copy-start | bytes 3145732
  2.5 35.7 %copy-start.4 = (bf16[1024,512]{1,0:T(8,128)(2,1)S(1)}, bf16[1024,512]{1,0:T(8,128)(2,1)}, u32[]{:S(2)}) copy-start(bf16[1024,512]{1,0:T(8,128)(2,1)} %k_ref.3) | copy-start | bytes 3145732
  3.6 4.2 %collective-permute-start = (bf16[272,128]{1,0:T(8,128)(2,1)S(1)}, bf16[272,128]{1,0:T(8,128)(2,1)S(1)}, u32[]{:S(2)}, u32[]{:S(2)}) collective-permute-start(bf16[272,128]{1,0:T(8,128)(2,1)S(1)} %fusion.9), channel_id=1, source_target_pairs={{0,4},{4,0},{1,5},{5,1},{2,6},{6,2},{3,7},{7,3},{8,12},{12,8},{9,1... | collective-permute-start | bytes 208904 | tf_op jit(solution)/shard_map/ppermute | solution.py:207
  7.8 3.2 %collective-permute-start.3 = (bf16[272,128]{1,0:T(8,128)(2,1)S(1)}, bf16[272,128]{1,0:T(8,128)(2,1)S(1)}, u32[]{:S(2)}, u32[]{:S(2)}) collective-permute-start(bf16[272,128]{1,0:T(8,128)(2,1)S(1)} %fusion.8), channel_id=1, source_target_pairs={{0,24},{8,0},{16,8},{24,16},{1,25},{9,1},{17,9},{25,17},{2,26},{10... | collective-permute-start | bytes 208904 | tf_op jit(solution)/shard_map/ppermute | solution.py:207
  8.6 4.7 %collective-permute-start.2 = (bf16[272,128]{1,0:T(8,128)(2,1)S(1)}, bf16[272,128]{1,0:T(8,128)(2,1)S(1)}, u32[]{:S(2)}, u32[]{:S(2)}) collective-permute-start(bf16[272,128]{1,0:T(8,128)(2,1)S(1)} %fusion.8), channel_id=1, source_target_pairs={{0,16},{8,24},{16,0},{24,8},{1,17},{9,25},{17,1},{25,9},{2,18},{10... | collective-permute-start | bytes 208904 | tf_op jit(solution)/shard_map/ppermute | solution.py:207
  9.2 6.2 %collective-permute-start.1 = (bf16[272,128]{1,0:T(8,128)(2,1)S(1)}, bf16[272,128]{1,0:T(8,128)(2,1)S(1)}, u32[]{:S(2)}, u32[]{:S(2)}) collective-permute-start(bf16[272,128]{1,0:T(8,128)(2,1)S(1)} %fusion.8), channel_id=1, source_target_pairs={{0,8},{8,16},{16,24},{24,0},{1,9},{9,17},{17,25},{25,1},{2,10},{10... | collective-permute-start | bytes 208904 | tf_op jit(solution)/shard_map/ppermute | solution.py:207
  15.4 3.3 %collective-permute-start.4 = (bf16[272,128]{1,0:T(8,128)(2,1)S(1)}, bf16[272,128]{1,0:T(8,128)(2,1)S(1)}, u32[]{:S(2)}, u32[]{:S(2)}) collective-permute-start(bf16[272,128]{1,0:T(8,128)(2,1)S(1)} %get-tuple-element.13), channel_id=1, source_target_pairs={{0,32},{32,0},{64,96},{96,64},{128,160},{160,128},{192,224},{224,1... | collective-permute-start | bytes 208904 | tf_op jit(solution)/shard_map/ppermute | solution.py:228
  19.4 9.1 %collective-permute-start.7 = (bf16[272,128]{1,0:T(8,128)(2,1)}, bf16[272,128]{1,0:T(8,128)(2,1)}, u32[]{:S(2)}, u32[]{:S(2)}) collective-permute-start(bf16[272,128]{1,0:T(8,128)(2,1)} %fusion.6), channel_id=1, source_target_pairs={{0,192},{32,224},{64,0},{96,32},{128,64},{160,96},{192,128},{224,1... | collective-permute-start | bytes 208904 | tf_op jit(solution)/shard_map/ppermute | solution.py:207
  25.2 7.6 %collective-permute-start.6 = (bf16[272,128]{1,0:T(8,128)(2,1)}, bf16[272,128]{1,0:T(8,128)(2,1)}, u32[]{:S(2)}, u32[]{:S(2)}) collective-permute-start(bf16[272,128]{1,0:T(8,128)(2,1)} %fusion.6), channel_id=1, source_target_pairs={{0,128},{32,160},{64,192},{96,224},{128,0},{160,32},{192,64},{224,... | collective-permute-start | bytes 208904 | tf_op jit(solution)/shard_map/ppermute | solution.py:207
  26.1 6.9 %collective-permute-start.5 = (bf16[272,128]{1,0:T(8,128)(2,1)}, bf16[272,128]{1,0:T(8,128)(2,1)}, u32[]{:S(2)}, u32[]{:S(2)}) collective-permute-start(bf16[272,128]{1,0:T(8,128)(2,1)} %fusion.6), channel_id=1, source_target_pairs={{0,64},{32,96},{64,128},{96,160},{128,192},{160,224},{192,0},{224,... | collective-permute-start | bytes 208904 | tf_op jit(solution)/shard_map/ppermute | solution.py:207
  34.1 7.3 %collective-permute-start.8 = (bf16[272,128]{1,0:T(8,128)(2,1)S(1)}, bf16[272,128]{1,0:T(8,128)(2,1)S(1)}, u32[]{:S(2)}, u32[]{:S(2)}) collective-permute-start(bf16[272,128]{1,0:T(8,128)(2,1)S(1)} %get-tuple-element.11), channel_id=1, source_target_pairs={{0,4},{4,0},{1,5},{5,1},{2,6},{6,2},{3,7},{7,3},{8,12},{12,8},{9,1... | collective-permute-start | bytes 208904 | tf_op jit(solution)/shard_map/ppermute | solution.py:207
  38.2 1.2 %copy-start.6 = (bf16[1024,512]{1,0:T(8,128)(2,1)S(1)}, bf16[1024,512]{1,0:T(8,128)(2,1)}, u32[]{:S(2)}) copy-start(bf16[1024,512]{1,0:T(8,128)(2,1)} %v_ref.3) | copy-start | bytes 3145732
  42.6 14.1 %collective-permute-start.14 = (bf16[512,512]{1,0:T(8,128)(2,1)S(1)}, bf16[512,512]{1,0:T(8,128)(2,1)S(1)}, u32[]{:S(2)}, u32[]{:S(2)}) collective-permute-start(bf16[512,512]{1,0:T(8,128)(2,1)S(1)} %shard_map.57.refs_1_), channel_id=1, source_target_pairs={{0,3},{1,0},{2,1},{3,2},{4,7},{5,4},{6,5},{7,6},{8,11},{9,8},{10,9... | collective-permute-start | bytes 1572872 | tf_op jit(solution)/shard_map/ppermute | solution.py:207
  45.4 14.8 %collective-permute-start.13 = (bf16[512,512]{1,0:T(8,128)(2,1)S(1)}, bf16[512,512]{1,0:T(8,128)(2,1)S(1)}, u32[]{:S(2)}, u32[]{:S(2)}) collective-permute-start(bf16[512,512]{1,0:T(8,128)(2,1)S(1)} %shard_map.57.refs_1_), channel_id=1, source_target_pairs={{0,1},{1,2},{2,3},{3,0},{4,5},{5,6},{6,7},{7,4},{8,9},{9,10},{10,1... | collective-permute-start | bytes 1572872 | tf_op jit(solution)/shard_map/ppermute | solution.py:207
  46.6 21.4 %collective-permute-start.11 = (bf16[512,512]{1,0:T(8,128)(2,1)S(1)}, bf16[512,512]{1,0:T(8,128)(2,1)S(1)}, u32[]{:S(2)}, u32[]{:S(2)}) collective-permute-start(bf16[512,512]{1,0:T(8,128)(2,1)S(1)} %shard_map.55.refs_1_.refs_4_.refs_5_.refs_2_.refs_3_), channel_id=1, source_target_pairs={{0,3},{1,0},{2,1},{3,2},{4,7},{5,4},{6,5},{7,6},{8,11},{9,8},{10,9... | collective-permute-start | bytes 1572872 | tf_op jit(solution)/shard_map/ppermute | solution.py:207
  49.3 22.1 %collective-permute-start.9 = (bf16[512,512]{1,0:T(8,128)(2,1)S(1)}, bf16[512,512]{1,0:T(8,128)(2,1)S(1)}, u32[]{:S(2)}, u32[]{:S(2)}) collective-permute-start(bf16[512,512]{1,0:T(8,128)(2,1)S(1)} %shard_map.55.refs_1_.refs_4_.refs_5_.refs_2_.refs_3_), channel_id=1, source_target_pairs={{0,1},{1,2},{2,3},{3,0},{4,5},{5,6},{6,7},{7,4},{8,9},{9,10},{10,1... | collective-permute-start | bytes 1572872 | tf_op jit(solution)/shard_map/ppermute | solution.py:207
  56.7 3.5 %copy-start.7 = (bf16[512,512]{1,0:T(8,128)(2,1)}, bf16[512,512]{1,0:T(8,128)(2,1)S(1)}, u32[]{:S(2)}) copy-start(bf16[512,512]{1,0:T(8,128)(2,1)S(1)} %collective-permute-done.14.refs_3_) | copy-start | bytes 1572868
  56.7 19.5 %collective-permute-start.16 = (bf16[256,512]{1,0:T(8,128)(2,1)S(1)}, bf16[256,512]{1,0:T(8,128)(2,1)S(1)}, u32[]{:S(2)}, u32[]{:S(2)}) collective-permute-start(bf16[256,512]{1,0:T(8,128)(2,1)S(1)} %slice.19), channel_id=1, source_target_pairs={{0,3},{1,0},{2,1},{3,2},{4,7},{5,4},{6,5},{7,6},{8,11},{9,8},{10,9... | collective-permute-start | bytes 786440 | tf_op jit(solution)/shard_map/ppermute | solution.py:207
  60.2 0.8 copy-start.9
  61.0 15.8 %collective-permute-start.15 = (bf16[256,512]{1,0:T(8,128)(2,1)S(1)}, bf16[256,512]{1,0:T(8,128)(2,1)}, u32[]{:S(2)}, u32[]{:S(2)}) collective-permute-start(bf16[256,512]{1,0:T(8,128)(2,1)S(1)} %slice.18), channel_id=1, source_target_pairs={{0,1},{1,2},{2,3},{3,0},{4,5},{5,6},{6,7},{7,4},{8,9},{9,10},{10,1... | collective-permute-start | bytes 786440 | tf_op jit(solution)/shard_map/ppermute | solution.py:207
  67.9 13.5 %collective-permute-start.12 = (bf16[256,512]{1,0:T(8,128)(2,1)S(1)}, bf16[256,512]{1,0:T(8,128)(2,1)S(1)}, u32[]{:S(2)}, u32[]{:S(2)}) collective-permute-start(bf16[256,512]{1,0:T(8,128)(2,1)S(1)} %slice.17), channel_id=1, source_target_pairs={{0,3},{1,0},{2,1},{3,2},{4,7},{5,4},{6,5},{7,6},{8,11},{9,8},{10,9... | collective-permute-start | bytes 786440 | tf_op jit(solution)/shard_map/ppermute | solution.py:207
  71.4 10.8 %collective-permute-start.10 = (bf16[256,512]{1,0:T(8,128)(2,1)S(1)}, bf16[256,512]{1,0:T(8,128)(2,1)S(1)}, u32[]{:S(2)}, u32[]{:S(2)}) collective-permute-start(bf16[256,512]{1,0:T(8,128)(2,1)S(1)} %slice.16), channel_id=1, source_target_pairs={{0,1},{1,2},{2,3},{3,0},{4,5},{5,6},{6,7},{7,4},{8,9},{9,10},{10,1... | collective-permute-start | bytes 786440 | tf_op jit(solution)/shard_map/ppermute | solution.py:207
  71.5 2.2 %copy-start = (bf16[2048,1024]{1,0:T(8,128)(2,1)S(1)}, bf16[2048,1024]{1,0:T(8,128)(2,1)}, u32[]{:S(2)}) copy-start(bf16[2048,1024]{1,0:T(8,128)(2,1)} %refs_6_.5) | copy-start | bytes 12582916
  73.7 3.0 %copy-start.1 = (bf16[2048,1024]{1,0:T(8,128)(2,1)S(1)}, bf16[2048,1024]{1,0:T(8,128)(2,1)}, u32[]{:S(2)}) copy-start(bf16[2048,1024]{1,0:T(8,128)(2,1)} %refs_6_.5) | copy-start | bytes 12582916
  73.7 3.0 %copy-start.8 = (bf16[512,512]{1,0:T(8,128)(2,1)S(1)}, bf16[512,512]{1,0:T(8,128)(2,1)}, u32[]{:S(2)}) copy-start(bf16[512,512]{1,0:T(8,128)(2,1)} %copy-done.7) | copy-start | bytes 1572868
  73.7 3.0 %copy-start.10 = (bf16[512,512]{1,0:T(8,128)(2,1)S(1)}, bf16[512,512]{1,0:T(8,128)(2,1)}, u32[]{:S(2)}) copy-start(bf16[512,512]{1,0:T(8,128)(2,1)} %copy-done.9) | copy-start | bytes 1572868

commit v2 on v1

v2 whole, which is shorter than its diff:
```python
import jax
import jax.numpy as jnp
from jax import lax
from jax.experimental import pallas as pl
from jax.experimental.pallas import tpu as pltpu
from jax.sharding import Mesh
from jax.sharding import PartitionSpec as P

DH = 128
SEG = 256
SEQ = ("seq_0", "seq_1", "seq_2")
BF = jnp.bfloat16
F32 = jnp.float32
ROWS = DH + 8


def feature(x):
    x = x.astype(F32)
    return jnp.where(x > 0.0, x + 1.0, jnp.exp(jnp.minimum(x, 0.0)))


def fetch(sources, targets, sems):
    segs = targets[0].shape[0] // SEG
    copies = []
    for s in range(segs):
        rows = pl.ds(s * SEG, SEG)
        group = []
        for i, (source, target) in enumerate(zip(sources, targets)):
            copy = pltpu.make_async_copy(source.at[rows], target.at[rows], sems.at[s * len(sources) + i])
            copy.start()
            group.append(copy)
        copies.append(group)
    return copies


def state_kernel(k_hbm, v_hbm, total_ref, inner_ref, norm_ref, k_ref, v_ref, sems):
    segs = k_ref.shape[0] // SEG
    heads = k_ref.shape[1] // DH
    copies = fetch((k_hbm, v_hbm), (k_ref, v_ref), sems)
    norms = [jnp.zeros((ROWS - DH, DH), F32)] * heads
    for s in range(segs):
        rows = slice(s * SEG, (s + 1) * SEG)
        for copy in copies[s]:
            copy.wait()
        for h in range(heads):
            cols = slice(h * DH, (h + 1) * DH)
            norm_ref[h, s : s + 1, :] = norms[h][:1]
            key_map = feature(k_ref[rows, cols]).astype(BF)
            mem = lax.dot_general(
                key_map, v_ref[rows, cols], (((0,), (0,)), ((), ())), preferred_element_type=F32
            )
            if s > 0:
                mem = mem + inner_ref[s - 1, h]
            norms[h] = norms[h] + jnp.dot(jnp.ones((ROWS - DH, SEG), BF), key_map, preferred_element_type=F32)
            if s < segs - 1:
                inner_ref[s, h] = mem
            else:
                total_ref[h, :DH, :] = mem
                total_ref[h, DH:, :] = norms[h]


def local_kernel(gate_ref, q_hbm, k_hbm, v_hbm, out_ref, q_ref, k_ref, v_ref, sems):
    heads = q_ref.shape[1] // DH
    scale = 1.0 / DH**0.5 * 1.4426950408889634
    copies = fetch((q_hbm, k_hbm, v_hbm), (q_ref, k_ref, v_ref), sems)
    for s in range(q_ref.shape[0] // SEG):
        rows = slice(s * SEG, (s + 1) * SEG)
        for copy in copies[s]:
            copy.wait()
        for h in range(heads):
            cols = slice(h * DH, (h + 1) * DH)
            rest = 1.0 - gate_ref[h : h + 1, :]
            scores = lax.dot_general(
                q_ref[rows, cols], k_ref[rows, cols], (((1,), (1,)), ((), ())), preferred_element_type=F32
            )
            row_at = lax.broadcasted_iota(jnp.int32, (SEG, SEG), 0)
            col_at = lax.broadcasted_iota(jnp.int32, (SEG, SEG), 1)
            scores = jnp.where(row_at >= col_at, scores * scale, -1e30)
            weights = jnp.exp2(scores - jnp.max(scores, axis=1, keepdims=True)).astype(BF)
            wide = jnp.concatenate([v_ref[rows, cols], jnp.ones((SEG, DH), BF)], axis=1)
            out = jnp.dot(weights, wide, preferred_element_type=F32)
            out_ref[rows, cols] = (out[:, :DH] * (rest / out[:, DH:])).astype(out_ref.dtype)


def context_kernel(first, gate_ref, q_ref, local_ref, own_ref, swapped_ref, inner_ref, norm_ref, out_ref):
    heads = q_ref.shape[1] // DH
    front = gate_ref[heads : heads + 1, :] == 0.0
    for h in range(heads):
        cols = slice(h * DH, (h + 1) * DH)
        low = h < heads // 2
        part = slice(h % (heads // 2) * ROWS, h % (heads // 2) * ROWS + DH + 1)
        own, swapped = own_ref[part, :], swapped_ref[part, :].astype(F32)
        before = jnp.where(front, own, swapped) if low else jnp.where(front, swapped, own)
        for i in range(out_ref.shape[0] // SEG):
            s = first + i
            rows = slice(s * SEG, (s + 1) * SEG)
            outs = slice(i * SEG, (i + 1) * SEG)
            query_map = feature(q_ref[rows, cols]).astype(BF)
            mem = before[:DH]
            norm = before[DH : DH + 1] + norm_ref[h, s : s + 1, :]
            if s > 0:
                mem = mem + inner_ref[s - 1, h]
            norm = jnp.broadcast_to(norm.astype(BF), (DH, DH))
            top = jnp.dot(query_map, mem.astype(BF), preferred_element_type=F32)
            bottom = lax.dot_general(query_map, norm, (((1,), (1,)), ((), ())), preferred_element_type=F32)
            recall = gate_ref[h : h + 1, :] * (top / (bottom + 1.0))
            out_ref[outs, cols] = (recall + local_ref[rows, cols].astype(F32)).astype(BF)


def most_kernel(at_ref, own_ref, prev_ref, next_ref, w_ref, out_ref, *far_refs):
    width = own_ref.shape[1]
    groups = w_ref.shape[0] // width
    tile = w_ref.shape[1] // 4
    for j in range(4):
        cols = slice(j * tile, (j + 1) * tile)

        def part(offset):
            start = pl.multiple_of(lax.rem(at_ref[0] + offset, groups) * width, width)
            return w_ref[pl.ds(start, width), cols]

        acc = jnp.dot(own_ref[...], part(0), preferred_element_type=F32)
        acc = acc + jnp.dot(prev_ref[...], part(groups - 1), preferred_element_type=F32)
        out_ref[:, cols] = acc + jnp.dot(next_ref[...], part(1), preferred_element_type=F32)
        for far_ref in far_refs:
            far_ref[:, cols] = part(2)


def rest_kernel(first, most_ref, far_a_ref, far_b_ref, w_ref, *refs):
    out_ref, done_ref, sems = refs[-3:]
    rows, n = done_ref.shape
    tile = n // 4
    far = jnp.concatenate([far_a_ref[...], far_b_ref[...]], axis=0)
    copies = []
    for j in range(4):
        cols = pl.ds(j * tile, tile)
        acc = most_ref[:, cols] + jnp.dot(far, w_ref[:, cols], preferred_element_type=F32)
        done_ref[:, cols] = acc.astype(done_ref.dtype)
        copy = pltpu.make_async_copy(done_ref.at[:, cols], out_ref.at[pl.ds(first, rows), cols], sems.at[j])
        copy.start()
        copies.append(copy)
    for copy in copies:
        copy.wait()


VMEM_SPEC = pl.BlockSpec(memory_space=pltpu.VMEM)
SMEM_SPEC = pl.BlockSpec(memory_space=pltpu.SMEM)


def near_core(x):
    return pltpu.with_memory_space_constraint(x, pltpu.VMEM)


def params(mib):
    return pltpu.CompilerParams(vmem_limit_bytes=mib * 2**20)


HBM_SPEC = pl.BlockSpec(memory_space=pltpu.HBM)


def far_core(x):
    return pltpu.with_memory_space_constraint(x, pltpu.HBM)


def state_call(keys, values):
    heads = keys.shape[1] // DH
    segs = keys.shape[0] // SEG
    return pl.pallas_call(
        state_kernel,
        in_specs=[HBM_SPEC] * 2,
        out_specs=(VMEM_SPEC,) * 3,
        out_shape=(
            pltpu.VMEM((heads, ROWS, DH), F32),
            pltpu.VMEM((segs - 1, heads, DH, DH), F32),
            pltpu.VMEM((heads, 8, DH), F32),
        ),
        scratch_shapes=[pltpu.VMEM(keys.shape, BF)] * 2 + [pltpu.SemaphoreType.DMA((2 * segs,))],
        compiler_params=params(4),
        name="state",
    )(far_core(keys), far_core(values))


def local_call(gate, q, k, v):
    n, width = q.shape
    return pl.pallas_call(
        local_kernel,
        in_specs=[VMEM_SPEC] + [HBM_SPEC] * 3,
        out_specs=VMEM_SPEC,
        out_shape=pltpu.VMEM((n, width), BF),
        scratch_shapes=[pltpu.VMEM(q.shape, BF)] * 3 + [pltpu.SemaphoreType.DMA((3 * n // SEG,))],
        compiler_params=params(6),
        cost_estimate=pl.CostEstimate(
            flops=4 * n * SEG * width, transcendentals=n * SEG * 4, bytes_accessed=8 * n * width
        ),
        name="local",
    )(gate, *map(far_core, (q, k, v)))


def context_call(first, count, gate, q, local, own, swapped, inner, norm):
    return pl.pallas_call(
        lambda *refs: context_kernel(first, *refs),
        in_specs=[VMEM_SPEC] * 7,
        out_specs=VMEM_SPEC,
        out_shape=pltpu.VMEM((count * SEG, q.shape[1]), BF),
        compiler_params=params(3),
        cost_estimate=pl.CostEstimate(
            flops=4 * count * SEG * q.shape[1] * DH, transcendentals=0, bytes_accessed=6 * count * SEG * q.shape[1]
        ),
    )(gate, q, local, near_core(own), near_core(swapped), inner, norm)


def most_call(at, own, prev, nxt, weight, far_rows):
    rows, n = own.shape[0], weight.shape[1]
    return pl.pallas_call(
        most_kernel,
        in_specs=[SMEM_SPEC] + [VMEM_SPEC] * 4,
        out_specs=(VMEM_SPEC,) * (1 + far_rows),
        out_shape=(pltpu.VMEM((rows, n), F32),) + (pltpu.VMEM((own.shape[1], n), BF),) * far_rows,
        compiler_params=params(4),
        cost_estimate=pl.CostEstimate(
            flops=2 * rows * weight.shape[0] * n, transcendentals=0, bytes_accessed=2 * weight.shape[0] * n
        ),
    )(at, own, near_core(prev), near_core(nxt), weight)


def rest_call(most, far_a, far_b, weight, total_rows, first, so_far):
    rows, n = most.shape
    operands = [most, near_core(far_a), near_core(far_b), weight]
    specs = [VMEM_SPEC] * 4
    aliases = {}
    if so_far is not None:
        aliases = {len(operands): 0}
        operands.append(so_far)
        specs.append(pl.BlockSpec(memory_space=pl.ANY))
    return pl.pallas_call(
        lambda *refs: rest_kernel(first, *refs),
        in_specs=specs,
        out_specs=pl.BlockSpec(memory_space=pl.ANY),
        out_shape=jax.ShapeDtypeStruct((total_rows, n), BF),
        scratch_shapes=[pltpu.VMEM((rows, n), BF), pltpu.SemaphoreType.DMA((4,))],
        input_output_aliases=aliases,
        compiler_params=params(4),
        cost_estimate=pl.CostEstimate(
            flops=2 * rows * far_a.shape[1] * n, transcendentals=0, bytes_accessed=8 * rows * n
        ),
    )(*operands)


def ring(size, step):
    return [(i, (i + step) % size) for i in range(size)]


def turn(value, axis, step):
    return lax.ppermute(value, axis, ring(lax.axis_size(axis), step))


def plane_kernel(at_ref, mine_ref, got_ref, *refs):
    *piece_refs, plane_ref, sent_ref, before_ref = refs
    x = at_ref[1:2, :]
    plane = mine_ref[...] + got_ref[...].astype(F32)
    before = jnp.zeros_like(plane)
    for k, ref in enumerate(piece_refs):
        piece = ref[...].astype(F32)
        plane = plane + piece
        before = before + jnp.where(x > k, piece, 0.0)
    plane_ref[...] = plane
    sent_ref[...] = plane.astype(BF)
    before_ref[...] = before


def window_kernel(size, at_ref, plane_ref, below_ref, above_ref, in_ref, window_ref, distant_ref, before_ref):
    z = at_ref[2:3, :]
    below = below_ref[...].astype(F32)
    above = above_ref[...].astype(F32)
    window = plane_ref[...] + jnp.where(z > 0.0, below, 0.0) + jnp.where(z < size - 1.0, above, 0.0)
    window_ref[...] = window.astype(BF)
    distant_ref[...] = jnp.where(z == size - 1.0, above, window).astype(BF)
    before_ref[...] = in_ref[...] + jnp.where(z == 1.0, below, 0.0) + jnp.where(z == size - 1.0, above, 0.0)


def before_kernel(at_ref, in_ref, lower_ref, upper_ref, mine_ref, got_ref, own_ref, sent_ref):
    first = at_ref[0:1, :] == 0.0
    z = at_ref[2:3, :]
    before = in_ref[...] + jnp.where(z >= 4.0, lower_ref[...].astype(F32), 0.0)
    before = before + jnp.where(z >= 2.0, upper_ref[...].astype(F32), 0.0)
    sent_ref[...] = jnp.where(first, before + mine_ref[...], before).astype(BF)
    own_ref[...] = jnp.where(first, before, before + got_ref[...].astype(F32))


def glue_call(kernel, at, arrays, dtypes):
    return pl.pallas_call(
        kernel,
        in_specs=[VMEM_SPEC] * (1 + len(arrays)),
        out_specs=(VMEM_SPEC,) * len(dtypes),
        out_shape=tuple(pltpu.VMEM(arrays[0].shape, dtype) for dtype in dtypes),
        compiler_params=params(2),
    )(at, *map(near_core, arrays))


def states_before(total, at):
    heads = total.shape[0]
    halves = total.reshape(2, heads // 2 * ROWS, DH)
    core = lax.axis_index("seq_2")
    mine = lax.dynamic_index_in_dim(halves, core, 0, keepdims=False)
    theirs = lax.dynamic_index_in_dim(halves, 1 - core, 0, keepdims=False)
    got = lax.ppermute(theirs.astype(BF), "seq_2", ring(2, 1))
    sent = (mine + got.astype(F32)).astype(BF)
    size = lax.axis_size("seq_1")
    pieces = [lax.ppermute(sent, "seq_1", ring(size, k)) for k in range(1, size)]
    plane, sent, before = glue_call(plane_kernel, at, (mine, got, *pieces), (F32, BF, F32))
    size = lax.axis_size("seq_0")
    below = lax.ppermute(sent, "seq_0", ring(size, 1))
    above = lax.ppermute(sent, "seq_0", ring(size, -1))
    window, distant, before = glue_call(
        lambda *refs: window_kernel(size, *refs), at, (plane, below, above, before), (BF, BF, F32)
    )
    lower = lax.ppermute(distant, "seq_0", [(0, 5), (1, 6), (2, 7), (7, 4)])
    upper = lax.ppermute(window, "seq_0", [(i, i + 2) for i in range(size - 2)])
    own, sent = glue_call(before_kernel, at, (before, lower, upper, mine, got), (F32, BF))
    return own, lax.ppermute(sent, "seq_2", ring(2, 1))


def layer(queries, keys, values, gate_bias, out_weight):
    rows = queries.shape[0]
    spans = ((0, 2), (2, 2))
    near_at = jnp.stack([lax.axis_index(axis).astype(F32) for axis in reversed(SEQ)])
    near_at = jnp.pad(jnp.broadcast_to(near_at[:, None], (3, DH)), ((0, 5), (0, 0)))
    gate = jnp.broadcast_to(jax.nn.sigmoid(gate_bias)[:, None], (gate_bias.shape[0], DH))
    gate = near_core(jnp.concatenate([gate, near_at[:4]], axis=0))
    near_at = near_core(near_at)
    at = jnp.full((1,), lax.axis_index("head"), jnp.int32)
    total, inner, norm = state_call(keys, values)
    own_before, swapped_before = states_before(total, near_at)
    near_q = near_core(queries)
    local = local_call(gate, queries, keys, values)
    weight = near_core(out_weight)
    out = far_weight = None
    pieces = []
    for c, (first, count) in enumerate(spans):
        own = context_call(first, count, gate, near_q, local, own_before, swapped_before, inner, norm)
        half = own.shape[0] // 2
        prev = turn(own, "head", 1)
        nxt = turn(own, "head", -1)
        far_a = turn(prev[:half], "head", 1)
        far_b = turn(nxt[half:], "head", -1)
        most, *extra = most_call(at, own, prev, nxt, weight, c == 1)
        far_weight = extra[0] if extra else far_weight
        pieces.append((most, far_a, far_b))
    for c, (first, count) in enumerate(spans):
        out = rest_call(*pieces[c], far_weight, rows, first * SEG, out)
    return out


def solution(mesh):
    finer = Mesh(
        mesh.devices.reshape(8, 4, 2, mesh.shape["head"]), ("seq_0", "seq_1", "seq_2", "head")
    )
    placed = (P(SEQ, "head"), P(SEQ, "head"), P(SEQ, "head"), P("head"), P(None, "head"))
    return jax.shard_map(layer, mesh=finer, in_specs=placed, out_specs=P(SEQ, "head"), check_vma=False)
```

time: 84.9 us -> 79.5 us (0.936)
  local copies, waits for them, and re-layouts: 6.74 us -> 2.43 us
  starting transfers between devices: 32.6 us -> 35.5 us
  waiting for transfers between devices: 28.4 us -> 26.3 us
  other arithmetic: 1.85 us -> 0.18 us
    unnamed x24 -> x6, local copies, waits for them, and re-layouts: 6.65 us -> 2.19 us
    ppermute x17, starting transfers between devices: 32.6 us -> 35.5 us  [the longest x8 11.4 us: turn(): return lax.ppermute(value, axis, ring(lax.axis_size(axis), step))]
    ppermute x17, waiting for transfers between devices: 28.4 us -> 26.3 us  [the longest x8 19.3 us: turn(): return lax.ppermute(value, axis, ring(lax.axis_size(axis), step))]
    convert_element_type x4 -> x1, other arithmetic: 1.78 us -> 0.02 us  [states_before(): sent = (mine + got.astype(F32)).astype(BF)]
    pallas_call x7 -> x11, Pallas kernels: 14.8 us -> 14.6 us  [the longest x1 3.87 us: local_call(): pl.pallas_call(local_kernel, in_specs=[VMEM_SPEC] + [HBM_SPEC] * 3, out_s...]
  transfers between devices with their start and end apart: 17 -> 17, of which waited for: 11 -> 9; matrix products, arithmetic and copies ran while one was open for 0% -> 0% of each run, Pallas kernels for 12% -> 12%
where the time goes in v2:
time: 79.5 us; the launch traced here: 79.4 us
  starting transfers between devices  35.5 us (45%)
  waiting for transfers between devices  26.3 us (33%)
  Pallas kernels  14.6 us (18%)
  local copies, waits for them, and re-layouts  2.43 us (3%)
    ppermute x8, waiting for transfers between devices, turn(): return lax.ppermute(value, axis, ring(lax.axis_size(axis), step))  19.3 us
    ppermute x8, starting transfers between devices, turn(): return lax.ppermute(value, axis, ring(lax.axis_size(axis), step))  11.4 us
    ppermute x1, starting transfers between devices, states_before(): lower = lax.ppermute(distant, 'seq_0', [(0, 5), (1, 6), (2, 7), (7, 4)])  4.99 us
    ppermute x1, starting transfers between devices, states_before(): return (own, lax.ppermute(sent, 'seq_2', ring(2, 1)))  4.14 us
    ppermute x1, starting transfers between devices, states_before(): above = lax.ppermute(sent, 'seq_0', ring(size, -1))  4.03 us
    pallas_call x1, Pallas kernels, local_call(): pl.pallas_call(local_kernel, in_specs=[VMEM_SPEC] + [HBM_SPEC] * 3, out_s...  3.87 us
    pallas_call x2, Pallas kernels, most_call(): pl.pallas_call(most_kernel, in_specs=[SMEM_SPEC] + [VMEM_SPEC] * 4, out_s...  3.72 us
    ppermute x1, starting transfers between devices, states_before(): upper = lax.ppermute(window, 'seq_0', [(i, i + 2) for i in range(size - 2)])  3.66 us
  transfers between devices with their start and end apart: 17, of which 9 were waited for; matrix products, arithmetic and copies ran while one was open for 0% of the time, Pallas kernels for 12%

profile of v2, /device:TPU:1, one launch (start us, length us, event | category | flops | bytes accessed | tf_op | source)
XLA Modules:
  0.0 79.4 jit_solution(3135315412394126434)
XLA Ops:
  0.0 0.0 copy-start.2
  0.0 2.4 %state.1 = (f32[4,136,128]{2,1,0:T(8,128)S(1)}, f32[3,4,128,128]{3,2,1,0:T(8,128)S(1)}, f32[4,8,128]{2,1,0:T(8,128)S(1)}) custom-call(bf16[1024,512]{1,0:T(8,128)(2,1)} %k_hbm.3, bf16[1024,512]{1,0:T(8,128)(2,1)} %v_hbm.3), custom_call_target="tpu_custom_call" | custom-call | tf_op jit(solution)/shard_map/state/pallas_call | solution.py:167
  2.4 3.3 %collective-permute-start = (bf16[272,128]{1,0:T(8,128)(2,1)S(1)}, bf16[272,128]{1,0:T(8,128)(2,1)S(1)}, u32[]{:S(2)}, u32[]{:S(2)}) collective-permute-start(bf16[272,128]{1,0:T(8,128)(2,1)S(1)} %fusion), channel_id=1, source_target_pairs={{0,4},{4,0},{1,5},{5,1},{2,6},{6,2},{3,7},{7,3},{8,12},{12,8},{9,1... | collective-permute-start | bytes 208904 | tf_op jit(solution)/shard_map/ppermute | solution.py:305
  5.7 0.9 %collective-permute-done.got_ref = bf16[272,128]{1,0:T(8,128)(2,1)S(1)} collective-permute-done((bf16[272,128]{1,0:T(8,128)(2,1)S(1)}, bf16[272,128]{1,0:T(8,128)(2,1)S(1)}, u32[]{:S(2)}, u32[]{:S(2)}) %collective-permute-start) | collective-permute-done | bytes 69664 | tf_op jit(solution)/shard_map/ppermute | solution.py:305
  6.7 0.1 collective-permute-start.1
  6.8 1.9 %collective-permute-start.2 = (bf16[272,128]{1,0:T(8,128)(2,1)S(1)}, bf16[272,128]{1,0:T(8,128)(2,1)S(1)}, u32[]{:S(2)}, u32[]{:S(2)}) collective-permute-start(bf16[272,128]{1,0:T(8,128)(2,1)S(1)} %get-tuple-element.31), channel_id=1, source_target_pairs={{0,16},{8,24},{16,0},{24,8},{1,17},{9,25},{17,1},{25,9},{2,18},{10... | collective-permute-start | bytes 208904 | tf_op jit(solution)/shard_map/ppermute | solution.py:308
  8.7 1.2 %collective-permute-start.3 = (bf16[272,128]{1,0:T(8,128)(2,1)S(1)}, bf16[272,128]{1,0:T(8,128)(2,1)S(1)}, u32[]{:S(2)}, u32[]{:S(2)}) collective-permute-start(bf16[272,128]{1,0:T(8,128)(2,1)S(1)} %get-tuple-element.31), channel_id=1, source_target_pairs={{0,24},{8,0},{16,8},{24,16},{1,25},{9,1},{17,9},{25,17},{2,26},{10... | collective-permute-start | bytes 208904 | tf_op jit(solution)/shard_map/ppermute | solution.py:308
  9.9 0.1 select_maximum_fusion
  9.9 2.1 %collective-permute-done.1.refs_0_ = bf16[272,128]{1,0:T(8,128)(2,1)S(1)} collective-permute-done((bf16[272,128]{1,0:T(8,128)(2,1)S(1)}, bf16[272,128]{1,0:T(8,128)(2,1)S(1)}, u32[]{:S(2)}, u32[]{:S(2)}) %collective-permute-start.1) | collective-permute-done | bytes 69664 | tf_op jit(solution)/shard_map/ppermute | solution.py:308
  12.0 0.6 collective-permute-done.2.refs_1_
  12.6 0.6 collective-permute-done.3.refs_2_
  13.1 0.1 pad.10.at_ref.refs_0_
  13.2 0.1 shard_map.55
  13.3 0.7 collective-permute-start.4
  14.0 4.0 %collective-permute-start.5 = (bf16[272,128]{1,0:T(8,128)(2,1)S(1)}, bf16[272,128]{1,0:T(8,128)(2,1)S(1)}, u32[]{:S(2)}, u32[]{:S(2)}) collective-permute-start(bf16[272,128]{1,0:T(8,128)(2,1)S(1)} %get-tuple-element.20), channel_id=1, source_target_pairs={{0,224},{32,0},{64,32},{96,64},{128,96},{160,128},{192,160},{224,1... | collective-permute-start | bytes 208904 | tf_op jit(solution)/shard_map/ppermute | solution.py:312
  18.1 1.6 %collective-permute-done.4.refs_2_ = bf16[272,128]{1,0:T(8,128)(2,1)S(1)} collective-permute-done((bf16[272,128]{1,0:T(8,128)(2,1)S(1)}, bf16[272,128]{1,0:T(8,128)(2,1)S(1)}, u32[]{:S(2)}, u32[]{:S(2)}) %collective-permute-start.4) | collective-permute-done | bytes 69664 | tf_op jit(solution)/shard_map/ppermute | solution.py:311
  19.7 0.0 collective-permute-done.5.refs_3_
  19.7 0.1 shard_map.56
  19.7 5.0 %collective-permute-start.6 = (bf16[272,128]{1,0:T(8,128)(2,1)S(1)}, bf16[272,128]{1,0:T(8,128)(2,1)S(1)}, u32[]{:S(2)}, u32[]{:S(2)}) collective-permute-start(bf16[272,128]{1,0:T(8,128)(2,1)S(1)} %get-tuple-element.23), channel_id=1, source_target_pairs={{0,160},{32,192},{64,224},{224,128},{1,161},{33,193},{65,225},{225... | collective-permute-start | bytes 208904 | tf_op jit(solution)/shard_map/ppermute | solution.py:316
  24.7 3.7 %collective-permute-start.7 = (bf16[272,128]{1,0:T(8,128)(2,1)S(1)}, bf16[272,128]{1,0:T(8,128)(2,1)S(1)}, u32[]{:S(2)}, u32[]{:S(2)}) collective-permute-start(bf16[272,128]{1,0:T(8,128)(2,1)S(1)} %get-tuple-element.24), channel_id=1, source_target_pairs={{0,64},{32,96},{64,128},{96,160},{128,192},{160,224},{1,65},{33,97... | collective-permute-start | bytes 208904 | tf_op jit(solution)/shard_map/ppermute | solution.py:317
  28.4 0.0 copy-done.2
  28.4 0.0 collective-permute-done.6.lower_ref
  28.4 1.3 %collective-permute-done.7.upper_ref = bf16[272,128]{1,0:T(8,128)(2,1)S(1)} collective-permute-done((bf16[272,128]{1,0:T(8,128)(2,1)S(1)}, bf16[272,128]{1,0:T(8,128)(2,1)S(1)}, u32[]{:S(2)}, u32[]{:S(2)}) %collective-permute-start.7) | collective-permute-done | bytes 69664 | tf_op jit(solution)/shard_map/ppermute | solution.py:317
  29.8 0.1 shard_map.57
  29.8 4.1 %collective-permute-start.8 = (bf16[272,128]{1,0:T(8,128)(2,1)S(1)}, bf16[272,128]{1,0:T(8,128)(2,1)S(1)}, u32[]{:S(2)}, u32[]{:S(2)}) collective-permute-start(bf16[272,128]{1,0:T(8,128)(2,1)S(1)} %get-tuple-element.26), channel_id=1, source_target_pairs={{0,4},{4,0},{1,5},{5,1},{2,6},{6,2},{3,7},{7,3},{8,12},{12,8},{9,1... | collective-permute-start | bytes 208904 | tf_op jit(solution)/shard_map/ppermute | solution.py:319
  34.0 0.1 pad_maximum_fusion
  34.0 0.1 broadcast.11.gate_ref.refs_0_
  34.1 0.0 copy-start
  34.1 3.9 %local.1.refs_2_ = bf16[1024,512]{1,0:T(8,128)(2,1)S(1)} custom-call(f32[8,128]{1,0:T(8,128)S(1)} %broadcast.11.gate_ref.refs_0_, bf16[1024,512]{1,0:T(8,128)(2,1)} %refs_1_.3, bf16[1024,512]{1,0:T(8,128)(2,1)} %k_hbm.3, bf16[1024,512]{1,0:T(8,128)(2,1)} %v_hbm.3), custom_call_target="tpu_custom_call" | custom-call | flops 536870912 | bytes 4194304 | tf_op jit(solution)/shard_map/local/pallas_call | solution.py:184
  38.0 0.0 collective-permute-done.8.refs_4_
  38.0 0.0 copy-done
  38.0 0.6 shard_map.58.own_ref
  38.6 1.4 %collective-permute-start.9 = (bf16[512,512]{1,0:T(8,128)(2,1)S(1)}, bf16[512,512]{1,0:T(8,128)(2,1)S(1)}, u32[]{:S(2)}, u32[]{:S(2)}) collective-permute-start(bf16[512,512]{1,0:T(8,128)(2,1)S(1)} %shard_map.58.own_ref), channel_id=1, source_target_pairs={{0,1},{1,2},{2,3},{3,0},{4,5},{5,6},{6,7},{7,4},{8,9},{9,10},{10,1... | collective-permute-start | bytes 1572872 | tf_op jit(solution)/shard_map/ppermute | solution.py:253
  40.0 1.5 %collective-permute-start.10 = (bf16[512,512]{1,0:T(8,128)(2,1)S(1)}, bf16[512,512]{1,0:T(8,128)(2,1)S(1)}, u32[]{:S(2)}, u32[]{:S(2)}) collective-permute-start(bf16[512,512]{1,0:T(8,128)(2,1)S(1)} %shard_map.58.own_ref), channel_id=1, source_target_pairs={{0,3},{1,0},{2,1},{3,2},{4,7},{5,4},{6,5},{7,6},{8,11},{9,8},{10,9... | collective-permute-start | bytes 1572872 | tf_op jit(solution)/shard_map/ppermute | solution.py:253
  41.5 0.6 shard_map.60.own_ref
  42.1 0.3 collective-permute-start.13
  42.4 2.7 %collective-permute-start.14 = (bf16[512,512]{1,0:T(8,128)(2,1)S(1)}, bf16[512,512]{1,0:T(8,128)(2,1)S(1)}, u32[]{:S(2)}, u32[]{:S(2)}) collective-permute-start(bf16[512,512]{1,0:T(8,128)(2,1)S(1)} %shard_map.60.own_ref), channel_id=1, source_target_pairs={{0,3},{1,0},{2,1},{3,2},{4,7},{5,4},{6,5},{7,6},{8,11},{9,8},{10,9... | collective-permute-start | bytes 1572872 | tf_op jit(solution)/shard_map/ppermute | solution.py:253
  45.1 8.5 %collective-permute-done.9.prev_ref = bf16[512,512]{1,0:T(8,128)(2,1)S(1)} collective-permute-done((bf16[512,512]{1,0:T(8,128)(2,1)S(1)}, bf16[512,512]{1,0:T(8,128)(2,1)S(1)}, u32[]{:S(2)}, u32[]{:S(2)}) %collective-permute-start.9) | collective-permute-done | bytes 524320 | tf_op jit(solution)/shard_map/ppermute | solution.py:253
  53.5 0.1 collective-permute-start.11
  53.6 0.0 collective-permute-done.10.next_ref
  53.7 2.7 %collective-permute-start.12 = (bf16[256,512]{1,0:T(8,128)(2,1)S(1)}, bf16[256,512]{1,0:T(8,128)(2,1)S(1)}, u32[]{:S(2)}, u32[]{:S(2)}) collective-permute-start(bf16[256,512]{1,0:T(8,128)(2,1)S(1)} %slice.22), channel_id=1, source_target_pairs={{0,3},{1,0},{2,1},{3,2},{4,7},{5,4},{6,5},{7,6},{8,11},{9,8},{10,9... | collective-permute-start | bytes 786440 | tf_op jit(solution)/shard_map/ppermute | solution.py:253
  56.4 8.4 %collective-permute-done.13.prev_ref = bf16[512,512]{1,0:T(8,128)(2,1)S(1)} collective-permute-done((bf16[512,512]{1,0:T(8,128)(2,1)S(1)}, bf16[512,512]{1,0:T(8,128)(2,1)S(1)}, u32[]{:S(2)}, u32[]{:S(2)}) %collective-permute-start.13) | collective-permute-done | bytes 524320 | tf_op jit(solution)/shard_map/ppermute | solution.py:253
  64.8 0.1 collective-permute-start.15
  64.9 0.0 collective-permute-done.14.next_ref
  64.9 2.7 %collective-permute-start.16 = (bf16[256,512]{1,0:T(8,128)(2,1)S(1)}, bf16[256,512]{1,0:T(8,128)(2,1)S(1)}, u32[]{:S(2)}, u32[]{:S(2)}) collective-permute-start(bf16[256,512]{1,0:T(8,128)(2,1)S(1)} %slice.24), channel_id=1, source_target_pairs={{0,3},{1,0},{2,1},{3,2},{4,7},{5,4},{6,5},{7,6},{8,11},{9,8},{10,9... | collective-permute-start | bytes 786440 | tf_op jit(solution)/shard_map/ppermute | solution.py:253
  67.6 0.0 copy-start.1
  67.6 2.2 %copy-done.1 = bf16[2048,1024]{1,0:T(8,128)(2,1)S(1)} copy-done((bf16[2048,1024]{1,0:T(8,128)(2,1)S(1)}, bf16[2048,1024]{1,0:T(8,128)(2,1)}, u32[]{:S(2)}) %copy-start.1) | copy-done | bytes 4194328
  69.8 1.9 %shard_map.59 = (f32[512,1024]{1,0:T(8,128)S(1)}, bf16[512,1024]{1,0:T(8,128)(2,1)S(1)}) custom-call(s32[1]{0:T(128)} %bitcast.at_ref, bf16[512,512]{1,0:T(8,128)(2,1)S(1)} %shard_map.58.own_ref, bf16[512,512]{1,0:T(8,128)(2,1)S(1)} %collective-permute-done.9.prev_ref, bf16[512,512]{1,0:T(8,128)(2,1)S(1)} %collective-permute-done.10.next_ref, ...), custom_call_target="tpu_custom_call" | custom-call | flops 2147483648 | bytes 4194304 | tf_op jit(solution)/shard_map/pallas_call | solution.py:213
  71.7 1.8 %shard_map.61.refs_0_ = f32[512,1024]{1,0:T(8,128)S(1)} custom-call(s32[1]{0:T(128)} %bitcast.at_ref, bf16[512,512]{1,0:T(8,128)(2,1)S(1)} %shard_map.60.own_ref, bf16[512,512]{1,0:T(8,128)(2,1)S(1)} %collective-permute-done.13.prev_ref, bf16[512,512]{1,0:T(8,128)(2,1)S(1)} %collective-permute-done.14.next_ref, bf16[2048,1024]{1,0:T(8,128)(2,1)S(1)} %copy-done.1), custom_call_target="tpu_custom_call" | custom-call | flops 2147483648 | bytes 4194304 | tf_op jit(solution)/shard_map/pallas_call | solution.py:213
  73.5 2.4 %collective-permute-done.15.refs_1_ = bf16[256,512]{1,0:T(8,128)(2,1)S(1)} collective-permute-done((bf16[256,512]{1,0:T(8,128)(2,1)S(1)}, bf16[256,512]{1,0:T(8,128)(2,1)S(1)}, u32[]{:S(2)}, u32[]{:S(2)}) %collective-permute-start.15) | collective-permute-done | bytes 262176 | tf_op jit(solution)/shard_map/ppermute | solution.py:253
  76.0 0.0 collective-permute-done.16.refs_2_
  76.0 1.6 %shard_map.62.refs_4_ = bf16[1024,1024]{1,0:T(8,128)(2,1)} custom-call(f32[512,1024]{1,0:T(8,128)S(1)} %shard_map.61.refs_0_, bf16[256,512]{1,0:T(8,128)(2,1)S(1)} %collective-permute-done.15.refs_1_, bf16[256,512]{1,0:T(8,128)(2,1)S(1)} %collective-permute-done.16.refs_2_, bf16[512,1024]{1,0:T(8,128)(2,1)S(1)} %get-tuple-element.30.refs_3_), custom_call_target="tpu_custom_call" | custom-call | flops 536870912 | bytes 4194304 | tf_op jit(solution)/shard_map/pallas_call | solution.py:234
  77.6 0.0 collective-permute-done.11.refs_1_
  77.6 0.0 collective-permute-done.12.refs_2_
  77.6 1.6 %shard_map.63 = bf16[1024,1024]{1,0:T(8,128)(2,1)} custom-call(f32[512,1024]{1,0:T(8,128)S(1)} %get-tuple-element.29.refs_0_, bf16[256,512]{1,0:T(8,128)(2,1)S(1)} %collective-permute-done.11.refs_1_, bf16[256,512]{1,0:T(8,128)(2,1)S(1)} %collective-permute-done.12.refs_2_, ...), custom_call_target="tpu_custom_call", output_to_operand_aliasing={{}: (4, {})} | custom-call | flops 536870912 | bytes 4194304 | tf_op jit(solution)/shard_map/pallas_call | solution.py:234
  (7 shorter events, 0.1 us)
Async XLA Ops:
  0.0 28.4 %copy-start.2 = (f32[4]{0:T(128)S(1)}, f32[4]{0:T(128)}, u32[]{:S(2)}) copy-start(f32[4]{0:T(128)} %param.8) | copy-start | bytes 52
  2.4 4.2 %collective-permute-start = (bf16[272,128]{1,0:T(8,128)(2,1)S(1)}, bf16[272,128]{1,0:T(8,128)(2,1)S(1)}, u32[]{:S(2)}, u32[]{:S(2)}) collective-permute-start(bf16[272,128]{1,0:T(8,128)(2,1)S(1)} %fusion), channel_id=1, source_target_pairs={{0,4},{4,0},{1,5},{5,1},{2,6},{6,2},{3,7},{7,3},{8,12},{12,8},{9,1... | collective-permute-start | bytes 208904 | tf_op jit(solution)/shard_map/ppermute | solution.py:305
  6.7 5.3 %collective-permute-start.1 = (bf16[272,128]{1,0:T(8,128)(2,1)S(1)}, bf16[272,128]{1,0:T(8,128)(2,1)S(1)}, u32[]{:S(2)}, u32[]{:S(2)}) collective-permute-start(bf16[272,128]{1,0:T(8,128)(2,1)S(1)} %get-tuple-element.31), channel_id=1, source_target_pairs={{0,8},{8,16},{16,24},{24,0},{1,9},{9,17},{17,25},{25,1},{2,10},{10... | collective-permute-start | bytes 208904 | tf_op jit(solution)/shard_map/ppermute | solution.py:308
  6.8 5.8 %collective-permute-start.2 = (bf16[272,128]{1,0:T(8,128)(2,1)S(1)}, bf16[272,128]{1,0:T(8,128)(2,1)S(1)}, u32[]{:S(2)}, u32[]{:S(2)}) collective-permute-start(bf16[272,128]{1,0:T(8,128)(2,1)S(1)} %get-tuple-element.31), channel_id=1, source_target_pairs={{0,16},{8,24},{16,0},{24,8},{1,17},{9,25},{17,1},{25,9},{2,18},{10... | collective-permute-start | bytes 208904 | tf_op jit(solution)/shard_map/ppermute | solution.py:308
  8.7 4.4 %collective-permute-start.3 = (bf16[272,128]{1,0:T(8,128)(2,1)S(1)}, bf16[272,128]{1,0:T(8,128)(2,1)S(1)}, u32[]{:S(2)}, u32[]{:S(2)}) collective-permute-start(bf16[272,128]{1,0:T(8,128)(2,1)S(1)} %get-tuple-element.31), channel_id=1, source_target_pairs={{0,24},{8,0},{16,8},{24,16},{1,25},{9,1},{17,9},{25,17},{2,26},{10... | collective-permute-start | bytes 208904 | tf_op jit(solution)/shard_map/ppermute | solution.py:308
  13.3 6.4 %collective-permute-start.4 = (bf16[272,128]{1,0:T(8,128)(2,1)S(1)}, bf16[272,128]{1,0:T(8,128)(2,1)S(1)}, u32[]{:S(2)}, u32[]{:S(2)}) collective-permute-start(bf16[272,128]{1,0:T(8,128)(2,1)S(1)} %get-tuple-element.20), channel_id=1, source_target_pairs={{0,32},{32,64},{64,96},{96,128},{128,160},{160,192},{192,224},{224... | collective-permute-start | bytes 208904 | tf_op jit(solution)/shard_map/ppermute | solution.py:311
  14.0 5.6 %collective-permute-start.5 = (bf16[272,128]{1,0:T(8,128)(2,1)S(1)}, bf16[272,128]{1,0:T(8,128)(2,1)S(1)}, u32[]{:S(2)}, u32[]{:S(2)}) collective-permute-start(bf16[272,128]{1,0:T(8,128)(2,1)S(1)} %get-tuple-element.20), channel_id=1, source_target_pairs={{0,224},{32,0},{64,32},{96,64},{128,96},{160,128},{192,160},{224,1... | collective-permute-start | bytes 208904 | tf_op jit(solution)/shard_map/ppermute | solution.py:312
  19.7 8.7 %collective-permute-start.6 = (bf16[272,128]{1,0:T(8,128)(2,1)S(1)}, bf16[272,128]{1,0:T(8,128)(2,1)S(1)}, u32[]{:S(2)}, u32[]{:S(2)}) collective-permute-start(bf16[272,128]{1,0:T(8,128)(2,1)S(1)} %get-tuple-element.23), channel_id=1, source_target_pairs={{0,160},{32,192},{64,224},{224,128},{1,161},{33,193},{65,225},{225... | collective-permute-start | bytes 208904 | tf_op jit(solution)/shard_map/ppermute | solution.py:316
  24.7 5.0 %collective-permute-start.7 = (bf16[272,128]{1,0:T(8,128)(2,1)S(1)}, bf16[272,128]{1,0:T(8,128)(2,1)S(1)}, u32[]{:S(2)}, u32[]{:S(2)}) collective-permute-start(bf16[272,128]{1,0:T(8,128)(2,1)S(1)} %get-tuple-element.24), channel_id=1, source_target_pairs={{0,64},{32,96},{64,128},{96,160},{128,192},{160,224},{1,65},{33,97... | collective-permute-start | bytes 208904 | tf_op jit(solution)/shard_map/ppermute | solution.py:317
  29.8 8.2 %collective-permute-start.8 = (bf16[272,128]{1,0:T(8,128)(2,1)S(1)}, bf16[272,128]{1,0:T(8,128)(2,1)S(1)}, u32[]{:S(2)}, u32[]{:S(2)}) collective-permute-start(bf16[272,128]{1,0:T(8,128)(2,1)S(1)} %get-tuple-element.26), channel_id=1, source_target_pairs={{0,4},{4,0},{1,5},{5,1},{2,6},{6,2},{3,7},{7,3},{8,12},{12,8},{9,1... | collective-permute-start | bytes 208904 | tf_op jit(solution)/shard_map/ppermute | solution.py:319
  34.1 3.9 %copy-start = (bf16[1024,512]{1,0:T(8,128)(2,1)S(1)}, bf16[1024,512]{1,0:T(8,128)(2,1)}, u32[]{:S(2)}) copy-start(bf16[1024,512]{1,0:T(8,128)(2,1)} %refs_1_.3) | copy-start | bytes 3145732
  38.6 14.9 %collective-permute-start.9 = (bf16[512,512]{1,0:T(8,128)(2,1)S(1)}, bf16[512,512]{1,0:T(8,128)(2,1)S(1)}, u32[]{:S(2)}, u32[]{:S(2)}) collective-permute-start(bf16[512,512]{1,0:T(8,128)(2,1)S(1)} %shard_map.58.own_ref), channel_id=1, source_target_pairs={{0,1},{1,2},{2,3},{3,0},{4,5},{5,6},{6,7},{7,4},{8,9},{9,10},{10,1... | collective-permute-start | bytes 1572872 | tf_op jit(solution)/shard_map/ppermute | solution.py:253
  40.0 13.6 %collective-permute-start.10 = (bf16[512,512]{1,0:T(8,128)(2,1)S(1)}, bf16[512,512]{1,0:T(8,128)(2,1)S(1)}, u32[]{:S(2)}, u32[]{:S(2)}) collective-permute-start(bf16[512,512]{1,0:T(8,128)(2,1)S(1)} %shard_map.58.own_ref), channel_id=1, source_target_pairs={{0,3},{1,0},{2,1},{3,2},{4,7},{5,4},{6,5},{7,6},{8,11},{9,8},{10,9... | collective-permute-start | bytes 1572872 | tf_op jit(solution)/shard_map/ppermute | solution.py:253
  42.1 22.6 %collective-permute-start.13 = (bf16[512,512]{1,0:T(8,128)(2,1)S(1)}, bf16[512,512]{1,0:T(8,128)(2,1)S(1)}, u32[]{:S(2)}, u32[]{:S(2)}) collective-permute-start(bf16[512,512]{1,0:T(8,128)(2,1)S(1)} %shard_map.60.own_ref), channel_id=1, source_target_pairs={{0,1},{1,2},{2,3},{3,0},{4,5},{5,6},{6,7},{7,4},{8,9},{9,10},{10,1... | collective-permute-start | bytes 1572872 | tf_op jit(solution)/shard_map/ppermute | solution.py:253
  42.4 22.5 %collective-permute-start.14 = (bf16[512,512]{1,0:T(8,128)(2,1)S(1)}, bf16[512,512]{1,0:T(8,128)(2,1)S(1)}, u32[]{:S(2)}, u32[]{:S(2)}) collective-permute-start(bf16[512,512]{1,0:T(8,128)(2,1)S(1)} %shard_map.60.own_ref), channel_id=1, source_target_pairs={{0,3},{1,0},{2,1},{3,2},{4,7},{5,4},{6,5},{7,6},{8,11},{9,8},{10,9... | collective-permute-start | bytes 1572872 | tf_op jit(solution)/shard_map/ppermute | solution.py:253
  53.5 24.1 %collective-permute-start.11 = (bf16[256,512]{1,0:T(8,128)(2,1)S(1)}, bf16[256,512]{1,0:T(8,128)(2,1)S(1)}, u32[]{:S(2)}, u32[]{:S(2)}) collective-permute-start(bf16[256,512]{1,0:T(8,128)(2,1)S(1)} %slice.21), channel_id=1, source_target_pairs={{0,1},{1,2},{2,3},{3,0},{4,5},{5,6},{6,7},{7,4},{8,9},{9,10},{10,1... | collective-permute-start | bytes 786440 | tf_op jit(solution)/shard_map/ppermute | solution.py:253
  53.7 23.9 %collective-permute-start.12 = (bf16[256,512]{1,0:T(8,128)(2,1)S(1)}, bf16[256,512]{1,0:T(8,128)(2,1)S(1)}, u32[]{:S(2)}, u32[]{:S(2)}) collective-permute-start(bf16[256,512]{1,0:T(8,128)(2,1)S(1)} %slice.22), channel_id=1, source_target_pairs={{0,3},{1,0},{2,1},{3,2},{4,7},{5,4},{6,5},{7,6},{8,11},{9,8},{10,9... | collective-permute-start | bytes 786440 | tf_op jit(solution)/shard_map/ppermute | solution.py:253
  64.8 11.2 %collective-permute-start.15 = (bf16[256,512]{1,0:T(8,128)(2,1)S(1)}, bf16[256,512]{1,0:T(8,128)(2,1)S(1)}, u32[]{:S(2)}, u32[]{:S(2)}) collective-permute-start(bf16[256,512]{1,0:T(8,128)(2,1)S(1)} %slice.23), channel_id=1, source_target_pairs={{0,1},{1,2},{2,3},{3,0},{4,5},{5,6},{6,7},{7,4},{8,9},{9,10},{10,1... | collective-permute-start | bytes 786440 | tf_op jit(solution)/shard_map/ppermute | solution.py:253
  64.9 11.1 %collective-permute-start.16 = (bf16[256,512]{1,0:T(8,128)(2,1)S(1)}, bf16[256,512]{1,0:T(8,128)(2,1)S(1)}, u32[]{:S(2)}, u32[]{:S(2)}) collective-permute-start(bf16[256,512]{1,0:T(8,128)(2,1)S(1)} %slice.24), channel_id=1, source_target_pairs={{0,3},{1,0},{2,1},{3,2},{4,7},{5,4},{6,5},{7,6},{8,11},{9,8},{10,9... | collective-permute-start | bytes 786440 | tf_op jit(solution)/shard_map/ppermute | solution.py:253
  67.6 2.2 %copy-start.1 = (bf16[2048,1024]{1,0:T(8,128)(2,1)S(1)}, bf16[2048,1024]{1,0:T(8,128)(2,1)}, u32[]{:S(2)}) copy-start(bf16[2048,1024]{1,0:T(8,128)(2,1)} %w_ref.3) | copy-start | bytes 12582916

commit v3 on v2

v3 whole, which is shorter than its diff:
```python
import jax
import jax.numpy as jnp
from jax import lax
from jax.experimental import pallas as pl
from jax.experimental.pallas import tpu as pltpu
from jax.sharding import Mesh
from jax.sharding import PartitionSpec as P

DH = 128
SEG = 256
SEQ = ("seq_0", "seq_1", "seq_2")
BF = jnp.bfloat16
F32 = jnp.float32
ROWS = DH + 8


def feature(x):
    x = x.astype(F32)
    return jnp.where(x > 0.0, x + 1.0, jnp.exp(jnp.minimum(x, 0.0)))


def fetch(start, sources, targets, sems):
    segs = targets[0].shape[0] // SEG
    copies = []
    for s in range(segs):
        rows = pl.ds(s * SEG, SEG)
        taken = pl.ds(start + s * SEG, SEG)
        group = []
        for i, (source, target) in enumerate(zip(sources, targets)):
            copy = pltpu.make_async_copy(source.at[taken], target.at[rows], sems.at[s * len(sources) + i])
            copy.start()
            group.append(copy)
        copies.append(group)
    return copies


def own_half(heads):
    return lax.axis_index("seq_2") * (heads // 2)


def state_kernel(bias_hbm, k_hbm, v_hbm, total_ref, inner_ref, norm_ref, gate_ref, k_ref, v_ref, bias_ref, sems):
    segs = k_ref.shape[0] // SEG
    heads = k_ref.shape[1] // DH
    first = own_half(heads)
    copies = fetch(0, (k_hbm, v_hbm), (k_ref, v_ref), sems)
    bias_copy = pltpu.make_async_copy(bias_hbm, bias_ref, sems.at[2 * segs])
    bias_copy.start()
    norms = [jnp.zeros((ROWS - DH, DH), F32)] * heads
    for s in range(segs):
        rows = slice(s * SEG, (s + 1) * SEG)
        for copy in copies[s]:
            copy.wait()
        for h in range(heads):
            cols = pl.ds(pl.multiple_of(lax.rem(first + h, heads) * DH, DH), DH)
            norm_ref[h, s : s + 1, :] = norms[h][:1]
            key_map = feature(k_ref[rows, cols]).astype(BF)
            mem = lax.dot_general(
                key_map, v_ref[rows, cols], (((0,), (0,)), ((), ())), preferred_element_type=F32
            )
            if s > 0:
                mem = mem + inner_ref[s - 1, h]
            norms[h] = norms[h] + jnp.dot(jnp.ones((ROWS - DH, SEG), BF), key_map, preferred_element_type=F32)
            if s < segs - 1:
                inner_ref[s, h] = mem
            else:
                total_ref[h, :DH, :] = mem
                total_ref[h, DH:, :] = norms[h]
    bias_copy.wait()
    for h in range(heads):
        bias = jnp.full((1, DH), bias_ref[lax.rem(first + h, heads)], F32)
        gate_ref[h : h + 1, :] = 1.0 / (1.0 + jnp.exp(-bias))


def local_kernel(start, gate_ref, q_hbm, k_hbm, v_hbm, out_ref, map_ref, q_ref, k_ref, v_ref, sems):
    heads = q_ref.shape[1] // DH
    first = own_half(heads)
    scale = 1.0 / DH**0.5 * 1.4426950408889634
    copies = fetch(start, (q_hbm, k_hbm, v_hbm), (q_ref, k_ref, v_ref), sems)
    for s in range(q_ref.shape[0] // SEG):
        rows = slice(s * SEG, (s + 1) * SEG)
        for copy in copies[s]:
            copy.wait()
        for h in range(heads):
            half, at = divmod(h, heads // 2)
            outs = slice(at * DH, (at + 1) * DH)
            cols = pl.ds(pl.multiple_of(lax.rem(first + h, heads) * DH, DH), DH)
            rest = 1.0 - gate_ref[h : h + 1, :]
            query = q_ref[rows, cols]
            map_ref[half, rows, outs] = feature(query).astype(BF)
            scores = lax.dot_general(
                query, k_ref[rows, cols], (((1,), (1,)), ((), ())), preferred_element_type=F32
            )
            row_at = lax.broadcasted_iota(jnp.int32, (SEG, SEG), 0)
            col_at = lax.broadcasted_iota(jnp.int32, (SEG, SEG), 1)
            scores = jnp.where(row_at >= col_at, scores * scale, -1e30)
            weights = jnp.exp2(scores - jnp.max(scores, axis=1, keepdims=True)).astype(BF)
            wide = jnp.concatenate([v_ref[rows, cols], jnp.ones((SEG, DH), BF)], axis=1)
            out = jnp.dot(weights, wide, preferred_element_type=F32)
            out_ref[half, rows, outs] = (out[:, :DH] * (rest / out[:, DH:])).astype(out_ref.dtype)


def context_kernel(half, gate_ref, before_ref, inner_ref, norm_ref, *refs):
    out_ref = refs[-1]
    parts = (len(refs) - 1) // 2
    count = out_ref.shape[1] // DH
    for i in range(count):
        h = half * count + i
        cols = slice(i * DH, (i + 1) * DH)
        before = before_ref[i * ROWS : i * ROWS + DH, :].astype(F32)
        norm_before = before_ref[i * ROWS + DH : i * ROWS + DH + 1, :].astype(F32)
        for s in range(out_ref.shape[0] // SEG):
            local_ref, map_ref = refs[s * parts * SEG // out_ref.shape[0] * 2 :][:2]
            at = s * SEG % map_ref.shape[1]
            query_map = map_ref[half, at : at + SEG, cols]
            mem = before
            norm = norm_before + norm_ref[h, s : s + 1, :]
            if s > 0:
                mem = mem + inner_ref[s - 1, h]
            norm = jnp.broadcast_to(norm.astype(BF), (DH, DH))
            top = jnp.dot(query_map, mem.astype(BF), preferred_element_type=F32)
            bottom = lax.dot_general(query_map, norm, (((1,), (1,)), ((), ())), preferred_element_type=F32)
            recall = gate_ref[h : h + 1, :] * (top / (bottom + 1.0))
            local = local_ref[half, at : at + SEG, cols].astype(F32)
            out_ref[s * SEG : (s + 1) * SEG, cols] = (recall + local).astype(BF)


def weight_part(w_ref, half, offset, width, cols):
    groups = w_ref.shape[0] // (2 * width)
    group = lax.rem(lax.axis_index("head") + offset, groups)
    core = lax.axis_index("seq_2")
    part = core if half == 0 else 1 - core
    return w_ref[pl.ds(pl.multiple_of((group * 2 + part) * width, width), width), cols]


def most_kernel(half, own_ref, prev_ref, next_ref, w_ref, *refs):
    out_ref = refs[-1]
    _, width = own_ref.shape
    tile = w_ref.shape[1] // 4
    for j in range(4):
        cols = slice(j * tile, (j + 1) * tile)
        acc = jnp.dot(own_ref[...], weight_part(w_ref, half, 0, width, cols), preferred_element_type=F32)
        acc = acc + jnp.dot(prev_ref[...], weight_part(w_ref, half, 3, width, cols), preferred_element_type=F32)
        acc = acc + jnp.dot(next_ref[...], weight_part(w_ref, half, 1, width, cols), preferred_element_type=F32)
        if len(refs) > 1:
            sum_ref, far_a_ref, far_b_ref = refs[:3]
            far = jnp.concatenate([far_a_ref[...], far_b_ref[...]], axis=0)
            acc = acc + jnp.dot(far, weight_part(w_ref, 0, 2, width, cols), preferred_element_type=F32)
            acc = acc + sum_ref[:, cols]
        out_ref[:, cols] = acc


def rest_kernel(most_ref, far_a_ref, far_b_ref, w_ref, out_ref, done_ref, sems):
    _, n = done_ref.shape
    half, width = far_a_ref.shape
    tile = n // 4
    copies = []
    for i, far_ref in enumerate((far_a_ref, far_b_ref)):
        outs = pl.ds(i * half, half)
        for j in range(4):
            cols = pl.ds(j * tile, tile)
            acc = jnp.dot(far_ref[...], weight_part(w_ref, 1, 2, width, cols), preferred_element_type=F32)
            done_ref[outs, cols] = (most_ref[outs, cols] + acc).astype(done_ref.dtype)
            copy = pltpu.make_async_copy(done_ref.at[outs, cols], out_ref.at[outs, cols], sems.at[i * 4 + j])
            copy.start()
            copies.append(copy)
    for copy in copies:
        copy.wait()


VMEM_SPEC = pl.BlockSpec(memory_space=pltpu.VMEM)


def near_core(x):
    return pltpu.with_memory_space_constraint(x, pltpu.VMEM)


def params(mib):
    return pltpu.CompilerParams(vmem_limit_bytes=mib * 2**20)


HBM_SPEC = pl.BlockSpec(memory_space=pltpu.HBM)


def far_core(x):
    return pltpu.with_memory_space_constraint(x, pltpu.HBM)


def state_call(bias, keys, values):
    heads = keys.shape[1] // DH
    segs = keys.shape[0] // SEG
    return pl.pallas_call(
        state_kernel,
        in_specs=[HBM_SPEC] * 3,
        out_specs=(VMEM_SPEC,) * 4,
        out_shape=(
            pltpu.VMEM((heads, ROWS, DH), F32),
            pltpu.VMEM((segs - 1, heads, DH, DH), F32),
            pltpu.VMEM((heads, 8, DH), F32),
            pltpu.VMEM((8, DH), F32),
        ),
        scratch_shapes=[pltpu.VMEM(keys.shape, BF)] * 2
        + [pltpu.SMEM(bias.shape, F32), pltpu.SemaphoreType.DMA((2 * segs + 1,))],
        compiler_params=params(4),
        name="state",
    )(*map(far_core, (bias, keys, values)))


def local_call(gate, q, k, v, start, count):
    width = q.shape[1]
    shape = (2, count, width // 2)
    return pl.pallas_call(
        lambda *refs: local_kernel(start, *refs),
        in_specs=[VMEM_SPEC] + [HBM_SPEC] * 3,
        out_specs=(VMEM_SPEC,) * 2,
        out_shape=(pltpu.VMEM(shape, BF),) * 2,
        scratch_shapes=[pltpu.VMEM((count, width), BF)] * 3 + [pltpu.SemaphoreType.DMA((3 * count // SEG,))],
        compiler_params=params(5),
        cost_estimate=pl.CostEstimate(
            flops=4 * count * SEG * width, transcendentals=count * SEG * 4, bytes_accessed=8 * count * width
        ),
    )(gate, *map(far_core, (q, k, v)))


def context_call(half, gate, before, inner, norm, parts):
    rows = sum(part[0].shape[1] for part in parts)
    width = parts[0][0].shape[2]
    flat = [x for part in parts for x in part]
    return pl.pallas_call(
        lambda *refs: context_kernel(half, *refs),
        in_specs=[VMEM_SPEC] * (4 + len(flat)),
        out_specs=VMEM_SPEC,
        out_shape=pltpu.VMEM((rows, width), BF),
        compiler_params=params(3),
        cost_estimate=pl.CostEstimate(
            flops=4 * rows * width * DH, transcendentals=0, bytes_accessed=6 * rows * width
        ),
    )(gate, near_core(before), inner, norm, *flat)


def most_call(half, own, prev, nxt, weight, *more):
    rows, n = own.shape[0], weight.shape[1]
    operands = [own, near_core(prev), near_core(nxt), weight, *(near_core(x) for x in more)]
    return pl.pallas_call(
        lambda *refs: most_kernel(half, *refs),
        in_specs=[VMEM_SPEC] * len(operands),
        out_specs=VMEM_SPEC,
        out_shape=pltpu.VMEM((rows, n), F32),
        compiler_params=params(4),
        cost_estimate=pl.CostEstimate(
            flops=2 * rows * weight.shape[0] * n // 2, transcendentals=0, bytes_accessed=2 * weight.shape[0] * n
        ),
    )(*operands)


def rest_call(most, far_a, far_b, weight):
    rows, n = most.shape
    return pl.pallas_call(
        rest_kernel,
        in_specs=[VMEM_SPEC] * 4,
        out_specs=pl.BlockSpec(memory_space=pl.ANY),
        out_shape=jax.ShapeDtypeStruct((rows, n), BF),
        scratch_shapes=[pltpu.VMEM((rows, n), BF), pltpu.SemaphoreType.DMA((8,))],
        compiler_params=params(4),
        cost_estimate=pl.CostEstimate(
            flops=2 * rows * far_a.shape[1] * n, transcendentals=0, bytes_accessed=8 * rows * n
        ),
        name="rest",
    )(near_core(most), near_core(far_a), near_core(far_b), weight)


def ring(size, step):
    return [(i, (i + step) % size) for i in range(size)]


def turn(value, axis, step):
    return lax.ppermute(value, axis, ring(lax.axis_size(axis), step))


def plane_kernel(mine_ref, got_ref, *refs):
    *piece_refs, plane_ref, sent_ref, before_ref = refs
    x = lax.axis_index("seq_1")
    plane = mine_ref[...] + got_ref[...].astype(F32)
    before = jnp.zeros_like(plane)
    for k, ref in enumerate(piece_refs):
        piece = ref[...].astype(F32)
        plane = plane + piece
        before = before + jnp.where(x > k, piece, 0.0)
    plane_ref[...] = plane
    sent_ref[...] = plane.astype(BF)
    before_ref[...] = before


def window_kernel(plane_ref, below_ref, above_ref, in_ref, window_ref, distant_ref, before_ref):
    z = lax.axis_index("seq_0")
    last = lax.axis_size("seq_0") - 1
    below = below_ref[...].astype(F32)
    above = above_ref[...].astype(F32)
    window = plane_ref[...] + jnp.where(z > 0, below, 0.0) + jnp.where(z < last, above, 0.0)
    window_ref[...] = window.astype(BF)
    distant_ref[...] = jnp.where(z == last, above, window).astype(BF)
    before_ref[...] = in_ref[...] + jnp.where(z == 1, below, 0.0) + jnp.where(z == last, above, 0.0)


def before_kernel(in_ref, lower_ref, upper_ref, mine_ref, got_ref, own_ref, sent_ref):
    first = lax.axis_index("seq_2") == 0
    z = lax.axis_index("seq_0")
    before = in_ref[...] + jnp.where(z >= 4, lower_ref[...].astype(F32), 0.0)
    before = before + jnp.where(z >= 2, upper_ref[...].astype(F32), 0.0)
    sent_ref[...] = jnp.where(first, before + mine_ref[...], before).astype(BF)
    own_ref[...] = jnp.where(first, before, before + got_ref[...].astype(F32))


def glue_call(kernel, arrays, dtypes):
    return pl.pallas_call(
        kernel,
        in_specs=[VMEM_SPEC] * len(arrays),
        out_specs=(VMEM_SPEC,) * len(dtypes),
        out_shape=tuple(pltpu.VMEM(arrays[0].shape, dtype) for dtype in dtypes),
        compiler_params=params(2),
    )(*map(near_core, arrays))


def states_before(total):
    heads = total.shape[0]
    halves = total.reshape(2, heads // 2 * ROWS, DH)
    mine, theirs = halves[0], halves[1]
    got = lax.ppermute(theirs.astype(BF), "seq_2", ring(2, 1))
    sent = (mine + got.astype(F32)).astype(BF)
    size = lax.axis_size("seq_1")
    pieces = [lax.ppermute(sent, "seq_1", ring(size, k)) for k in range(1, size)]
    plane, sent, before = glue_call(plane_kernel, (mine, got, *pieces), (F32, BF, F32))
    size = lax.axis_size("seq_0")
    below = lax.ppermute(sent, "seq_0", ring(size, 1))
    above = lax.ppermute(sent, "seq_0", ring(size, -1))
    window, distant, before = glue_call(window_kernel, (plane, below, above, before), (BF, BF, F32))
    upper = lax.ppermute(window, "seq_0", [(i, i + 2) for i in range(size - 2)])
    lower = lax.ppermute(distant, "seq_0", [(0, 5), (1, 6), (2, 7), (7, 4)])
    own, sent = glue_call(before_kernel, (before, lower, upper, mine, got), (F32, BF))
    return own, lax.ppermute(sent, "seq_2", ring(2, 1))


def layer(queries, keys, values, gate_bias, out_weight):
    rows = queries.shape[0]
    total, inner, norm, gate = state_call(gate_bias, keys, values)
    befores = states_before(total)
    parts = []
    for i in range(2):
        parts.append(local_call(gate, queries, keys, values, i * rows // 2, rows // 2))
    weight = near_core(out_weight)
    pieces = []
    for c in range(2):
        own = context_call(c, gate, befores[c], inner, norm, parts)
        prev = turn(own, "head", 1)
        nxt = turn(own, "head", -1)
        far_a = turn(prev[: rows // 2], "head", 1)
        far_b = turn(nxt[rows // 2 :], "head", -1)
        pieces.append((own, prev, nxt, far_a, far_b))
    most = most_call(0, *pieces[0][:3], weight)
    most = most_call(1, *pieces[1][:3], weight, most, *pieces[0][3:])
    return rest_call(most, *pieces[1][3:], weight)


def solution(mesh):
    finer = Mesh(
        mesh.devices.reshape(8, 4, 2, mesh.shape["head"]), ("seq_0", "seq_1", "seq_2", "head")
    )
    placed = (P(SEQ, "head"), P(SEQ, "head"), P(SEQ, "head"), P("head"), P(None, "head"))
    return jax.shard_map(layer, mesh=finer, in_specs=placed, out_specs=P(SEQ, "head"), check_vma=False)
```

time: 79.5 us -> 76.9 us (0.967)
  local copies, waits for them, and re-layouts: 2.43 us -> 0.1 us
    unnamed x6 -> x2, local copies, waits for them, and re-layouts: 2.19 us -> 0.01 us
    ppermute x8, waiting for transfers between devices: 19.3 us -> 21.1 us  [turn(): return lax.ppermute(value, axis, ring(lax.axis_size(axis), step))]
    ppermute x1, waiting for transfers between devices: 1.31 us -> 0.01 us  [states_before(): upper = lax.ppermute(window, 'seq_0', [(i, i + 2) for i in range(size - 2)])]
  transfers between devices with their start and end apart: 17 -> 17, of which waited for: 9 -> 9; matrix products, arithmetic and copies ran while one was open for 0% -> 0% of each run, Pallas kernels for 12% -> 13%
where the time goes in v3:
time: 76.9 us; the launch traced here: 76.7 us
  starting transfers between devices  34.9 us (45%)
  waiting for transfers between devices  26.9 us (35%)
  Pallas kernels  14.4 us (19%)
    ppermute x8, waiting for transfers between devices, turn(): return lax.ppermute(value, axis, ring(lax.axis_size(axis), step))  21.1 us
    ppermute x8, starting transfers between devices, turn(): return lax.ppermute(value, axis, ring(lax.axis_size(axis), step))  11.5 us
    ppermute x1, starting transfers between devices, states_before(): lower = lax.ppermute(distant, 'seq_0', [(0, 5), (1, 6), (2, 7), (7, 4)])  4.99 us
    pallas_call x2, Pallas kernels, local_call(): pl.pallas_call(lambda *refs: local_kernel(start, *refs), in_specs=[VMEM_S...  4.9 us
    pallas_call x2, Pallas kernels, most_call(): pl.pallas_call(lambda *refs: most_kernel(half, *refs), in_specs=[VMEM_SPE...  4.14 us
    ppermute x1, starting transfers between devices, states_before(): above = lax.ppermute(sent, 'seq_0', ring(size, -1))  4.03 us
    ppermute x1, starting transfers between devices, states_before(): upper = lax.ppermute(window, 'seq_0', [(i, i + 2) for i in range(size - 2)])  3.66 us
    ppermute x1, starting transfers between devices, states_before(): return (own, lax.ppermute(sent, 'seq_2', ring(2, 1)))  3.57 us
  transfers between devices with their start and end apart: 17, of which 9 were waited for; matrix products, arithmetic and copies ran while one was open for 0% of the time, Pallas kernels for 13%

profile of v3, /device:TPU:1, one launch (start us, length us, event | category | flops | bytes accessed | tf_op | source)
XLA Modules:
  0.0 76.7 jit_solution(17476172419249950812)
XLA Ops:
  0.0 2.4 %state.1 = (f32[4,136,128]{2,1,0:T(8,128)S(1)}, f32[3,4,128,128]{3,2,1,0:T(8,128)S(1)}, f32[4,8,128]{2,1,0:T(8,128)S(1)}, f32[8,128]{1,0:T(8,128)S(1)}) custom-call(f32[4]{0:T(128)} %bias_hbm.1, bf16[1024,512]{1,0:T(8,128)(2,1)} %refs_2_.3, bf16[1024,512]{1,0:T(8,128)(2,1)} %refs_3_.5), custom_call_target="tpu_custom_call" | custom-call | tf_op jit(solution)/shard_map/state/pallas_call | solution.py:191
  2.5 3.3 %collective-permute-start = (bf16[272,128]{1,0:T(8,128)(2,1)S(1)}, bf16[272,128]{1,0:T(8,128)(2,1)S(1)}, u32[]{:S(2)}, u32[]{:S(2)}) collective-permute-start(bf16[272,128]{1,0:T(8,128)(2,1)S(1)} %bitcast.5), channel_id=1, source_target_pairs={{0,4},{4,0},{1,5},{5,1},{2,6},{6,2},{3,7},{7,3},{8,12},{12,8},{9,1... | collective-permute-start | bytes 208904 | tf_op jit(solution)/shard_map/ppermute | solution.py:327
  5.8 0.9 %collective-permute-done.got_ref = bf16[272,128]{1,0:T(8,128)(2,1)S(1)} collective-permute-done((bf16[272,128]{1,0:T(8,128)(2,1)S(1)}, bf16[272,128]{1,0:T(8,128)(2,1)S(1)}, u32[]{:S(2)}, u32[]{:S(2)}) %collective-permute-start) | collective-permute-done | bytes 69664 | tf_op jit(solution)/shard_map/ppermute | solution.py:327
  6.7 0.1 collective-permute-start.1
  6.8 1.9 %collective-permute-start.2 = (bf16[272,128]{1,0:T(8,128)(2,1)S(1)}, bf16[272,128]{1,0:T(8,128)(2,1)S(1)}, u32[]{:S(2)}, u32[]{:S(2)}) collective-permute-start(bf16[272,128]{1,0:T(8,128)(2,1)S(1)} %add_convert_fusion), channel_id=1, source_target_pairs={{0,16},{8,24},{16,0},{24,8},{1,17},{9,25},{17,1},{25,9},{2,18},{10... | collective-permute-start | bytes 208904 | tf_op jit(solution)/shard_map/ppermute | solution.py:330
  8.7 1.2 %collective-permute-start.3 = (bf16[272,128]{1,0:T(8,128)(2,1)S(1)}, bf16[272,128]{1,0:T(8,128)(2,1)S(1)}, u32[]{:S(2)}, u32[]{:S(2)}) collective-permute-start(bf16[272,128]{1,0:T(8,128)(2,1)S(1)} %add_convert_fusion), channel_id=1, source_target_pairs={{0,24},{8,0},{16,8},{24,16},{1,25},{9,1},{17,9},{25,17},{2,26},{10... | collective-permute-start | bytes 208904 | tf_op jit(solution)/shard_map/ppermute | solution.py:330
  9.9 2.1 %collective-permute-done.1.refs_0_ = bf16[272,128]{1,0:T(8,128)(2,1)S(1)} collective-permute-done((bf16[272,128]{1,0:T(8,128)(2,1)S(1)}, bf16[272,128]{1,0:T(8,128)(2,1)S(1)}, u32[]{:S(2)}, u32[]{:S(2)}) %collective-permute-start.1) | collective-permute-done | bytes 69664 | tf_op jit(solution)/shard_map/ppermute | solution.py:330
  12.0 0.6 collective-permute-done.2.refs_1_
  12.6 0.6 collective-permute-done.3.refs_2_
  13.1 0.1 shard_map.55
  13.2 0.7 collective-permute-start.4
  14.0 4.0 %collective-permute-start.5 = (bf16[272,128]{1,0:T(8,128)(2,1)S(1)}, bf16[272,128]{1,0:T(8,128)(2,1)S(1)}, u32[]{:S(2)}, u32[]{:S(2)}) collective-permute-start(bf16[272,128]{1,0:T(8,128)(2,1)S(1)} %get-tuple-element.24), channel_id=1, source_target_pairs={{0,224},{32,0},{64,32},{96,64},{128,96},{160,128},{192,160},{224,1... | collective-permute-start | bytes 208904 | tf_op jit(solution)/shard_map/ppermute | solution.py:334
  18.0 1.6 %collective-permute-done.4.below_ref = bf16[272,128]{1,0:T(8,128)(2,1)S(1)} collective-permute-done((bf16[272,128]{1,0:T(8,128)(2,1)S(1)}, bf16[272,128]{1,0:T(8,128)(2,1)S(1)}, u32[]{:S(2)}, u32[]{:S(2)}) %collective-permute-start.4) | collective-permute-done | bytes 69664 | tf_op jit(solution)/shard_map/ppermute | solution.py:333
  19.6 0.0 collective-permute-done.5.above_ref
  19.6 0.1 shard_map.56
  19.7 5.0 %collective-permute-start.6 = (bf16[272,128]{1,0:T(8,128)(2,1)S(1)}, bf16[272,128]{1,0:T(8,128)(2,1)S(1)}, u32[]{:S(2)}, u32[]{:S(2)}) collective-permute-start(bf16[272,128]{1,0:T(8,128)(2,1)S(1)} %get-tuple-element.27), channel_id=1, source_target_pairs={{0,160},{32,192},{64,224},{224,128},{1,161},{33,193},{65,225},{225... | collective-permute-start | bytes 208904 | tf_op jit(solution)/shard_map/ppermute | solution.py:337
  24.7 3.7 %collective-permute-start.7 = (bf16[272,128]{1,0:T(8,128)(2,1)S(1)}, bf16[272,128]{1,0:T(8,128)(2,1)S(1)}, u32[]{:S(2)}, u32[]{:S(2)}) collective-permute-start(bf16[272,128]{1,0:T(8,128)(2,1)S(1)} %get-tuple-element.28), channel_id=1, source_target_pairs={{0,64},{32,96},{64,128},{96,160},{128,192},{160,224},{1,65},{33,97... | collective-permute-start | bytes 208904 | tf_op jit(solution)/shard_map/ppermute | solution.py:336
  28.4 2.5 %shard_map.58 = (bf16[2,512,256]{2,1,0:T(8,128)(2,1)S(1)}, bf16[2,512,256]{2,1,0:T(8,128)(2,1)S(1)}) custom-call(f32[8,128]{1,0:T(8,128)S(1)} %get-tuple-element.21.refs_0_, bf16[1024,512]{1,0:T(8,128)(2,1)} %refs_1_.3, bf16[1024,512]{1,0:T(8,128)(2,1)} %refs_2_.3, bf16[1024,512]{1,0:T(8,128)(2,1)} %refs_3_.5), custom_call_target="tpu_custom_call" | custom-call | flops 268435456 | bytes 2097152 | tf_op jit(solution)/shard_map/pallas_call | solution.py:211
  30.8 0.0 collective-permute-done.6.lower_ref
  30.8 0.0 collective-permute-done.7.upper_ref
  30.8 0.1 shard_map.57
  30.9 3.6 %collective-permute-start.8 = (bf16[272,128]{1,0:T(8,128)(2,1)S(1)}, bf16[272,128]{1,0:T(8,128)(2,1)S(1)}, u32[]{:S(2)}, u32[]{:S(2)}) collective-permute-start(bf16[272,128]{1,0:T(8,128)(2,1)S(1)} %get-tuple-element.29), channel_id=1, source_target_pairs={{0,4},{4,0},{1,5},{5,1},{2,6},{6,2},{3,7},{7,3},{8,12},{12,8},{9,1... | collective-permute-start | bytes 208904 | tf_op jit(solution)/shard_map/ppermute | solution.py:339
  34.5 2.4 %shard_map.59 = (bf16[2,512,256]{2,1,0:T(8,128)(2,1)S(1)}, bf16[2,512,256]{2,1,0:T(8,128)(2,1)S(1)}) custom-call(f32[8,128]{1,0:T(8,128)S(1)} %get-tuple-element.21.refs_0_, bf16[1024,512]{1,0:T(8,128)(2,1)} %refs_1_.3, bf16[1024,512]{1,0:T(8,128)(2,1)} %refs_2_.3, bf16[1024,512]{1,0:T(8,128)(2,1)} %refs_3_.5), custom_call_target="tpu_custom_call" | custom-call | flops 268435456 | bytes 2097152 | tf_op jit(solution)/shard_map/pallas_call | solution.py:211
  36.9 0.0 copy-start
  37.0 0.4 shard_map.61.refs_0_
  37.4 1.4 %collective-permute-start.11 = (bf16[1024,256]{1,0:T(8,128)(2,1)S(1)}, bf16[1024,256]{1,0:T(8,128)(2,1)S(1)}, u32[]{:S(2)}, u32[]{:S(2)}) collective-permute-start(bf16[1024,256]{1,0:T(8,128)(2,1)S(1)} %shard_map.61.refs_0_), channel_id=1, source_target_pairs={{0,1},{1,2},{2,3},{3,0},{4,5},{5,6},{6,7},{7,4},{8,9},{9,10},{10,1... | collective-permute-start | bytes 1572872 | tf_op jit(solution)/shard_map/ppermute | solution.py:276
  38.8 1.5 %collective-permute-start.12 = (bf16[1024,256]{1,0:T(8,128)(2,1)S(1)}, bf16[1024,256]{1,0:T(8,128)(2,1)S(1)}, u32[]{:S(2)}, u32[]{:S(2)}) collective-permute-start(bf16[1024,256]{1,0:T(8,128)(2,1)S(1)} %shard_map.61.refs_0_), channel_id=1, source_target_pairs={{0,3},{1,0},{2,1},{3,2},{4,7},{5,4},{6,5},{7,6},{8,11},{9,8},{10,9... | collective-permute-start | bytes 1572872 | tf_op jit(solution)/shard_map/ppermute | solution.py:276
  40.3 0.0 collective-permute-done.8.refs_1_
  40.3 0.5 shard_map.60.refs_0_
  40.8 0.3 collective-permute-start.9
  41.0 2.7 %collective-permute-start.10 = (bf16[1024,256]{1,0:T(8,128)(2,1)S(1)}, bf16[1024,256]{1,0:T(8,128)(2,1)S(1)}, u32[]{:S(2)}, u32[]{:S(2)}) collective-permute-start(bf16[1024,256]{1,0:T(8,128)(2,1)S(1)} %shard_map.60.refs_0_), channel_id=1, source_target_pairs={{0,3},{1,0},{2,1},{3,2},{4,7},{5,4},{6,5},{7,6},{8,11},{9,8},{10,9... | collective-permute-start | bytes 1572872 | tf_op jit(solution)/shard_map/ppermute | solution.py:276
  43.7 8.6 %collective-permute-done.11.refs_1_ = bf16[1024,256]{1,0:T(8,128)(2,1)S(1)} collective-permute-done((bf16[1024,256]{1,0:T(8,128)(2,1)S(1)}, bf16[1024,256]{1,0:T(8,128)(2,1)S(1)}, u32[]{:S(2)}, u32[]{:S(2)}) %collective-permute-start.11) | collective-permute-done | bytes 524320 | tf_op jit(solution)/shard_map/ppermute | solution.py:276
  52.3 0.1 collective-permute-start.13
  52.4 0.0 collective-permute-done.12.refs_2_
  52.4 2.7 %collective-permute-start.14 = (bf16[512,256]{1,0:T(8,128)(2,1)S(1)}, bf16[512,256]{1,0:T(8,128)(2,1)S(1)}, u32[]{:S(2)}, u32[]{:S(2)}) collective-permute-start(bf16[512,256]{1,0:T(8,128)(2,1)S(1)} %slice.29), channel_id=1, source_target_pairs={{0,3},{1,0},{2,1},{3,2},{4,7},{5,4},{6,5},{7,6},{8,11},{9,8},{10,9... | collective-permute-start | bytes 786440 | tf_op jit(solution)/shard_map/ppermute | solution.py:276
  55.2 8.4 %collective-permute-done.9.refs_1_ = bf16[1024,256]{1,0:T(8,128)(2,1)S(1)} collective-permute-done((bf16[1024,256]{1,0:T(8,128)(2,1)S(1)}, bf16[1024,256]{1,0:T(8,128)(2,1)S(1)}, u32[]{:S(2)}, u32[]{:S(2)}) %collective-permute-start.9) | collective-permute-done | bytes 524320 | tf_op jit(solution)/shard_map/ppermute | solution.py:276
  63.5 0.1 collective-permute-start.15
  63.6 0.0 collective-permute-done.10.refs_2_
  63.7 2.7 %collective-permute-start.16 = (bf16[512,256]{1,0:T(8,128)(2,1)S(1)}, bf16[512,256]{1,0:T(8,128)(2,1)S(1)}, u32[]{:S(2)}, u32[]{:S(2)}) collective-permute-start(bf16[512,256]{1,0:T(8,128)(2,1)S(1)} %slice.31), channel_id=1, source_target_pairs={{0,3},{1,0},{2,1},{3,2},{4,7},{5,4},{6,5},{7,6},{8,11},{9,8},{10,9... | collective-permute-start | bytes 786440 | tf_op jit(solution)/shard_map/ppermute | solution.py:276
  66.4 0.0 copy-done
  66.4 1.8 %shard_map.62.refs_4_ = f32[1024,1024]{1,0:T(8,128)S(1)} custom-call(bf16[1024,256]{1,0:T(8,128)(2,1)S(1)} %shard_map.61.refs_0_, bf16[1024,256]{1,0:T(8,128)(2,1)S(1)} %collective-permute-done.11.refs_1_, bf16[1024,256]{1,0:T(8,128)(2,1)S(1)} %collective-permute-done.12.refs_2_, bf16[2048,1024]{1,0:T(8,128)(2,1)S(1)} %copy-done), custom_call_target="tpu_custom_call" | custom-call | flops 2147483648 | bytes 4194304 | tf_op jit(solution)/shard_map/pallas_call | solution.py:243
  68.2 0.9 %collective-permute-done.13.refs_5_ = bf16[512,256]{1,0:T(8,128)(2,1)S(1)} collective-permute-done((bf16[512,256]{1,0:T(8,128)(2,1)S(1)}, bf16[512,256]{1,0:T(8,128)(2,1)S(1)}, u32[]{:S(2)}, u32[]{:S(2)}) %collective-permute-start.13) | collective-permute-done | bytes 262176 | tf_op jit(solution)/shard_map/ppermute | solution.py:276
  69.1 0.0 collective-permute-done.14.refs_6_
  69.1 2.3 %shard_map.63.most_ref = f32[1024,1024]{1,0:T(8,128)S(1)} custom-call(bf16[1024,256]{1,0:T(8,128)(2,1)S(1)} %shard_map.60.refs_0_, bf16[1024,256]{1,0:T(8,128)(2,1)S(1)} %collective-permute-done.9.refs_1_, bf16[1024,256]{1,0:T(8,128)(2,1)S(1)} %collective-permute-done.10.refs_2_, bf16[2048,1024]{1,0:T(8,128)(2,1)S(1)} %copy-done, ...), custom_call_target="tpu_custom_call" | custom-call | flops 2147483648 | bytes 4194304 | tf_op jit(solution)/shard_map/pallas_call | solution.py:243
  71.5 3.3 %collective-permute-done.15.far_a_ref = bf16[512,256]{1,0:T(8,128)(2,1)S(1)} collective-permute-done((bf16[512,256]{1,0:T(8,128)(2,1)S(1)}, bf16[512,256]{1,0:T(8,128)(2,1)S(1)}, u32[]{:S(2)}, u32[]{:S(2)}) %collective-permute-start.15) | collective-permute-done | bytes 262176 | tf_op jit(solution)/shard_map/ppermute | solution.py:276
  74.8 0.0 collective-permute-done.16.far_b_ref
  74.8 1.8 %rest.1 = bf16[1024,1024]{1,0:T(8,128)(2,1)} custom-call(f32[1024,1024]{1,0:T(8,128)S(1)} %shard_map.63.most_ref, bf16[512,256]{1,0:T(8,128)(2,1)S(1)} %collective-permute-done.15.far_a_ref, bf16[512,256]{1,0:T(8,128)(2,1)S(1)} %collective-permute-done.16.far_b_ref, bf16[2048,1024]{1,0:T(8,128)(2,1)S(1)} %copy-done), custom_call_target="tpu_custom_call" | custom-call | flops 536870912 | bytes 8388608 | tf_op jit(solution)/shard_map/rest/pallas_call | solution.py:257
  (7 shorter events, 0.1 us)
Async XLA Ops:
  2.5 4.2 %collective-permute-start = (bf16[272,128]{1,0:T(8,128)(2,1)S(1)}, bf16[272,128]{1,0:T(8,128)(2,1)S(1)}, u32[]{:S(2)}, u32[]{:S(2)}) collective-permute-start(bf16[272,128]{1,0:T(8,128)(2,1)S(1)} %bitcast.5), channel_id=1, source_target_pairs={{0,4},{4,0},{1,5},{5,1},{2,6},{6,2},{3,7},{7,3},{8,12},{12,8},{9,1... | collective-permute-start | bytes 208904 | tf_op jit(solution)/shard_map/ppermute | solution.py:327
  6.7 5.3 %collective-permute-start.1 = (bf16[272,128]{1,0:T(8,128)(2,1)S(1)}, bf16[272,128]{1,0:T(8,128)(2,1)S(1)}, u32[]{:S(2)}, u32[]{:S(2)}) collective-permute-start(bf16[272,128]{1,0:T(8,128)(2,1)S(1)} %add_convert_fusion), channel_id=1, source_target_pairs={{0,8},{8,16},{16,24},{24,0},{1,9},{9,17},{17,25},{25,1},{2,10},{10... | collective-permute-start | bytes 208904 | tf_op jit(solution)/shard_map/ppermute | solution.py:330
  6.8 5.8 %collective-permute-start.2 = (bf16[272,128]{1,0:T(8,128)(2,1)S(1)}, bf16[272,128]{1,0:T(8,128)(2,1)S(1)}, u32[]{:S(2)}, u32[]{:S(2)}) collective-permute-start(bf16[272,128]{1,0:T(8,128)(2,1)S(1)} %add_convert_fusion), channel_id=1, source_target_pairs={{0,16},{8,24},{16,0},{24,8},{1,17},{9,25},{17,1},{25,9},{2,18},{10... | collective-permute-start | bytes 208904 | tf_op jit(solution)/shard_map/ppermute | solution.py:330
  8.7 4.4 %collective-permute-start.3 = (bf16[272,128]{1,0:T(8,128)(2,1)S(1)}, bf16[272,128]{1,0:T(8,128)(2,1)S(1)}, u32[]{:S(2)}, u32[]{:S(2)}) collective-permute-start(bf16[272,128]{1,0:T(8,128)(2,1)S(1)} %add_convert_fusion), channel_id=1, source_target_pairs={{0,24},{8,0},{16,8},{24,16},{1,25},{9,1},{17,9},{25,17},{2,26},{10... | collective-permute-start | bytes 208904 | tf_op jit(solution)/shard_map/ppermute | solution.py:330
  13.2 6.4 %collective-permute-start.4 = (bf16[272,128]{1,0:T(8,128)(2,1)S(1)}, bf16[272,128]{1,0:T(8,128)(2,1)S(1)}, u32[]{:S(2)}, u32[]{:S(2)}) collective-permute-start(bf16[272,128]{1,0:T(8,128)(2,1)S(1)} %get-tuple-element.24), channel_id=1, source_target_pairs={{0,32},{32,64},{64,96},{96,128},{128,160},{160,192},{192,224},{224... | collective-permute-start | bytes 208904 | tf_op jit(solution)/shard_map/ppermute | solution.py:333
  14.0 5.6 %collective-permute-start.5 = (bf16[272,128]{1,0:T(8,128)(2,1)S(1)}, bf16[272,128]{1,0:T(8,128)(2,1)S(1)}, u32[]{:S(2)}, u32[]{:S(2)}) collective-permute-start(bf16[272,128]{1,0:T(8,128)(2,1)S(1)} %get-tuple-element.24), channel_id=1, source_target_pairs={{0,224},{32,0},{64,32},{96,64},{128,96},{160,128},{192,160},{224,1... | collective-permute-start | bytes 208904 | tf_op jit(solution)/shard_map/ppermute | solution.py:334
  19.7 11.1 %collective-permute-start.6 = (bf16[272,128]{1,0:T(8,128)(2,1)S(1)}, bf16[272,128]{1,0:T(8,128)(2,1)S(1)}, u32[]{:S(2)}, u32[]{:S(2)}) collective-permute-start(bf16[272,128]{1,0:T(8,128)(2,1)S(1)} %get-tuple-element.27), channel_id=1, source_target_pairs={{0,160},{32,192},{64,224},{224,128},{1,161},{33,193},{65,225},{225... | collective-permute-start | bytes 208904 | tf_op jit(solution)/shard_map/ppermute | solution.py:337
  24.7 6.1 %collective-permute-start.7 = (bf16[272,128]{1,0:T(8,128)(2,1)S(1)}, bf16[272,128]{1,0:T(8,128)(2,1)S(1)}, u32[]{:S(2)}, u32[]{:S(2)}) collective-permute-start(bf16[272,128]{1,0:T(8,128)(2,1)S(1)} %get-tuple-element.28), channel_id=1, source_target_pairs={{0,64},{32,96},{64,128},{96,160},{128,192},{160,224},{1,65},{33,97... | collective-permute-start | bytes 208904 | tf_op jit(solution)/shard_map/ppermute | solution.py:336
  30.9 9.4 %collective-permute-start.8 = (bf16[272,128]{1,0:T(8,128)(2,1)S(1)}, bf16[272,128]{1,0:T(8,128)(2,1)S(1)}, u32[]{:S(2)}, u32[]{:S(2)}) collective-permute-start(bf16[272,128]{1,0:T(8,128)(2,1)S(1)} %get-tuple-element.29), channel_id=1, source_target_pairs={{0,4},{4,0},{1,5},{5,1},{2,6},{6,2},{3,7},{7,3},{8,12},{12,8},{9,1... | collective-permute-start | bytes 208904 | tf_op jit(solution)/shard_map/ppermute | solution.py:339
  36.9 29.5 %copy-start = (bf16[2048,1024]{1,0:T(8,128)(2,1)S(1)}, bf16[2048,1024]{1,0:T(8,128)(2,1)}, u32[]{:S(2)}) copy-start(bf16[2048,1024]{1,0:T(8,128)(2,1)} %w_ref.1) | copy-start | bytes 12582916
  37.4 14.9 %collective-permute-start.11 = (bf16[1024,256]{1,0:T(8,128)(2,1)S(1)}, bf16[1024,256]{1,0:T(8,128)(2,1)S(1)}, u32[]{:S(2)}, u32[]{:S(2)}) collective-permute-start(bf16[1024,256]{1,0:T(8,128)(2,1)S(1)} %shard_map.61.refs_0_), channel_id=1, source_target_pairs={{0,1},{1,2},{2,3},{3,0},{4,5},{5,6},{6,7},{7,4},{8,9},{9,10},{10,1... | collective-permute-start | bytes 1572872 | tf_op jit(solution)/shard_map/ppermute | solution.py:276
  38.8 13.6 %collective-permute-start.12 = (bf16[1024,256]{1,0:T(8,128)(2,1)S(1)}, bf16[1024,256]{1,0:T(8,128)(2,1)S(1)}, u32[]{:S(2)}, u32[]{:S(2)}) collective-permute-start(bf16[1024,256]{1,0:T(8,128)(2,1)S(1)} %shard_map.61.refs_0_), channel_id=1, source_target_pairs={{0,3},{1,0},{2,1},{3,2},{4,7},{5,4},{6,5},{7,6},{8,11},{9,8},{10,9... | collective-permute-start | bytes 1572872 | tf_op jit(solution)/shard_map/ppermute | solution.py:276
  40.8 22.7 %collective-permute-start.9 = (bf16[1024,256]{1,0:T(8,128)(2,1)S(1)}, bf16[1024,256]{1,0:T(8,128)(2,1)S(1)}, u32[]{:S(2)}, u32[]{:S(2)}) collective-permute-start(bf16[1024,256]{1,0:T(8,128)(2,1)S(1)} %shard_map.60.refs_0_), channel_id=1, source_target_pairs={{0,1},{1,2},{2,3},{3,0},{4,5},{5,6},{6,7},{7,4},{8,9},{9,10},{10,1... | collective-permute-start | bytes 1572872 | tf_op jit(solution)/shard_map/ppermute | solution.py:276
  41.0 22.6 %collective-permute-start.10 = (bf16[1024,256]{1,0:T(8,128)(2,1)S(1)}, bf16[1024,256]{1,0:T(8,128)(2,1)S(1)}, u32[]{:S(2)}, u32[]{:S(2)}) collective-permute-start(bf16[1024,256]{1,0:T(8,128)(2,1)S(1)} %shard_map.60.refs_0_), channel_id=1, source_target_pairs={{0,3},{1,0},{2,1},{3,2},{4,7},{5,4},{6,5},{7,6},{8,11},{9,8},{10,9... | collective-permute-start | bytes 1572872 | tf_op jit(solution)/shard_map/ppermute | solution.py:276
  52.3 16.8 %collective-permute-start.13 = (bf16[512,256]{1,0:T(8,128)(2,1)S(1)}, bf16[512,256]{1,0:T(8,128)(2,1)S(1)}, u32[]{:S(2)}, u32[]{:S(2)}) collective-permute-start(bf16[512,256]{1,0:T(8,128)(2,1)S(1)} %slice.28), channel_id=1, source_target_pairs={{0,1},{1,2},{2,3},{3,0},{4,5},{5,6},{6,7},{7,4},{8,9},{9,10},{10,1... | collective-permute-start | bytes 786440 | tf_op jit(solution)/shard_map/ppermute | solution.py:276
  52.4 16.7 %collective-permute-start.14 = (bf16[512,256]{1,0:T(8,128)(2,1)S(1)}, bf16[512,256]{1,0:T(8,128)(2,1)S(1)}, u32[]{:S(2)}, u32[]{:S(2)}) collective-permute-start(bf16[512,256]{1,0:T(8,128)(2,1)S(1)} %slice.29), channel_id=1, source_target_pairs={{0,3},{1,0},{2,1},{3,2},{4,7},{5,4},{6,5},{7,6},{8,11},{9,8},{10,9... | collective-permute-start | bytes 786440 | tf_op jit(solution)/shard_map/ppermute | solution.py:276
  63.5 11.2 %collective-permute-start.15 = (bf16[512,256]{1,0:T(8,128)(2,1)S(1)}, bf16[512,256]{1,0:T(8,128)(2,1)S(1)}, u32[]{:S(2)}, u32[]{:S(2)}) collective-permute-start(bf16[512,256]{1,0:T(8,128)(2,1)S(1)} %slice.30), channel_id=1, source_target_pairs={{0,1},{1,2},{2,3},{3,0},{4,5},{5,6},{6,7},{7,4},{8,9},{9,10},{10,1... | collective-permute-start | bytes 786440 | tf_op jit(solution)/shard_map/ppermute | solution.py:276
  63.7 11.1 %collective-permute-start.16 = (bf16[512,256]{1,0:T(8,128)(2,1)S(1)}, bf16[512,256]{1,0:T(8,128)(2,1)S(1)}, u32[]{:S(2)}, u32[]{:S(2)}) collective-permute-start(bf16[512,256]{1,0:T(8,128)(2,1)S(1)} %slice.31), channel_id=1, source_target_pairs={{0,3},{1,0},{2,1},{3,2},{4,7},{5,4},{6,5},{7,6},{8,11},{9,8},{10,9... | collective-permute-start | bytes 786440 | tf_op jit(solution)/shard_map/ppermute | solution.py:276

commit v4 on v3

--- a/solution.py
+++ b/solution.py
@@ -38,48 +38,85 @@
     return lax.axis_index("seq_2") * (heads // 2)
 
 
-def state_kernel(bias_hbm, k_hbm, v_hbm, total_ref, inner_ref, norm_ref, gate_ref, k_ref, v_ref, bias_ref, sems):
+def add_states(first, count, k_ref, v_ref, s, last, norms, refs):
+    total_ref, inner_ref, norm_ref = refs
+    rows = slice(s * SEG, (s + 1) * SEG)
+    for h in range(count):
+        cols = pl.ds(first(h), DH)
+        norm_ref[h, s : s + 1, :] = norms[h][:1]
+        key_map = feature(k_ref[rows, cols]).astype(BF)
+        mem = lax.dot_general(
+            key_map, v_ref[rows, cols], (((0,), (0,)), ((), ())), preferred_element_type=F32
+        )
+        if s > 0:
+            mem = mem + inner_ref[s - 1, h]
+        norms[h] = norms[h] + jnp.dot(jnp.ones((ROWS - DH, SEG), BF), key_map, preferred_element_type=F32)
+        if not last:
+            inner_ref[s, h] = mem
+        else:
+            total_ref[h * ROWS : h * ROWS + DH, :] = mem.astype(total_ref.dtype)
+            total_ref[h * ROWS + DH : (h + 1) * ROWS, :] = norms[h].astype(total_ref.dtype)
+
+
+def other_state_kernel(bias_hbm, k_hbm, v_hbm, total_ref, inner_ref, norm_ref, gate_ref, kv_ref, k_ref, v_ref, bias_ref, sems):
     segs = k_ref.shape[0] // SEG
-    heads = k_ref.shape[1] // DH
-    first = own_half(heads)
-    copies = fetch(0, (k_hbm, v_hbm), (k_ref, v_ref), sems)
-    bias_copy = pltpu.make_async_copy(bias_hbm, bias_ref, sems.at[2 * segs])
-    bias_copy.start()
-    norms = [jnp.zeros((ROWS - DH, DH), F32)] * heads
+    heads = 2 * k_ref.shape[1] // DH
+    width = k_ref.shape[1]
+    mine = pl.multiple_of(lax.axis_index("seq_2") * width, width)
+    theirs = pl.multiple_of((1 - lax.axis_index("seq_2")) * width, width)
+    copies = fetch(0, (k_hbm.at[:, pl.ds(theirs, width)], v_hbm.at[:, pl.ds(theirs, width)]), (k_ref, v_ref), sems)
+    extra = [
+        pltpu.make_async_copy(bias_hbm, bias_ref, sems.at[2 * segs]),
+        pltpu.make_async_copy(k_hbm.at[:, pl.ds(mine, width)], kv_ref.at[0], sems.at[2 * segs + 1]),
+        pltpu.make_async_copy(v_hbm.at[:, pl.ds(mine, width)], kv_ref.at[1], sems.at[2 * segs + 2]),
+    ]
+    for copy in extra:
+        copy.start()
+    norms = [jnp.zeros((ROWS - DH, DH), F32)] * (heads // 2)
     for s in range(segs):
-        rows = slice(s * SEG, (s + 1) * SEG)
         for copy in copies[s]:
             copy.wait()
-        for h in range(heads):
-            cols = pl.ds(pl.multiple_of(lax.rem(first + h, heads) * DH, DH), DH)
-            norm_ref[h, s : s + 1, :] = norms[h][:1]
-            key_map = feature(k_ref[rows, cols]).astype(BF)
-            mem = lax.dot_general(
-                key_map, v_ref[rows, cols], (((0,), (0,)), ((), ())), preferred_element_type=F32
-            )
-            if s > 0:
-                mem = mem + inner_ref[s - 1, h]
-            norms[h] = norms[h] + jnp.dot(jnp.ones((ROWS - DH, SEG), BF), key_map, preferred_element_type=F32)
-            if s < segs - 1:
-                inner_ref[s, h] = mem
-            else:
-                total_ref[h, :DH, :] = mem
-                total_ref[h, DH:, :] = norms[h]
-    bias_copy.wait()
+        add_states(lambda h: h * DH, heads // 2, k_ref, v_ref, s, s == segs - 1, norms, (total_ref, inner_ref, norm_ref))
+    for copy in extra:
+        copy.wait()
     for h in range(heads):
-        bias = jnp.full((1, DH), bias_ref[lax.rem(first + h, heads)], F32)
+        bias = jnp.full((1, DH), bias_ref[lax.rem(own_half(heads) + h, heads)], F32)
         gate_ref[h : h + 1, :] = 1.0 / (1.0 + jnp.exp(-bias))
 
 
-def local_kernel(start, gate_ref, q_hbm, k_hbm, v_hbm, out_ref, map_ref, q_ref, k_ref, v_ref, sems):
+def own_state_kernel(kv_ref, total_ref, inner_ref, norm_ref):
+    segs = kv_ref.shape[1] // SEG
+    count = kv_ref.shape[2] // DH
+    norms = [jnp.zeros((ROWS - DH, DH), F32)] * count
+    for s in range(segs):
+        add_states(
+            lambda h: h * DH, count, kv_ref.at[0], kv_ref.at[1], s, s == segs - 1, norms, (total_ref, inner_ref, norm_ref)
+        )
+
+
+def local_kernel(gate_ref, *refs):
+    ahead = len(refs) > 4
+    if ahead:
+        q_hbm, k_hbm, v_hbm, out_ref, map_ref, next_ref, q_ref, k_ref, v_ref, sems = refs
+        count = q_ref.shape[0]
+        copies = fetch(0, (q_hbm, k_hbm, v_hbm), (q_ref, k_ref, v_ref), sems)
+        more = [
+            pltpu.make_async_copy(ref.at[pl.ds(count, count)], next_ref.at[i], sems.at[3 * count // SEG + i])
+            for i, ref in enumerate((q_hbm, k_hbm, v_hbm))
+        ]
+        for copy in more:
+            copy.start()
+    else:
+        next_ref, out_ref, map_ref = refs
+        q_ref, k_ref, v_ref = (next_ref.at[i] for i in range(3))
     heads = q_ref.shape[1] // DH
     first = own_half(heads)
     scale = 1.0 / DH**0.5 * 1.4426950408889634
-    copies = fetch(start, (q_hbm, k_hbm, v_hbm), (q_ref, k_ref, v_ref), sems)
     for s in range(q_ref.shape[0] // SEG):
         rows = slice(s * SEG, (s + 1) * SEG)
-        for copy in copies[s]:
-            copy.wait()
+        if ahead:
+            for copy in copies[s]:
+                copy.wait()
         for h in range(heads):
             half, at = divmod(h, heads // 2)
             outs = slice(at * DH, (at + 1) * DH)
@@ -97,6 +134,9 @@
             wide = jnp.concatenate([v_ref[rows, cols], jnp.ones((SEG, DH), BF)], axis=1)
             out = jnp.dot(weights, wide, preferred_element_type=F32)
             out_ref[half, rows, outs] = (out[:, :DH] * (rest / out[:, DH:])).astype(out_ref.dtype)
+    if ahead:
+        for copy in more:
+            copy.wait()
 
 
 def context_kernel(half, gate_ref, before_ref, inner_ref, norm_ref, *refs):
@@ -113,9 +153,9 @@
             at = s * SEG % map_ref.shape[1]
             query_map = map_ref[half, at : at + SEG, cols]
             mem = before
-            norm = norm_before + norm_ref[h, s : s + 1, :]
+            norm = norm_before + norm_ref[i, s : s + 1, :]
             if s > 0:
-                mem = mem + inner_ref[s - 1, h]
+                mem = mem + inner_ref[s - 1, i]
             norm = jnp.broadcast_to(norm.astype(BF), (DH, DH))
             top = jnp.dot(query_map, mem.astype(BF), preferred_element_type=F32)
             bottom = lax.dot_general(query_map, norm, (((1,), (1,)), ((), ())), preferred_element_type=F32)
@@ -185,40 +225,58 @@
     return pltpu.with_memory_space_constraint(x, pltpu.HBM)
 
 
-def state_call(bias, keys, values):
-    heads = keys.shape[1] // DH
-    segs = keys.shape[0] // SEG
+def state_calls(bias, keys, values):
+    rows, width = keys.shape
+    half = width // 2
+    count = half // DH
+    segs = rows // SEG
+    shapes = (pltpu.VMEM((segs - 1, count, DH, DH), F32), pltpu.VMEM((count, 8, DH), F32))
+    theirs, *other, gate, kv = pl.pallas_call(
+        other_state_kernel,
+        in_specs=[HBM_SPEC] * 3,
+        out_specs=(VMEM_SPEC,) * 5,
+        out_shape=(
+            pltpu.VMEM((count * ROWS, DH), BF),
+            *shapes,
+            pltpu.VMEM((8, DH), F32),
+            pltpu.VMEM((2, rows, half), BF),
+        ),
+        scratch_shapes=[pltpu.VMEM((rows, half), BF)] * 2
+        + [pltpu.SMEM(bias.shape, F32), pltpu.SemaphoreType.DMA((2 * segs + 3,))],
+        compiler_params=params(4),
+        name="other_state",
+    )(*map(far_core, (bias, keys, values)))
+    mine, *own = pl.pallas_call(
+        own_state_kernel,
+        in_specs=[VMEM_SPEC],
+        out_specs=(VMEM_SPEC,) * 3,
+        out_shape=(pltpu.VMEM((count * ROWS, DH), F32), *shapes),
+        compiler_params=params(4),
+        name="own_state",
+    )(kv)
+    return mine, theirs, (own, other), gate
+
+
+def local_call(gate, operands, count, ahead):
+    width = operands[0].shape[-1]
+    shape = (2, count, width // 2)
+    out_shape = (pltpu.VMEM(shape, BF),) * 2
+    scratch = []
+    if ahead:
+        out_shape += (pltpu.VMEM((3, count, width), BF),)
+        scratch = [pltpu.VMEM((count, width), BF)] * 3 + [pltpu.SemaphoreType.DMA((3 * count // SEG + 3,))]
+        operands = tuple(map(far_core, operands))
     return pl.pallas_call(
-        state_kernel,
-        in_specs=[HBM_SPEC] * 3,
-        out_specs=(VMEM_SPEC,) * 4,
-        out_shape=(
-            pltpu.VMEM((heads, ROWS, DH), F32),
-            pltpu.VMEM((segs - 1, heads, DH, DH), F32),
-            pltpu.VMEM((heads, 8, DH), F32),
-            pltpu.VMEM((8, DH), F32),
-        ),
-        scratch_shapes=[pltpu.VMEM(keys.shape, BF)] * 2
-        + [pltpu.SMEM(bias.shape, F32), pltpu.SemaphoreType.DMA((2 * segs + 1,))],
-        compiler_params=params(4),
-        name="state",
-    )(*map(far_core, (bias, keys, values)))
-
-
-def local_call(gate, q, k, v, start, count):
-    width = q.shape[1]
-    shape = (2, count, width // 2)
-    return pl.pallas_call(
-        lambda *refs: local_kernel(start, *refs),
-        in_specs=[VMEM_SPEC] + [HBM_SPEC] * 3,
-        out_specs=(VMEM_SPEC,) * 2,
-        out_shape=(pltpu.VMEM(shape, BF),) * 2,
-        scratch_shapes=[pltpu.VMEM((count, width), BF)] * 3 + [pltpu.SemaphoreType.DMA((3 * count // SEG,))],
+        local_kernel,
+        in_specs=[VMEM_SPEC] + [HBM_SPEC if ahead else VMEM_SPEC] * len(operands),
+        out_specs=(VMEM_SPEC,) * len(out_shape),
+        out_shape=out_shape,
+        scratch_shapes=scratch,
         compiler_params=params(5),
         cost_estimate=pl.CostEstimate(
             flops=4 * count * SEG * width, transcendentals=count * SEG * 4, bytes_accessed=8 * count * width
         ),
-    )(gate, *map(far_core, (q, k, v)))
+    )(gate, *operands)
 
 
 def context_call(half, gate, before, inner, norm, parts):
@@ -320,11 +378,8 @@
     )(*map(near_core, arrays))
 
 
-def states_before(total):
-    heads = total.shape[0]
-    halves = total.reshape(2, heads // 2 * ROWS, DH)
-    mine, theirs = halves[0], halves[1]
-    got = lax.ppermute(theirs.astype(BF), "seq_2", ring(2, 1))
+def states_before(mine, theirs):
+    got = lax.ppermute(theirs, "seq_2", ring(2, 1))
     sent = (mine + got.astype(F32)).astype(BF)
     size = lax.axis_size("seq_1")
     pieces = [lax.ppermute(sent, "seq_1", ring(size, k)) for k in range(1, size)]
@@ -341,15 +396,14 @@
 
 def layer(queries, keys, values, gate_bias, out_weight):
     rows = queries.shape[0]
-    total, inner, norm, gate = state_call(gate_bias, keys, values)
-    befores = states_before(total)
-    parts = []
-    for i in range(2):
-        parts.append(local_call(gate, queries, keys, values, i * rows // 2, rows // 2))
+    mine, theirs, inners, gate = state_calls(gate_bias, keys, values)
+    befores = states_before(mine, theirs)
+    *part, ahead = local_call(gate, (queries, keys, values), rows // 2, True)
+    parts = [part, local_call(gate, (ahead,), rows // 2, False)]
     weight = near_core(out_weight)
     pieces = []
     for c in range(2):
-        own = context_call(c, gate, befores[c], inner, norm, parts)
+        own = context_call(c, gate, befores[c], *inners[c], parts)
         prev = turn(own, "head", 1)
         nxt = turn(own, "head", -1)
         far_a = turn(prev[: rows // 2], "head", 1)

time: 76.9 us -> 75.1 us (0.977)
  Pallas kernels: 14.4 us -> 13.1 us
    pallas_call x3 -> x4, Pallas kernels: 7.33 us -> 6.08 us  [the longest x2 3.5 us: local_call(): pl.pallas_call(local_kernel, in_specs=[VMEM_SPEC] + [HBM_SPEC if ahead el...]
  transfers between devices with their start and end apart: 17 -> 17, of which waited for: 9 -> 9; matrix products, arithmetic and copies ran while one was open for 0% -> 0% of each run, Pallas kernels for 13% -> 12%
where the time goes in v4:
time: 75.1 us; the launch traced here: 75 us
  starting transfers between devices  34.7 us (46%)
  waiting for transfers between devices  26.7 us (36%)
  Pallas kernels  13.1 us (17%)
    ppermute x8, waiting for transfers between devices, turn(): return lax.ppermute(value, axis, ring(lax.axis_size(axis), step))  21.3 us
    ppermute x8, starting transfers between devices, turn(): return lax.ppermute(value, axis, ring(lax.axis_size(axis), step))  11.3 us
    ppermute x1, starting transfers between devices, states_before(): lower = lax.ppermute(distant, 'seq_0', [(0, 5), (1, 6), (2, 7), (7, 4)])  5 us
    pallas_call x2, Pallas kernels, most_call(): pl.pallas_call(lambda *refs: most_kernel(half, *refs), in_specs=[VMEM_SPE...  4.14 us
    ppermute x1, starting transfers between devices, states_before(): above = lax.ppermute(sent, 'seq_0', ring(size, -1))  4.03 us
    ppermute x1, starting transfers between devices, states_before(): upper = lax.ppermute(window, 'seq_0', [(i, i + 2) for i in range(size - 2)])  3.66 us
    ppermute x1, starting transfers between devices, states_before(): return (own, lax.ppermute(sent, 'seq_2', ring(2, 1)))  3.57 us
    pallas_call x2, Pallas kernels, local_call(): pl.pallas_call(local_kernel, in_specs=[VMEM_SPEC] + [HBM_SPEC if ahead el...  3.5 us
  transfers between devices with their start and end apart: 17, of which 9 were waited for; matrix products, arithmetic and copies ran while one was open for 0% of the time, Pallas kernels for 12%

profile of v4, /device:TPU:1, one launch (start us, length us, event | category | flops | bytes accessed | tf_op | source)
XLA Modules:
  0.0 75.0 jit_solution(17693034073831733035)
XLA Ops:
  0.0 2.1 %other_state.1 = (bf16[272,128]{1,0:T(8,128)(2,1)S(1)}, f32[3,2,128,128]{3,2,1,0:T(8,128)S(1)}, f32[2,8,128]{2,1,0:T(8,128)S(1)}, f32[8,128]{1,0:T(8,128)S(1)}, bf16[2,1024,256]{2,1,0:T(8,128)(2,1)S(1)}) custom-call(f32[4]{0:T(128)} %bias_hbm.1, bf16[1024,512]{1,0:T(8,128)(2,1)} %refs_1_.1, bf16[1024,512]{1,0:T(8,128)(2,1)} %refs_2_.1), custom_call_target="tpu_custom_call" | custom-call | tf_op jit(solution)/shard_map/other_state/pallas_call | solution.py:234
  2.1 3.3 %collective-permute-start = (bf16[272,128]{1,0:T(8,128)(2,1)S(1)}, bf16[272,128]{1,0:T(8,128)(2,1)S(1)}, u32[]{:S(2)}, u32[]{:S(2)}) collective-permute-start(bf16[272,128]{1,0:T(8,128)(2,1)S(1)} %get-tuple-element.29), channel_id=1, source_target_pairs={{0,4},{4,0},{1,5},{5,1},{2,6},{6,2},{3,7},{7,3},{8,12},{12,8},{9,1... | collective-permute-start | bytes 208904 | tf_op jit(solution)/shard_map/ppermute | solution.py:382
  5.4 0.5 own_state.1
  5.9 0.5 collective-permute-done.got_ref
  6.4 0.1 collective-permute-start.1
  6.5 1.9 %collective-permute-start.2 = (bf16[272,128]{1,0:T(8,128)(2,1)S(1)}, bf16[272,128]{1,0:T(8,128)(2,1)S(1)}, u32[]{:S(2)}, u32[]{:S(2)}) collective-permute-start(bf16[272,128]{1,0:T(8,128)(2,1)S(1)} %add_convert_fusion), channel_id=1, source_target_pairs={{0,16},{8,24},{16,0},{24,8},{1,17},{9,25},{17,1},{25,9},{2,18},{10... | collective-permute-start | bytes 208904 | tf_op jit(solution)/shard_map/ppermute | solution.py:385
  8.4 1.2 %collective-permute-start.3 = (bf16[272,128]{1,0:T(8,128)(2,1)S(1)}, bf16[272,128]{1,0:T(8,128)(2,1)S(1)}, u32[]{:S(2)}, u32[]{:S(2)}) collective-permute-start(bf16[272,128]{1,0:T(8,128)(2,1)S(1)} %add_convert_fusion), channel_id=1, source_target_pairs={{0,24},{8,0},{16,8},{24,16},{1,25},{9,1},{17,9},{25,17},{2,26},{10... | collective-permute-start | bytes 208904 | tf_op jit(solution)/shard_map/ppermute | solution.py:385
  9.6 2.1 %collective-permute-done.1.refs_0_ = bf16[272,128]{1,0:T(8,128)(2,1)S(1)} collective-permute-done((bf16[272,128]{1,0:T(8,128)(2,1)S(1)}, bf16[272,128]{1,0:T(8,128)(2,1)S(1)}, u32[]{:S(2)}, u32[]{:S(2)}) %collective-permute-start.1) | collective-permute-done | bytes 69664 | tf_op jit(solution)/shard_map/ppermute | solution.py:385
  11.7 0.6 collective-permute-done.2.refs_1_
  12.2 0.6 collective-permute-done.3.refs_2_
  12.8 0.1 shard_map.55
  12.9 0.7 collective-permute-start.4
  13.7 4.0 %collective-permute-start.5 = (bf16[272,128]{1,0:T(8,128)(2,1)S(1)}, bf16[272,128]{1,0:T(8,128)(2,1)S(1)}, u32[]{:S(2)}, u32[]{:S(2)}) collective-permute-start(bf16[272,128]{1,0:T(8,128)(2,1)S(1)} %get-tuple-element.31), channel_id=1, source_target_pairs={{0,224},{32,0},{64,32},{96,64},{128,96},{160,128},{192,160},{224,1... | collective-permute-start | bytes 208904 | tf_op jit(solution)/shard_map/ppermute | solution.py:389
  17.7 1.6 %collective-permute-done.4.below_ref = bf16[272,128]{1,0:T(8,128)(2,1)S(1)} collective-permute-done((bf16[272,128]{1,0:T(8,128)(2,1)S(1)}, bf16[272,128]{1,0:T(8,128)(2,1)S(1)}, u32[]{:S(2)}, u32[]{:S(2)}) %collective-permute-start.4) | collective-permute-done | bytes 69664 | tf_op jit(solution)/shard_map/ppermute | solution.py:388
  19.3 0.0 collective-permute-done.5.above_ref
  19.3 0.1 shard_map.56
  19.4 5.0 %collective-permute-start.6 = (bf16[272,128]{1,0:T(8,128)(2,1)S(1)}, bf16[272,128]{1,0:T(8,128)(2,1)S(1)}, u32[]{:S(2)}, u32[]{:S(2)}) collective-permute-start(bf16[272,128]{1,0:T(8,128)(2,1)S(1)} %get-tuple-element.34), channel_id=1, source_target_pairs={{0,160},{32,192},{64,224},{224,128},{1,161},{33,193},{65,225},{225... | collective-permute-start | bytes 208904 | tf_op jit(solution)/shard_map/ppermute | solution.py:392
  24.4 3.7 %collective-permute-start.7 = (bf16[272,128]{1,0:T(8,128)(2,1)S(1)}, bf16[272,128]{1,0:T(8,128)(2,1)S(1)}, u32[]{:S(2)}, u32[]{:S(2)}) collective-permute-start(bf16[272,128]{1,0:T(8,128)(2,1)S(1)} %get-tuple-element.35), channel_id=1, source_target_pairs={{0,64},{32,96},{64,128},{96,160},{128,192},{160,224},{1,65},{33,97... | collective-permute-start | bytes 208904 | tf_op jit(solution)/shard_map/ppermute | solution.py:391
  28.0 2.5 %shard_map.58 = (bf16[2,512,256]{2,1,0:T(8,128)(2,1)S(1)}, bf16[2,512,256]{2,1,0:T(8,128)(2,1)S(1)}, bf16[3,512,512]{2,1,0:T(8,128)(2,1)S(1)}) custom-call(f32[8,128]{1,0:T(8,128)S(1)} %get-tuple-element.26.gate_ref.refs_0_, bf16[1024,512]{1,0:T(8,128)(2,1)} %refs_0_.1, bf16[1024,512]{1,0:T(8,128)(2,1)} %refs_1_.1, bf16[1024,512]{1,0:T(8,128)(2,1)} %refs_2_.1), custom_call_target="tpu_custom_call" | custom-call | flops 268435456 | bytes 2097152 | tf_op jit(solution)/shard_map/pallas_call | solution.py:269
  30.5 0.0 collective-permute-done.6.lower_ref
  30.5 0.0 collective-permute-done.7.upper_ref
  30.6 0.1 shard_map.57
  30.6 3.6 %collective-permute-start.8 = (bf16[272,128]{1,0:T(8,128)(2,1)S(1)}, bf16[272,128]{1,0:T(8,128)(2,1)S(1)}, u32[]{:S(2)}, u32[]{:S(2)}) collective-permute-start(bf16[272,128]{1,0:T(8,128)(2,1)S(1)} %get-tuple-element.36), channel_id=1, source_target_pairs={{0,4},{4,0},{1,5},{5,1},{2,6},{6,2},{3,7},{7,3},{8,12},{12,8},{9,1... | collective-permute-start | bytes 208904 | tf_op jit(solution)/shard_map/ppermute | solution.py:394
  34.2 1.0 %shard_map.59 = (bf16[2,512,256]{2,1,0:T(8,128)(2,1)S(1)}, bf16[2,512,256]{2,1,0:T(8,128)(2,1)S(1)}) custom-call(f32[8,128]{1,0:T(8,128)S(1)} %get-tuple-element.26.gate_ref.refs_0_, bf16[3,512,512]{2,1,0:T(8,128)(2,1)S(1)} %get-tuple-element.41.refs_0_), custom_call_target="tpu_custom_call" | custom-call | flops 268435456 | bytes 2097152 | tf_op jit(solution)/shard_map/pallas_call | solution.py:269
  35.2 0.0 copy-start
  35.2 0.4 shard_map.61.refs_0_
  35.7 1.4 %collective-permute-start.11 = (bf16[1024,256]{1,0:T(8,128)(2,1)S(1)}, bf16[1024,256]{1,0:T(8,128)(2,1)S(1)}, u32[]{:S(2)}, u32[]{:S(2)}) collective-permute-start(bf16[1024,256]{1,0:T(8,128)(2,1)S(1)} %shard_map.61.refs_0_), channel_id=1, source_target_pairs={{0,1},{1,2},{2,3},{3,0},{4,5},{5,6},{6,7},{7,4},{8,9},{9,10},{10,1... | collective-permute-start | bytes 1572872 | tf_op jit(solution)/shard_map/ppermute | solution.py:334
  37.1 1.5 %collective-permute-start.12 = (bf16[1024,256]{1,0:T(8,128)(2,1)S(1)}, bf16[1024,256]{1,0:T(8,128)(2,1)S(1)}, u32[]{:S(2)}, u32[]{:S(2)}) collective-permute-start(bf16[1024,256]{1,0:T(8,128)(2,1)S(1)} %shard_map.61.refs_0_), channel_id=1, source_target_pairs={{0,3},{1,0},{2,1},{3,2},{4,7},{5,4},{6,5},{7,6},{8,11},{9,8},{10,9... | collective-permute-start | bytes 1572872 | tf_op jit(solution)/shard_map/ppermute | solution.py:334
  38.6 0.0 collective-permute-done.8.refs_1_
  38.6 0.5 shard_map.60.refs_0_
  39.0 0.1 collective-permute-start.9
  39.1 2.7 %collective-permute-start.10 = (bf16[1024,256]{1,0:T(8,128)(2,1)S(1)}, bf16[1024,256]{1,0:T(8,128)(2,1)S(1)}, u32[]{:S(2)}, u32[]{:S(2)}) collective-permute-start(bf16[1024,256]{1,0:T(8,128)(2,1)S(1)} %shard_map.60.refs_0_), channel_id=1, source_target_pairs={{0,3},{1,0},{2,1},{3,2},{4,7},{5,4},{6,5},{7,6},{8,11},{9,8},{10,9... | collective-permute-start | bytes 1572872 | tf_op jit(solution)/shard_map/ppermute | solution.py:334
  41.8 8.8 %collective-permute-done.11.refs_1_ = bf16[1024,256]{1,0:T(8,128)(2,1)S(1)} collective-permute-done((bf16[1024,256]{1,0:T(8,128)(2,1)S(1)}, bf16[1024,256]{1,0:T(8,128)(2,1)S(1)}, u32[]{:S(2)}, u32[]{:S(2)}) %collective-permute-start.11) | collective-permute-done | bytes 524320 | tf_op jit(solution)/shard_map/ppermute | solution.py:334
  50.6 0.1 collective-permute-start.13
  50.7 0.0 collective-permute-done.12.refs_2_
  50.7 2.7 %collective-permute-start.14 = (bf16[512,256]{1,0:T(8,128)(2,1)S(1)}, bf16[512,256]{1,0:T(8,128)(2,1)S(1)}, u32[]{:S(2)}, u32[]{:S(2)}) collective-permute-start(bf16[512,256]{1,0:T(8,128)(2,1)S(1)} %slice.17), channel_id=1, source_target_pairs={{0,3},{1,0},{2,1},{3,2},{4,7},{5,4},{6,5},{7,6},{8,11},{9,8},{10,9... | collective-permute-start | bytes 786440 | tf_op jit(solution)/shard_map/ppermute | solution.py:334
  53.4 8.4 %collective-permute-done.9.refs_1_ = bf16[1024,256]{1,0:T(8,128)(2,1)S(1)} collective-permute-done((bf16[1024,256]{1,0:T(8,128)(2,1)S(1)}, bf16[1024,256]{1,0:T(8,128)(2,1)S(1)}, u32[]{:S(2)}, u32[]{:S(2)}) %collective-permute-start.9) | collective-permute-done | bytes 524320 | tf_op jit(solution)/shard_map/ppermute | solution.py:334
  61.8 0.1 collective-permute-start.15
  61.9 0.0 collective-permute-done.10.refs_2_
  61.9 2.7 %collective-permute-start.16 = (bf16[512,256]{1,0:T(8,128)(2,1)S(1)}, bf16[512,256]{1,0:T(8,128)(2,1)S(1)}, u32[]{:S(2)}, u32[]{:S(2)}) collective-permute-start(bf16[512,256]{1,0:T(8,128)(2,1)S(1)} %slice.19), channel_id=1, source_target_pairs={{0,3},{1,0},{2,1},{3,2},{4,7},{5,4},{6,5},{7,6},{8,11},{9,8},{10,9... | collective-permute-start | bytes 786440 | tf_op jit(solution)/shard_map/ppermute | solution.py:334
  64.7 0.0 copy-done
  64.7 1.8 %shard_map.62.refs_4_ = f32[1024,1024]{1,0:T(8,128)S(1)} custom-call(bf16[1024,256]{1,0:T(8,128)(2,1)S(1)} %shard_map.61.refs_0_, bf16[1024,256]{1,0:T(8,128)(2,1)S(1)} %collective-permute-done.11.refs_1_, bf16[1024,256]{1,0:T(8,128)(2,1)S(1)} %collective-permute-done.12.refs_2_, bf16[2048,1024]{1,0:T(8,128)(2,1)S(1)} %copy-done), custom_call_target="tpu_custom_call" | custom-call | flops 2147483648 | bytes 4194304 | tf_op jit(solution)/shard_map/pallas_call | solution.py:301
  66.5 0.9 %collective-permute-done.13.refs_5_ = bf16[512,256]{1,0:T(8,128)(2,1)S(1)} collective-permute-done((bf16[512,256]{1,0:T(8,128)(2,1)S(1)}, bf16[512,256]{1,0:T(8,128)(2,1)S(1)}, u32[]{:S(2)}, u32[]{:S(2)}) %collective-permute-start.13) | collective-permute-done | bytes 262176 | tf_op jit(solution)/shard_map/ppermute | solution.py:334
  67.4 0.0 collective-permute-done.14.refs_6_
  67.4 2.3 %shard_map.63.most_ref = f32[1024,1024]{1,0:T(8,128)S(1)} custom-call(bf16[1024,256]{1,0:T(8,128)(2,1)S(1)} %shard_map.60.refs_0_, bf16[1024,256]{1,0:T(8,128)(2,1)S(1)} %collective-permute-done.9.refs_1_, bf16[1024,256]{1,0:T(8,128)(2,1)S(1)} %collective-permute-done.10.refs_2_, bf16[2048,1024]{1,0:T(8,128)(2,1)S(1)} %copy-done, ...), custom_call_target="tpu_custom_call" | custom-call | flops 2147483648 | bytes 4194304 | tf_op jit(solution)/shard_map/pallas_call | solution.py:301
  69.8 3.3 %collective-permute-done.15.far_a_ref = bf16[512,256]{1,0:T(8,128)(2,1)S(1)} collective-permute-done((bf16[512,256]{1,0:T(8,128)(2,1)S(1)}, bf16[512,256]{1,0:T(8,128)(2,1)S(1)}, u32[]{:S(2)}, u32[]{:S(2)}) %collective-permute-start.15) | collective-permute-done | bytes 262176 | tf_op jit(solution)/shard_map/ppermute | solution.py:334
  73.0 0.0 collective-permute-done.16.far_b_ref
  73.0 1.8 %rest.1 = bf16[1024,1024]{1,0:T(8,128)(2,1)} custom-call(f32[1024,1024]{1,0:T(8,128)S(1)} %shard_map.63.most_ref, bf16[512,256]{1,0:T(8,128)(2,1)S(1)} %collective-permute-done.15.far_a_ref, bf16[512,256]{1,0:T(8,128)(2,1)S(1)} %collective-permute-done.16.far_b_ref, bf16[2048,1024]{1,0:T(8,128)(2,1)S(1)} %copy-done), custom_call_target="tpu_custom_call" | custom-call | flops 536870912 | bytes 8388608 | tf_op jit(solution)/shard_map/rest/pallas_call | solution.py:315
  (5 shorter events, 0.1 us)
Async XLA Ops:
  2.1 4.2 %collective-permute-start = (bf16[272,128]{1,0:T(8,128)(2,1)S(1)}, bf16[272,128]{1,0:T(8,128)(2,1)S(1)}, u32[]{:S(2)}, u32[]{:S(2)}) collective-permute-start(bf16[272,128]{1,0:T(8,128)(2,1)S(1)} %get-tuple-element.29), channel_id=1, source_target_pairs={{0,4},{4,0},{1,5},{5,1},{2,6},{6,2},{3,7},{7,3},{8,12},{12,8},{9,1... | collective-permute-start | bytes 208904 | tf_op jit(solution)/shard_map/ppermute | solution.py:382
  6.4 5.3 %collective-permute-start.1 = (bf16[272,128]{1,0:T(8,128)(2,1)S(1)}, bf16[272,128]{1,0:T(8,128)(2,1)S(1)}, u32[]{:S(2)}, u32[]{:S(2)}) collective-permute-start(bf16[272,128]{1,0:T(8,128)(2,1)S(1)} %add_convert_fusion), channel_id=1, source_target_pairs={{0,8},{8,16},{16,24},{24,0},{1,9},{9,17},{17,25},{25,1},{2,10},{10... | collective-permute-start | bytes 208904 | tf_op jit(solution)/shard_map/ppermute | solution.py:385
  6.5 5.8 %collective-permute-start.2 = (bf16[272,128]{1,0:T(8,128)(2,1)S(1)}, bf16[272,128]{1,0:T(8,128)(2,1)S(1)}, u32[]{:S(2)}, u32[]{:S(2)}) collective-permute-start(bf16[272,128]{1,0:T(8,128)(2,1)S(1)} %add_convert_fusion), channel_id=1, source_target_pairs={{0,16},{8,24},{16,0},{24,8},{1,17},{9,25},{17,1},{25,9},{2,18},{10... | collective-permute-start | bytes 208904 | tf_op jit(solution)/shard_map/ppermute | solution.py:385
  8.4 4.4 %collective-permute-start.3 = (bf16[272,128]{1,0:T(8,128)(2,1)S(1)}, bf16[272,128]{1,0:T(8,128)(2,1)S(1)}, u32[]{:S(2)}, u32[]{:S(2)}) collective-permute-start(bf16[272,128]{1,0:T(8,128)(2,1)S(1)} %add_convert_fusion), channel_id=1, source_target_pairs={{0,24},{8,0},{16,8},{24,16},{1,25},{9,1},{17,9},{25,17},{2,26},{10... | collective-permute-start | bytes 208904 | tf_op jit(solution)/shard_map/ppermute | solution.py:385
  12.9 6.4 %collective-permute-start.4 = (bf16[272,128]{1,0:T(8,128)(2,1)S(1)}, bf16[272,128]{1,0:T(8,128)(2,1)S(1)}, u32[]{:S(2)}, u32[]{:S(2)}) collective-permute-start(bf16[272,128]{1,0:T(8,128)(2,1)S(1)} %get-tuple-element.31), channel_id=1, source_target_pairs={{0,32},{32,64},{64,96},{96,128},{128,160},{160,192},{192,224},{224... | collective-permute-start | bytes 208904 | tf_op jit(solution)/shard_map/ppermute | solution.py:388
  13.7 5.6 %collective-permute-start.5 = (bf16[272,128]{1,0:T(8,128)(2,1)S(1)}, bf16[272,128]{1,0:T(8,128)(2,1)S(1)}, u32[]{:S(2)}, u32[]{:S(2)}) collective-permute-start(bf16[272,128]{1,0:T(8,128)(2,1)S(1)} %get-tuple-element.31), channel_id=1, source_target_pairs={{0,224},{32,0},{64,32},{96,64},{128,96},{160,128},{192,160},{224,1... | collective-permute-start | bytes 208904 | tf_op jit(solution)/shard_map/ppermute | solution.py:389
  19.4 11.2 %collective-permute-start.6 = (bf16[272,128]{1,0:T(8,128)(2,1)S(1)}, bf16[272,128]{1,0:T(8,128)(2,1)S(1)}, u32[]{:S(2)}, u32[]{:S(2)}) collective-permute-start(bf16[272,128]{1,0:T(8,128)(2,1)S(1)} %get-tuple-element.34), channel_id=1, source_target_pairs={{0,160},{32,192},{64,224},{224,128},{1,161},{33,193},{65,225},{225... | collective-permute-start | bytes 208904 | tf_op jit(solution)/shard_map/ppermute | solution.py:392
  24.4 6.2 %collective-permute-start.7 = (bf16[272,128]{1,0:T(8,128)(2,1)S(1)}, bf16[272,128]{1,0:T(8,128)(2,1)S(1)}, u32[]{:S(2)}, u32[]{:S(2)}) collective-permute-start(bf16[272,128]{1,0:T(8,128)(2,1)S(1)} %get-tuple-element.35), channel_id=1, source_target_pairs={{0,64},{32,96},{64,128},{96,160},{128,192},{160,224},{1,65},{33,97... | collective-permute-start | bytes 208904 | tf_op jit(solution)/shard_map/ppermute | solution.py:391
  30.6 8.0 %collective-permute-start.8 = (bf16[272,128]{1,0:T(8,128)(2,1)S(1)}, bf16[272,128]{1,0:T(8,128)(2,1)S(1)}, u32[]{:S(2)}, u32[]{:S(2)}) collective-permute-start(bf16[272,128]{1,0:T(8,128)(2,1)S(1)} %get-tuple-element.36), channel_id=1, source_target_pairs={{0,4},{4,0},{1,5},{5,1},{2,6},{6,2},{3,7},{7,3},{8,12},{12,8},{9,1... | collective-permute-start | bytes 208904 | tf_op jit(solution)/shard_map/ppermute | solution.py:394
  35.2 29.5 %copy-start = (bf16[2048,1024]{1,0:T(8,128)(2,1)S(1)}, bf16[2048,1024]{1,0:T(8,128)(2,1)}, u32[]{:S(2)}) copy-start(bf16[2048,1024]{1,0:T(8,128)(2,1)} %w_ref.1) | copy-start | bytes 12582916
  35.7 14.9 %collective-permute-start.11 = (bf16[1024,256]{1,0:T(8,128)(2,1)S(1)}, bf16[1024,256]{1,0:T(8,128)(2,1)S(1)}, u32[]{:S(2)}, u32[]{:S(2)}) collective-permute-start(bf16[1024,256]{1,0:T(8,128)(2,1)S(1)} %shard_map.61.refs_0_), channel_id=1, source_target_pairs={{0,1},{1,2},{2,3},{3,0},{4,5},{5,6},{6,7},{7,4},{8,9},{9,10},{10,1... | collective-permute-start | bytes 1572872 | tf_op jit(solution)/shard_map/ppermute | solution.py:334
  37.1 13.6 %collective-permute-start.12 = (bf16[1024,256]{1,0:T(8,128)(2,1)S(1)}, bf16[1024,256]{1,0:T(8,128)(2,1)S(1)}, u32[]{:S(2)}, u32[]{:S(2)}) collective-permute-start(bf16[1024,256]{1,0:T(8,128)(2,1)S(1)} %shard_map.61.refs_0_), channel_id=1, source_target_pairs={{0,3},{1,0},{2,1},{3,2},{4,7},{5,4},{6,5},{7,6},{8,11},{9,8},{10,9... | collective-permute-start | bytes 1572872 | tf_op jit(solution)/shard_map/ppermute | solution.py:334
  39.0 22.7 %collective-permute-start.9 = (bf16[1024,256]{1,0:T(8,128)(2,1)S(1)}, bf16[1024,256]{1,0:T(8,128)(2,1)S(1)}, u32[]{:S(2)}, u32[]{:S(2)}) collective-permute-start(bf16[1024,256]{1,0:T(8,128)(2,1)S(1)} %shard_map.60.refs_0_), channel_id=1, source_target_pairs={{0,1},{1,2},{2,3},{3,0},{4,5},{5,6},{6,7},{7,4},{8,9},{9,10},{10,1... | collective-permute-start | bytes 1572872 | tf_op jit(solution)/shard_map/ppermute | solution.py:334
  39.1 22.8 %collective-permute-start.10 = (bf16[1024,256]{1,0:T(8,128)(2,1)S(1)}, bf16[1024,256]{1,0:T(8,128)(2,1)S(1)}, u32[]{:S(2)}, u32[]{:S(2)}) collective-permute-start(bf16[1024,256]{1,0:T(8,128)(2,1)S(1)} %shard_map.60.refs_0_), channel_id=1, source_target_pairs={{0,3},{1,0},{2,1},{3,2},{4,7},{5,4},{6,5},{7,6},{8,11},{9,8},{10,9... | collective-permute-start | bytes 1572872 | tf_op jit(solution)/shard_map/ppermute | solution.py:334
  50.6 16.8 %collective-permute-start.13 = (bf16[512,256]{1,0:T(8,128)(2,1)S(1)}, bf16[512,256]{1,0:T(8,128)(2,1)S(1)}, u32[]{:S(2)}, u32[]{:S(2)}) collective-permute-start(bf16[512,256]{1,0:T(8,128)(2,1)S(1)} %slice.16), channel_id=1, source_target_pairs={{0,1},{1,2},{2,3},{3,0},{4,5},{5,6},{6,7},{7,4},{8,9},{9,10},{10,1... | collective-permute-start | bytes 786440 | tf_op jit(solution)/shard_map/ppermute | solution.py:334
  50.7 16.7 %collective-permute-start.14 = (bf16[512,256]{1,0:T(8,128)(2,1)S(1)}, bf16[512,256]{1,0:T(8,128)(2,1)S(1)}, u32[]{:S(2)}, u32[]{:S(2)}) collective-permute-start(bf16[512,256]{1,0:T(8,128)(2,1)S(1)} %slice.17), channel_id=1, source_target_pairs={{0,3},{1,0},{2,1},{3,2},{4,7},{5,4},{6,5},{7,6},{8,11},{9,8},{10,9... | collective-permute-start | bytes 786440 | tf_op jit(solution)/shard_map/ppermute | solution.py:334
  61.8 11.2 %collective-permute-start.15 = (bf16[512,256]{1,0:T(8,128)(2,1)S(1)}, bf16[512,256]{1,0:T(8,128)(2,1)S(1)}, u32[]{:S(2)}, u32[]{:S(2)}) collective-permute-start(bf16[512,256]{1,0:T(8,128)(2,1)S(1)} %slice.18), channel_id=1, source_target_pairs={{0,1},{1,2},{2,3},{3,0},{4,5},{5,6},{6,7},{7,4},{8,9},{9,10},{10,1... | collective-permute-start | bytes 786440 | tf_op jit(solution)/shard_map/ppermute | solution.py:334
  61.9 11.1 %collective-permute-start.16 = (bf16[512,256]{1,0:T(8,128)(2,1)S(1)}, bf16[512,256]{1,0:T(8,128)(2,1)S(1)}, u32[]{:S(2)}, u32[]{:S(2)}) collective-permute-start(bf16[512,256]{1,0:T(8,128)(2,1)S(1)} %slice.19), channel_id=1, source_target_pairs={{0,3},{1,0},{2,1},{3,2},{4,7},{5,4},{6,5},{7,6},{8,11},{9,8},{10,9... | collective-permute-start | bytes 786440 | tf_op jit(solution)/shard_map/ppermute | solution.py:334
